TPU v7x, 32 devices: a whole 2x2x4 slice. The times are simulated.
32 devices in a mesh: row: 4 (over y, x), col: 8 (over z, core).
Axes of the slice: x: 2, y: 2, z: 4, core: 2. Of those that a mesh axis runs over, the one named last changes fastest.
Arguments:
- initial_field: float32 [1, 512, 4096], P(None, 'row', 'col'), may hold values from -12 to 12
- information: float32 [512, 4096], P('row', 'col'), may hold values from -24 to 24
- kappa_squared: float32 [512, 4096], P('row', 'col'), may hold values from 0.05 to 2
- lumped_mass: float32 [512, 4096], P('row', 'col'), may hold values from 0.5 to 2
- noise_seeds: int32 [4, 8, 2, 4, 1], P('row', 'col'), may hold values from 0 to 1073741823
- colour_order: int32 [4], replicated, may hold values from 0 to 3, each once
Outputs:
- final_field: float32 [1, 512, 4096], P(None, 'row', 'col')
- energies: float32 [2, 4, 1], replicated
Inputs may be any that keep to these rules, and one draw needn't show every extreme that they name: `noise_seeds`: one seed for each tile of 128 x 512 nodes, sweep, colour phase and chain. `colour_order`: names each of the 4 block colours once.
All inputs are finite; a program needn't handle non-finite values.
Results may differ from a plain program's by a relative error of at most 0.0003.
Values sent between devices are 32-bit elements; how exact they have to be, the bound alone decides.
No kernel may reach another device: no remote copies, remote signals or barrier semaphores. Data moves between devices by JAX's collectives and lax.ppermute only.
A program may use at most 128 MiB of HBM per device.

v0:
```python
import jax
import jax.numpy as jnp
from jax import lax
from jax.sharding import PartitionSpec as P

SWEEPS = 2
COLOURS = 4


full_turn = 6.283185307179586
unit_step = 1.0 / 8388608.0
mix_factor = 73244475


def with_halo(block, sides, width):
    for axis, dim in sides:
        count = lax.axis_size(axis)
        forward = [(i, i + 1) for i in range(count - 1)]
        forward.append((count - 1, 0))
        backward = [(target, source) for source, target in forward]
        low = lax.ppermute(
            lax.slice_in_dim(block, block.shape[dim] - width, None, axis=dim), axis, forward
        )
        high = lax.ppermute(lax.slice_in_dim(block, 0, width, axis=dim), axis, backward)
        block = jnp.concatenate([low, block, high], axis=dim)
    return block


def crop_edges(source, amount):
    return source[..., amount : source.shape[-2] - amount, amount : source.shape[-1] - amount]


def stencil_sum(source):
    return (
        source[..., :-2, 1:-1]
        + source[..., 2:, 1:-1]
        + source[..., 1:-1, :-2]
        + source[..., 1:-1, 2:]
    )


def apply_precision(sample_field, stiffness, inverse):
    first_pass = stiffness * crop_edges(sample_field, 1) - stencil_sum(sample_field)
    scaled = inverse * first_pass
    return crop_edges(stiffness, 1) * crop_edges(scaled, 1) - stencil_sum(scaled)


def corners(source):
    return [
        source[..., first_index::2, second_index::2]
        for first_index in (0, 1)
        for second_index in (0, 1)
    ]


def join_corners(pieces):
    total = None
    for corner in range(4):
        piece = pieces[corner]
        row_parity, col_parity = (corner // 2, corner % 2)
        config = [(0, 0, 0)] * (piece.ndim - 2) + [
            (row_parity, 1 - row_parity, 1),
            (col_parity, 1 - col_parity, 1),
        ]
        padded = lax.pad(piece, jnp.zeros((), piece.dtype), config)
        total = padded if total is None else total + padded
    return total


def block_matrix(stiff_corners, inverse_corners, diagonal_corners):
    scaled = [stiff_corners[corner] * inverse_corners[corner] for corner in range(4)]
    matrix = [[None] * 4 for corner in range(4)]
    for corner in range(4):
        matrix[corner][corner] = diagonal_corners[corner]
    for first_index, second_index in ((0, 1), (0, 2), (1, 3), (2, 3)):
        element = -(scaled[first_index] + scaled[second_index])
        matrix[first_index][second_index] = element
        matrix[second_index][first_index] = element
    matrix[0][3] = inverse_corners[1] + inverse_corners[2]
    matrix[3][0] = matrix[0][3]
    matrix[1][2] = inverse_corners[0] + inverse_corners[3]
    matrix[2][1] = matrix[1][2]
    return matrix


def cholesky_rows(matrix):
    factor = [[None] * 4 for corner in range(4)]
    for first_index in range(4):
        for second_index in range(first_index + 1):
            running = matrix[first_index][second_index]
            for middle in range(second_index):
                running = running - factor[first_index][middle] * factor[second_index][middle]
            if first_index == second_index:
                factor[first_index][first_index] = jnp.sqrt(running)
            else:
                factor[first_index][second_index] = running / factor[second_index][second_index]
    return factor


def crop_matrix(matrix, amount):
    return [
        [None if element is None else crop_edges(element, amount) for element in matrix_row]
        for matrix_row in matrix
    ]


def resample(field_corners, applied_corners, info_corners, matrix, factor, noise_list):
    right_side = []
    for first_index in range(4):
        coupled = matrix[first_index][0] * field_corners[0]
        for second_index in range(1, 4):
            coupled = coupled + matrix[first_index][second_index] * field_corners[second_index]
        right_side.append(info_corners[first_index] - applied_corners[first_index] + coupled)
    forward = []
    for first_index in range(4):
        running = right_side[first_index]
        for second_index in range(first_index):
            running = running - factor[first_index][second_index] * forward[second_index]
        forward.append(running / factor[first_index][first_index])
    shifted = [forward[corner] + noise_list[corner] for corner in range(4)]
    result = [None] * 4
    for first_index in reversed(range(4)):
        running = shifted[first_index]
        for second_index in range(first_index + 1, 4):
            running = running - factor[second_index][first_index] * result[second_index]
        result[first_index] = running / factor[first_index][first_index]
    return result


def scramble(hashed):
    sixteen = jnp.full_like(hashed, 16)
    hashed = hashed ^ lax.shift_right_logical(hashed, sixteen)
    hashed = hashed * mix_factor
    hashed = hashed ^ lax.shift_right_logical(hashed, sixteen)
    hashed = hashed * mix_factor
    return hashed ^ lax.shift_right_logical(hashed, sixteen)


def gaussian(seed_nodes, offsets):
    first_hash = scramble(seed_nodes + 2 * offsets)
    second_hash = scramble(seed_nodes + 2 * offsets + 1)
    shift_nine = jnp.full_like(first_hash, 9)
    uniform_one = (
        lax.shift_right_logical(first_hash, shift_nine).astype(jnp.float32) + 1.0
    ) * unit_step
    uniform_two = lax.shift_right_logical(second_hash, shift_nine).astype(jnp.float32) * unit_step
    return jnp.sqrt(-2.0 * jnp.log(uniform_one)) * jnp.cos(full_turn * uniform_two)


def node_seeds(seed_table, which_rows, which_cols):
    result = jnp.zeros((seed_table.shape[-1], which_rows.shape[0], which_cols.shape[0]), jnp.int32)
    hit = (which_rows == 0)[:, None] & (which_cols == 0)[None, :]
    result = result + jnp.where(hit[None], seed_table[0, 0][:, None, None], 0)
    return result


def local(initial_field, information, kappa_squared, lumped_mass, noise_seeds, colour_order):
    chains, tile_rows, tile_cols = initial_field.shape
    total_rows = tile_rows * lax.axis_size("row")
    total_cols = tile_cols * lax.axis_size("col")
    row_start = lax.axis_index("row") * tile_rows
    col_start = lax.axis_index("col") * tile_cols
    kappa_ext, mass_ext = (
        with_halo(kappa_squared, (("row", 0), ("col", 1)), 1),
        with_halo(lumped_mass, (("row", 0), ("col", 1)), 1),
    )
    margin = 2
    info_margin = (information.shape[0] - tile_rows) // 2
    stiff_ext = kappa_ext * mass_ext + 4.0
    inverse_ext = 1.0 / mass_ext
    block_margin = margin - 2
    stiff_blocks = crop_edges(stiff_ext, 1)
    inverse_blocks = crop_edges(inverse_ext, 1)
    diagonal = stiff_blocks * stiff_blocks * inverse_blocks + stencil_sum(inverse_ext)
    matrix = block_matrix(corners(stiff_blocks), corners(inverse_blocks), corners(diagonal))
    factor = cholesky_rows(matrix)
    shrink_table = 1 - noise_seeds.shape[0] // 2

    def phase_tables(near_margin):
        half_rows = jnp.arange((tile_rows + 2 * near_margin) // 2, dtype=jnp.int32)
        half_cols = jnp.arange((tile_cols + 2 * near_margin) // 2, dtype=jnp.int32)
        block_rows = (row_start - near_margin) // 2 + half_rows
        block_cols = (col_start - near_margin) // 2 + half_cols
        block_colour = 2 * (block_rows % 2)[:, None] + (block_cols % 2)[None, :]
        offsets = []
        row_tiles = []
        col_tiles = []
        for corner in range(4):
            local_rows = 2 * half_rows + corner // 2 - near_margin
            local_cols = 2 * half_cols + corner % 2 - near_margin
            global_rows = (row_start + local_rows) % total_rows
            global_cols = (col_start + local_cols) % total_cols
            offsets.append(
                (global_rows % tile_rows)[:, None] * tile_cols + (global_cols % tile_cols)[None, :]
            )
            row_tiles.append(
                (local_rows >= 0).astype(jnp.int32)
                + (local_rows >= tile_rows).astype(jnp.int32)
                - shrink_table
            )
            col_tiles.append(
                (local_cols >= 0).astype(jnp.int32)
                + (local_cols >= tile_cols).astype(jnp.int32)
                - shrink_table
            )
        return (block_colour, offsets, row_tiles, col_tiles)

    def one_sweep(sweep_index, loop_state):
        sample_field, energies = loop_state
        seed_layer = lax.dynamic_index_in_dim(noise_seeds, sweep_index, 2, keepdims=False)
        for phase_index in range(COLOURS):
            extended = with_halo(sample_field, (("row", 1), ("col", 2)), 2)
            margin_now = (extended.shape[1] - tile_rows) // 2
            near_margin = margin_now - 2
            applied = apply_precision(
                extended,
                crop_edges(stiff_ext, margin - margin_now),
                crop_edges(inverse_ext, margin - margin_now),
            )
            inner_field = crop_edges(extended, margin_now)
            inner_applied = crop_edges(applied, near_margin)
            local_energy = jnp.sum(
                0.5 * inner_field * inner_applied - information * inner_field, axis=(1, 2)
            )
            energies = energies.at[sweep_index, phase_index].set(local_energy)
            dropped = (block_margin - near_margin) // 2
            block_colour, offsets, row_tiles, col_tiles = phase_tables(near_margin)
            chosen = block_colour == colour_order[phase_index]
            near_field = crop_edges(extended, 2)
            near_info = crop_edges(information, info_margin - near_margin)
            seed_table = seed_layer[:, :, phase_index, :]
            noise_list = []
            for corner in range(4):
                seeds_here = node_seeds(seed_table, row_tiles[corner], col_tiles[corner])
                noise_list.append(gaussian(seeds_here, offsets[corner]))
            before = corners(near_field)
            updated = resample(
                before,
                corners(applied),
                corners(near_info),
                crop_matrix(matrix, dropped),
                crop_matrix(factor, dropped),
                noise_list,
            )
            extended = join_corners(
                [jnp.where(chosen, updated[corner], before[corner]) for corner in range(4)]
            )
            sample_field = extended
        return (sample_field, energies)

    initial = (initial_field, jnp.zeros((SWEEPS, COLOURS, chains), jnp.float32))
    final_field, energies = lax.fori_loop(0, SWEEPS, one_sweep, initial)
    energies = lax.psum(energies, ("row", "col")) / (total_rows * total_cols)
    return (final_field, energies)


def solution(mesh):
    placed = (
        P(None, "row", "col"),
        P("row", "col"),
        P("row", "col"),
        P("row", "col"),
        P("row", "col", None, None, None),
        P(),
    )
    return jax.shard_map(
        local, mesh=mesh, in_specs=placed, out_specs=(P(None, "row", "col"), P()), check_vma=False
    )
```

profile of v0, /device:TPU:0, one launch (start us, length us, event | category | flops | bytes accessed | tf_op | source)
XLA Modules:
  0.0 570.5 jit_solution(7635717978839268749)
XLA Ops:
  1.6 3.0 collective-permute-start.16
  8.7 3.5 collective-permute-start.19
  12.4 3.5 collective-permute-start.23
  30.0 12.0 %slice.1365 = f32[64,256]{1,0:T(8,128)S(1)} slice(f32[128,512]{1,0:T(8,128)S(1)} %get-tuple-element.1169), slice={[0:128:2], [1:512:2]} | slice | bytes 131072 | tf_op jit(solution)/shard_map/slice | solution.py:50
  56.6 474.0 %while.22 = (s32[]{:T(128)}, f32[1,128,512]{2,1,0:T(8,128)S(1)}, f32[2,4,1]{1,2,0:T(1,128)}, s32[]{:T(128)}, s32[]{:T(128)}, /*index=5*/s32[4]{0:T(128)S(1)}, f3...) while((s32[]{:T(128)}, f32[1,128,512]{2,1,0:T(8,128)S(1)}, ...), condition=%wide.region_9.10_spmd, body=%wide.region_0.9_spmd.sunk | while | flops 21103232 | bytes 64269184 | solution.py:252
  108.1 3.6 pad.730
  111.7 3.6 pad.731
  127.0 2.9 slice.1683
  144.6 3.0 slice.1689
  148.9 3.3 fusion.562
  154.6 3.1 pad.732
  157.7 3.6 pad.733
  161.3 3.6 pad.734
  164.9 3.6 pad.735
  189.8 2.9 slice.1694
  198.3 3.0 slice.1697
  202.7 3.2 fusion.567
  208.2 4.5 pad.736
  212.7 3.6 pad.737
  216.3 3.6 pad.738
  219.9 3.7 pad.739
  252.2 3.2 slice.1702
  255.5 3.2 slice.1703
  258.7 3.2 slice.1704
  261.9 3.2 slice.1705
  283.2 3.6 pad.743
  344.5 3.6 pad.730
  348.1 3.6 pad.731
  363.3 2.9 slice.1683
  380.9 3.2 slice.1689
  385.4 3.3 fusion.562
  391.1 3.1 pad.732
  394.2 3.6 pad.733
  397.8 3.6 pad.734
  401.4 3.6 pad.735
  425.3 2.9 slice.1694
  433.8 3.2 slice.1697
  438.4 3.2 fusion.567
  444.0 4.5 pad.736
  448.4 3.6 pad.737
  452.0 3.6 pad.738
  455.7 3.7 pad.739
  487.4 3.2 slice.1702
  490.6 3.2 slice.1703
  493.9 3.2 slice.1704
  497.1 3.2 slice.1705
  518.6 3.6 pad.743
  531.4 38.3 %psum.7 = f32[2,4,1]{1,2,0:T(1,128)S(1)} all-reduce(f32[2,4,1]{1,2,0:T(1,128)S(1)} %copy-done.55), channel_id=1, replica_groups=mesh['row'=4,'col'=8] {'row','col'}, use_global_device_ids=true, to_apply=%region_10.11 | all-reduce | flops 8 | bytes 64 | tf_op jit(solution)/shard_map/psum | solution.py:253
  (482 shorter events, 362.8 us)
Async XLA Ops:
  1.6 7.0 %collective-permute-start.16 = (f32[1,512]{1,0:T(1,128)S(1)}, f32[1,512]{1,0:T(1,128)S(1)}, u32[]{:S(2)}, u32[]{:S(2)}) collective-permute-start(f32[1,512]{1,0:T(1,128)S(1)} %get-tuple-element.1176), channel_id=1, source_target_pairs={{0,8},{8,16},{16,24},{24,0},{1,9},{9,17},{17,25},{25,1},{2,10},{10... | collective-permute-start | bytes 6152 | tf_op jit(solution)/shard_map/ppermute | solution.py:21
  4.6 4.0 collective-permute-start.17
  5.6 6.7 %collective-permute-start.20 = (f32[1,512]{1,0:T(1,128)S(1)}, f32[1,512]{1,0:T(1,128)S(1)}, u32[]{:S(2)}, u32[]{:S(2)}) collective-permute-start(f32[1,512]{1,0:T(1,128)S(1)} %get-tuple-element.1174), channel_id=1, source_target_pairs={{0,8},{8,16},{16,24},{24,0},{1,9},{9,17},{17,25},{25,1},{2,10},{10... | collective-permute-start | bytes 6152 | tf_op jit(solution)/shard_map/ppermute | solution.py:21
  6.6 5.6 collective-permute-start.21
  8.6 7.3 %collective-permute-start.18 = (f32[130,1]{1,0:T(8,128)S(1)}, f32[130,1]{1,0:T(8,128)S(1)}, u32[]{:S(2)}, u32[]{:S(2)}) collective-permute-start(f32[130,1]{1,0:T(8,128)S(1)} %get-tuple-element.1172), channel_id=1, source_target_pairs={{0,1},{1,2},{2,3},{3,4},{4,5},{5,6},{6,7},{7,0},{8,9},{9,10},{10,1... | collective-permute-start | bytes 1568 | tf_op jit(solution)/shard_map/ppermute | solution.py:21
  8.7 7.2 %collective-permute-start.19 = (f32[130,1]{1,0:T(8,128)S(1)}, f32[130,1]{1,0:T(8,128)S(1)}, u32[]{:S(2)}, u32[]{:S(2)}) collective-permute-start(f32[130,1]{1,0:T(8,128)S(1)} %get-tuple-element.1173), channel_id=1, source_target_pairs={{1,0},{2,1},{3,2},{4,3},{5,4},{6,5},{7,6},{0,7},{9,8},{10,9},{11,1... | collective-permute-start | bytes 1568 | tf_op jit(solution)/shard_map/ppermute | solution.py:24
  12.3 5.7 collective-permute-start.22
  12.4 5.6 collective-permute-start.23
  56.7 92.1 %copy-start.6 = (f32[64,256]{1,0:T(8,128)}, f32[64,256]{1,0:T(8,128)S(1)}, u32[]{:S(2)}) copy-start(f32[64,256]{1,0:T(8,128)S(1)} %get-tuple-element.1649) | copy-start | bytes 196612 | tf_op jit(solution)/shard_map/while
  56.7 92.1 %copy-start.8 = (f32[64,256]{1,0:T(8,128)}, f32[64,256]{1,0:T(8,128)S(1)}, u32[]{:S(2)}) copy-start(f32[64,256]{1,0:T(8,128)S(1)} %get-tuple-element.1651) | copy-start | bytes 196612 | tf_op jit(solution)/shard_map/while
  56.7 144.6 %copy-start.2 = (f32[64,256]{1,0:T(8,128)}, f32[64,256]{1,0:T(8,128)S(1)}, u32[]{:S(2)}) copy-start(f32[64,256]{1,0:T(8,128)S(1)} %get-tuple-element.1644) | copy-start | bytes 196612 | tf_op jit(solution)/shard_map/while
  56.7 4.2 collective-permute-start
  58.3 4.5 collective-permute-start.1
  58.9 143.8 %copy-start.47 = (pred[256]{0:T(512)(128)(4,1)}, pred[256]{0:T(512)(128)(4,1)S(1)}, u32[]{:S(2)}) copy-start(pred[256]{0:T(512)(128)(4,1)S(1)} %get-tuple-element.1466) | copy-start | bytes 772 | tf_op jit(solution)/shard_map/while
  62.9 22.7 %collective-permute-start.2 = (f32[1,132,2]{2,1,0:T(8,128)S(1)}, f32[1,132,2]{2,1,0:T(8,128)S(1)}, u32[]{:S(2)}, u32[]{:S(2)}) collective-permute-start(f32[1,132,2]{2,1,0:T(8,128)S(1)} %get-tuple-element.1460), channel_id=1, source_target_pairs={{1,0},{2,1},{3,2},{4,3},{5,4},{6,5},{7,6},{0,7},{9,8},{10,9},{11,1... | collective-permute-start | bytes 3176 | tf_op jit(solution)/shard_map/while/body/eval_jaxpr/ppermute | solution.py:24
  64.9 20.6 %collective-permute-start.3 = (f32[1,132,2]{2,1,0:T(8,128)S(1)}, f32[1,132,2]{2,1,0:T(8,128)S(1)}, u32[]{:S(2)}, u32[]{:S(2)}) collective-permute-start(f32[1,132,2]{2,1,0:T(8,128)S(1)} %get-tuple-element.1461), channel_id=1, source_target_pairs={{0,1},{1,2},{2,3},{3,4},{4,5},{5,6},{6,7},{7,0},{8,9},{9,10},{10,1... | collective-permute-start | bytes 3176 | tf_op jit(solution)/shard_map/while/body/eval_jaxpr/ppermute | solution.py:21
  65.0 137.7 %copy-start.49 = (s32[64]{0:T(128)}, s32[64]{0:T(128)S(1)}, u32[]{:S(2)}) copy-start(s32[64]{0:T(128)S(1)} %fusion.556) | copy-start | bytes 772 | tf_op jit(solution)/shard_map/while
  116.4 3.7 collective-permute-start.4
  117.9 4.5 collective-permute-start.5
  122.5 13.1 %collective-permute-start.6 = (f32[1,132,2]{2,1,0:T(8,128)S(1)}, f32[1,132,2]{2,1,0:T(8,128)S(1)}, u32[]{:S(2)}, u32[]{:S(2)}) collective-permute-start(f32[1,132,2]{2,1,0:T(8,128)S(1)} %get-tuple-element.1483), channel_id=1, source_target_pairs={{1,0},{2,1},{3,2},{4,3},{5,4},{6,5},{7,6},{0,7},{9,8},{10,9},{11,1... | collective-permute-start | bytes 3176 | tf_op jit(solution)/shard_map/while/body/eval_jaxpr/ppermute | solution.py:24
  124.6 10.9 %collective-permute-start.7 = (f32[1,132,2]{2,1,0:T(8,128)S(1)}, f32[1,132,2]{2,1,0:T(8,128)S(1)}, u32[]{:S(2)}, u32[]{:S(2)}) collective-permute-start(f32[1,132,2]{2,1,0:T(8,128)S(1)} %get-tuple-element.1484), channel_id=1, source_target_pairs={{0,1},{1,2},{2,3},{3,4},{4,5},{5,6},{6,7},{7,0},{8,9},{9,10},{10,1... | collective-permute-start | bytes 3176 | tf_op jit(solution)/shard_map/while/body/eval_jaxpr/ppermute | solution.py:21
  169.7 3.7 collective-permute-start.8
  170.9 4.5 collective-permute-start.9
  176.1 12.7 %collective-permute-start.10 = (f32[1,132,2]{2,1,0:T(8,128)}, f32[1,132,2]{2,1,0:T(8,128)S(1)}, u32[]{:S(2)}, u32[]{:S(2)}) collective-permute-start(f32[1,132,2]{2,1,0:T(8,128)} %get-tuple-element.1499), channel_id=1, source_target_pairs={{1,0},{2,1},{3,2},{4,3},{5,4},{6,5},{7,6},{0,7},{9,8},{10,9},{11,1... | collective-permute-start | bytes 3176 | tf_op jit(solution)/shard_map/while/body/eval_jaxpr/ppermute | solution.py:24
  178.2 10.6 %collective-permute-start.11 = (f32[1,132,2]{2,1,0:T(8,128)S(1)}, f32[1,132,2]{2,1,0:T(8,128)S(1)}, u32[]{:S(2)}, u32[]{:S(2)}) collective-permute-start(f32[1,132,2]{2,1,0:T(8,128)S(1)} %get-tuple-element.1500), channel_id=1, source_target_pairs={{0,1},{1,2},{2,3},{3,4},{4,5},{5,6},{6,7},{7,0},{8,9},{9,10},{10,1... | collective-permute-start | bytes 3176 | tf_op jit(solution)/shard_map/while/body/eval_jaxpr/ppermute | solution.py:21
  224.9 3.7 collective-permute-start.12
  226.3 4.5 collective-permute-start.13
  231.5 15.4 %collective-permute-start.14 = (f32[1,132,2]{2,1,0:T(8,128)}, f32[1,132,2]{2,1,0:T(8,128)}, u32[]{:S(2)}, u32[]{:S(2)}) collective-permute-start(f32[1,132,2]{2,1,0:T(8,128)} %get-tuple-element.1515), channel_id=1, source_target_pairs={{1,0},{2,1},{3,2},{4,3},{5,4},{6,5},{7,6},{0,7},{9,8},{10,9},{11,1... | collective-permute-start | bytes 3176 | tf_op jit(solution)/shard_map/while/body/eval_jaxpr/ppermute | solution.py:24
  233.6 13.3 %collective-permute-start.15 = (f32[1,132,2]{2,1,0:T(8,128)}, f32[1,132,2]{2,1,0:T(8,128)}, u32[]{:S(2)}, u32[]{:S(2)}) collective-permute-start(f32[1,132,2]{2,1,0:T(8,128)} %get-tuple-element.1516), channel_id=1, source_target_pairs={{0,1},{1,2},{2,3},{3,4},{4,5},{5,6},{6,7},{7,0},{8,9},{9,10},{10,1... | collective-permute-start | bytes 3176 | tf_op jit(solution)/shard_map/while/body/eval_jaxpr/ppermute | solution.py:21
  294.1 143.0 %copy-start.2 = (f32[64,256]{1,0:T(8,128)}, f32[64,256]{1,0:T(8,128)S(1)}, u32[]{:S(2)}) copy-start(f32[64,256]{1,0:T(8,128)S(1)} %get-tuple-element.1644) | copy-start | bytes 196612 | tf_op jit(solution)/shard_map/while
  294.1 4.2 collective-permute-start
  294.5 4.5 collective-permute-start.1
  296.2 142.2 %copy-start.47 = (pred[256]{0:T(512)(128)(4,1)}, pred[256]{0:T(512)(128)(4,1)S(1)}, u32[]{:S(2)}) copy-start(pred[256]{0:T(512)(128)(4,1)S(1)} %get-tuple-element.1466) | copy-start | bytes 772 | tf_op jit(solution)/shard_map/while
  299.1 23.1 %collective-permute-start.2 = (f32[1,132,2]{2,1,0:T(8,128)S(1)}, f32[1,132,2]{2,1,0:T(8,128)S(1)}, u32[]{:S(2)}, u32[]{:S(2)}) collective-permute-start(f32[1,132,2]{2,1,0:T(8,128)S(1)} %get-tuple-element.1460), channel_id=1, source_target_pairs={{1,0},{2,1},{3,2},{4,3},{5,4},{6,5},{7,6},{0,7},{9,8},{10,9},{11,1... | collective-permute-start | bytes 3176 | tf_op jit(solution)/shard_map/while/body/eval_jaxpr/ppermute | solution.py:24
  301.4 20.8 %collective-permute-start.3 = (f32[1,132,2]{2,1,0:T(8,128)S(1)}, f32[1,132,2]{2,1,0:T(8,128)S(1)}, u32[]{:S(2)}, u32[]{:S(2)}) collective-permute-start(f32[1,132,2]{2,1,0:T(8,128)S(1)} %get-tuple-element.1461), channel_id=1, source_target_pairs={{0,1},{1,2},{2,3},{3,4},{4,5},{5,6},{6,7},{7,0},{8,9},{9,10},{10,1... | collective-permute-start | bytes 3176 | tf_op jit(solution)/shard_map/while/body/eval_jaxpr/ppermute | solution.py:21
  301.4 137.0 %copy-start.49 = (s32[64]{0:T(128)}, s32[64]{0:T(128)S(1)}, u32[]{:S(2)}) copy-start(s32[64]{0:T(128)S(1)} %fusion.556) | copy-start | bytes 772 | tf_op jit(solution)/shard_map/while
  352.9 3.7 collective-permute-start.4
  354.1 4.5 collective-permute-start.5
  358.7 13.1 %collective-permute-start.6 = (f32[1,132,2]{2,1,0:T(8,128)S(1)}, f32[1,132,2]{2,1,0:T(8,128)S(1)}, u32[]{:S(2)}, u32[]{:S(2)}) collective-permute-start(f32[1,132,2]{2,1,0:T(8,128)S(1)} %get-tuple-element.1483), channel_id=1, source_target_pairs={{1,0},{2,1},{3,2},{4,3},{5,4},{6,5},{7,6},{0,7},{9,8},{10,9},{11,1... | collective-permute-start | bytes 3176 | tf_op jit(solution)/shard_map/while/body/eval_jaxpr/ppermute | solution.py:24
  360.9 11.0 %collective-permute-start.7 = (f32[1,132,2]{2,1,0:T(8,128)S(1)}, f32[1,132,2]{2,1,0:T(8,128)S(1)}, u32[]{:S(2)}, u32[]{:S(2)}) collective-permute-start(f32[1,132,2]{2,1,0:T(8,128)S(1)} %get-tuple-element.1484), channel_id=1, source_target_pairs={{0,1},{1,2},{2,3},{3,4},{4,5},{5,6},{6,7},{7,0},{8,9},{9,10},{10,1... | collective-permute-start | bytes 3176 | tf_op jit(solution)/shard_map/while/body/eval_jaxpr/ppermute | solution.py:21
  406.2 3.7 collective-permute-start.8
  406.6 4.5 collective-permute-start.9
  411.7 12.5 %collective-permute-start.10 = (f32[1,132,2]{2,1,0:T(8,128)}, f32[1,132,2]{2,1,0:T(8,128)S(1)}, u32[]{:S(2)}, u32[]{:S(2)}) collective-permute-start(f32[1,132,2]{2,1,0:T(8,128)} %get-tuple-element.1499), channel_id=1, source_target_pairs={{1,0},{2,1},{3,2},{4,3},{5,4},{6,5},{7,6},{0,7},{9,8},{10,9},{11,1... | collective-permute-start | bytes 3176 | tf_op jit(solution)/shard_map/while/body/eval_jaxpr/ppermute | solution.py:24
  413.9 10.3 %collective-permute-start.11 = (f32[1,132,2]{2,1,0:T(8,128)S(1)}, f32[1,132,2]{2,1,0:T(8,128)S(1)}, u32[]{:S(2)}, u32[]{:S(2)}) collective-permute-start(f32[1,132,2]{2,1,0:T(8,128)S(1)} %get-tuple-element.1500), channel_id=1, source_target_pairs={{0,1},{1,2},{2,3},{3,4},{4,5},{5,6},{6,7},{7,0},{8,9},{9,10},{10,1... | collective-permute-start | bytes 3176 | tf_op jit(solution)/shard_map/while/body/eval_jaxpr/ppermute | solution.py:21
  460.6 3.7 collective-permute-start.12
  461.7 4.5 collective-permute-start.13
  466.9 15.2 %collective-permute-start.14 = (f32[1,132,2]{2,1,0:T(8,128)}, f32[1,132,2]{2,1,0:T(8,128)}, u32[]{:S(2)}, u32[]{:S(2)}) collective-permute-start(f32[1,132,2]{2,1,0:T(8,128)} %get-tuple-element.1515), channel_id=1, source_target_pairs={{1,0},{2,1},{3,2},{4,3},{5,4},{6,5},{7,6},{0,7},{9,8},{10,9},{11,1... | collective-permute-start | bytes 3176 | tf_op jit(solution)/shard_map/while/body/eval_jaxpr/ppermute | solution.py:24
  469.0 13.1 %collective-permute-start.15 = (f32[1,132,2]{2,1,0:T(8,128)}, f32[1,132,2]{2,1,0:T(8,128)}, u32[]{:S(2)}, u32[]{:S(2)}) collective-permute-start(f32[1,132,2]{2,1,0:T(8,128)} %get-tuple-element.1516), channel_id=1, source_target_pairs={{0,1},{1,2},{2,3},{3,4},{4,5},{5,6},{6,7},{7,0},{8,9},{9,10},{10,1... | collective-permute-start | bytes 3176 | tf_op jit(solution)/shard_map/while/body/eval_jaxpr/ppermute | solution.py:21
  (99 other events, 1269.8 us)
where the time goes:
time: 582 us; the launch traced here: 570 us
  local copies, waits for them, and re-layouts  356 us (61%)
  other arithmetic  95.8 us (16%)
  starting transfers between devices  49.4 us (8%)
  blocking collectives  38.3 us (7%)
  waiting for transfers between devices  26.1 us (4%)
    slice x84, local copies, waits for them, and re-layouts, corners(): source[..., first_index::2, second_index::2]  233 us
    pad x32, local copies, waits for them, and re-layouts, join_corners(): padded = lax.pad(piece, jnp.zeros((), piece.dtype), config)  103 us
    select_n x16, other arithmetic, one_sweep(): jnp.where(chosen, updated[corner], before[corner])  39.5 us
    psum x1, blocking collectives, local(): energies = lax.psum(energies, ('row', 'col')) / (total_rows * total_cols)  38.3 us
    ppermute x20, starting transfers between devices, with_halo(): lax.ppermute(lax.slice_in_dim(block, 0, width, axis=dim), axis, backward)  35.9 us
    ppermute x20, waiting for transfers between devices, with_halo(): lax.ppermute(lax.slice_in_dim(block, block.shape[dim] - width, None, axis...  16.6 us
    another operation x10, other arithmetic  16 us
    ppermute x20, starting transfers between devices, with_halo(): lax.ppermute(lax.slice_in_dim(block, block.shape[dim] - width, None, axis...  13.5 us
  transfers between devices with their start and end apart: 40, of which 15 were waited for; matrix products, arithmetic and copies ran while one was open for 20% of the time, Pallas kernels for 0%

commit v1 on v0

v1 whole, which is shorter than its diff:
```python
import functools

import jax
import jax.numpy as jnp
from jax import lax
from jax.experimental import pallas as pl
from jax.experimental.pallas import tpu as pltpu
from jax.sharding import PartitionSpec as P

SWEEPS = 2
COLOURS = 4
PHASES = SWEEPS * COLOURS
HALO = 2 * PHASES
CELL = 4
HC = HALO // CELL
LANES = 128
SUB = 8
GROUP = LANES // CELL
AXES = ("row", "col")
F32 = jnp.float32
I32 = jnp.int32

unit_step = 1.0 / 8388608.0
mix_factor = 73244475
SEED_BASE = 32768

SIN_COEFFS = (
    6.283185306485777,
    -41.34170192921984,
    81.60520938153618,
    -76.70366601553475,
    41.99996083008805,
    -14.336855962945094,
)


def lane_iota(shape):
    return lax.broadcasted_iota(I32, shape, len(shape) - 1)


def sub_iota(shape):
    return lax.broadcasted_iota(I32, shape, len(shape) - 2)


def lane_gather(value, index):
    return jnp.take_along_axis(value, index, axis=1, mode="promise_in_bounds")


def lroll(value, amount):
    amount = amount % value.shape[1]
    return pltpu.roll(value, amount, 1) if amount else value


def seed_tile(seeds_ref):
    lane = lane_iota((SUB, LANES))
    tile = jnp.zeros((SUB, LANES), I32)
    for phase in range(PHASES):
        seed = seeds_ref[0, 0, phase // COLOURS, phase % COLOURS, 0]
        tile = jnp.where(lane == phase, seed // SEED_BASE, tile)
        tile = jnp.where(lane == PHASES + phase, seed % SEED_BASE, tile)
    return tile.astype(F32)


def pack_kernel(seeds_ref, *refs):
    sources, (up_ref, down_ref, left_ref, right_ref) = refs[:4], refs[4:]
    rows, cols = sources[0].shape
    lane = lane_iota((SUB, LANES))
    per = LANES // HALO
    for a, source in enumerate(sources):
        for edge, out in ((0, left_ref), (1, right_ref)):
            for v in range(rows // (SUB * per)):
                packed = jnp.zeros((SUB, LANES), F32)
                for q in range(per):
                    top = SUB * (v * per + q)
                    start = (cols - LANES) if edge else 0
                    piece = source[top : top + SUB, start : start + LANES]
                    offset = HALO * q - (LANES - HALO if edge else 0)
                    piece = lroll(piece, offset)
                    packed = jnp.where(lane // HALO == q, piece, packed)
                out[a * HALO + SUB * v : a * HALO + SUB * (v + 1), :] = packed
        up_ref[a * HALO : (a + 1) * HALO, :] = source[0:HALO, :]
        down_ref[a * HALO : (a + 1) * HALO, :] = source[rows - HALO : rows, :]
    seeds = seed_tile(seeds_ref)
    base = 4 * HALO
    for out in (up_ref, down_ref, left_ref, right_ref):
        out[base : base + SUB, 0:LANES] = seeds


def corner_kernel(right_ref, left_ref, up_ref, down_ref):
    lane = lane_iota((SUB, LANES))
    for a in range(4):
        for out, top, shift in ((up_ref, 0, 0), (down_ref, HALO - SUB, 2 * HALO)):
            r = right_ref[a * HALO + top : a * HALO + top + SUB, :]
            l = left_ref[a * HALO + top : a * HALO + top + SUB, :]
            r = lroll(r, shift)
            l = lroll(l, shift + 2 * HALO)
            out[a * SUB : (a + 1) * SUB, :] = jnp.where(lane < 2 * HALO, r, l)
    for out in (up_ref, down_ref):
        out[4 * SUB : 5 * SUB, :] = right_ref[4 * HALO : 4 * HALO + SUB, :]
        out[5 * SUB : 6 * SUB, :] = left_ref[4 * HALO : 4 * HALO + SUB, :]


def scramble(hashed):
    sixteen = jnp.full_like(hashed, 16)
    hashed = hashed ^ lax.shift_right_logical(hashed, sixteen)
    hashed = hashed * mix_factor
    hashed = hashed ^ lax.shift_right_logical(hashed, sixteen)
    hashed = hashed * mix_factor
    return hashed ^ lax.shift_right_logical(hashed, sixteen)


def gaussian(first):
    nine = jnp.full_like(first, 9)
    one = lax.shift_right_logical(scramble(first), nine).astype(F32)
    two = lax.shift_right_logical(scramble(first + 1), nine).astype(F32)
    u1 = (one + 1.0) * unit_step
    v = 0.25 - jnp.abs(two * unit_step - 0.5)
    square = v * v
    poly = jnp.full_like(v, SIN_COEFFS[-1])
    for coeff in SIN_COEFFS[-2::-1]:
        poly = poly * square + coeff
    return jnp.sqrt(-2.0 * jnp.log(u1)) * (-(v * poly))


def shifted(value, rows, cols):
    if rows:
        value = pltpu.roll(value, (-rows) % value.shape[0], 0)
    if cols:
        value = pltpu.roll(value, (-cols) % value.shape[1], 1)
    return value


def locate(r, c):
    return (r % CELL) * CELL + c % CELL, r // CELL, c // CELL


def fetch(ref, r, c):
    plane, rows, cols = locate(r, c)
    return shifted(ref[plane], rows, cols)


def neighbour_sum(ref, r, c):
    return (
        fetch(ref, r - 1, c) + fetch(ref, r + 1, c) + fetch(ref, r, c - 1) + fetch(ref, r, c + 1)
    )


def fold(value):
    total = value[0:SUB]
    for top in range(SUB, value.shape[0], SUB):
        total = total + value[top : top + SUB]
    return total


def block_nodes(colour):
    r0, c0 = 2 * (colour // 2), 2 * (colour % 2)
    return [(r0, c0), (r0, c0 + 1), (r0 + 1, c0), (r0 + 1, c0 + 1)]


def main_kernel(
    tile_rows, tile_cols, nodes,
    order_ref, seeds_ref, x_ref, b_ref, kappa_ref, mass_ref,
    below_ref, above_ref, right_ref, left_ref, cbelow_ref, cabove_ref,
    out_ref, energy_ref,
    nat, X, W, S, I, B, LM, Z, EN, ST,
):
    mr = tile_rows // CELL
    er = mr + 2 * HC
    tiles = tile_cols // LANES
    lane = lane_iota((SUB, LANES))
    sub = sub_iota((SUB, LANES))
    per = LANES // HALO
    edge = tiles

    for a, source in enumerate((x_ref, b_ref, kappa_ref, mass_ref)):
        for t in range(tiles):
            lanes = slice(t * LANES, (t + 1) * LANES)
            page = a * (tiles + 1) + t
            nat[page, 0:tile_rows, :] = source[:, lanes]
            nat[page, tile_rows : tile_rows + HALO, :] = below_ref[a * HALO : (a + 1) * HALO, lanes]
            nat[page, tile_rows + HALO : tile_rows + 2 * HALO, :] = above_ref[
                a * HALO : (a + 1) * HALO, lanes
            ]
        page = a * (tiles + 1) + edge

        def put(top, right, left):
            nat[page, top : top + SUB, :] = jnp.where(
                lane < HALO, right, jnp.where(lane >= LANES - HALO, left, 1.0)
            )

        for g in range(tile_rows // SUB):
            v, q = g // per, g % per
            rows = slice(a * HALO + SUB * v, a * HALO + SUB * (v + 1))
            put(
                SUB * g,
                lroll(right_ref[rows, :], -HALO * q),
                lroll(left_ref[rows, :], LANES - HALO - HALO * q),
            )
        for start, corner in ((tile_rows, cbelow_ref), (tile_rows + HALO, cabove_ref)):
            value = corner[a * SUB : (a + 1) * SUB, :]
            for h in range(HALO // SUB):
                put(
                    start + SUB * h,
                    lroll(value, -HALO * h),
                    lroll(value, LANES - HALO - 2 * HALO - HALO * h),
                )

    wide = lane_iota((er, LANES))
    group = wide // GROUP
    into = [CELL * (wide % GROUP) + (group + CELL - t) % CELL for t in range(CELL)]
    halo_index = [CELL * (wide % GROUP) + c for c in range(CELL)]

    def planes(a, r):
        page = a * (tiles + 1)
        pieces = [
            lane_gather(nat[page + t, pl.ds(r, er, stride=CELL), :], into[t]) for t in range(CELL)
        ]
        outer = nat[page + edge, pl.ds(r, er, stride=CELL), :]
        result = []
        for c in range(CELL):
            value = pieces[(-c) % CELL]
            for g in range(1, CELL):
                value = jnp.where(group == g, pieces[(g - c) % CELL], value)
            result.append((lroll(value, -GROUP * c), lane_gather(outer, halo_index[c])))
        return result

    for r in range(CELL):
        for c, (inner, outer) in enumerate(planes(0, r)):
            X[r * CELL + c, :, 0:LANES] = inner
            X[r * CELL + c, :, LANES : 2 * LANES] = outer
        for c, (inner, outer) in enumerate(planes(1, r)):
            B[r * CELL + c, :, 0:LANES] = inner
            B[r * CELL + c, :, LANES : 2 * LANES] = outer
        both = zip(planes(2, r), planes(3, r))
        for c, (kappas, masses) in enumerate(both):
            for half in range(2):
                lanes = slice(half * LANES, (half + 1) * LANES)
                S[r * CELL + c, :, lanes] = kappas[half] * masses[half] + 4.0
                I[r * CELL + c, :, lanes] = 1.0 / masses[half]

    energy = jnp.zeros((SUB, LANES), F32)
    for r in range(CELL):
        for c in range(CELL):
            plane = r * CELL + c
            field = X[plane]
            first = S[plane] * field - neighbour_sum(X, r, c)
            scaled = I[plane] * first
            W[plane] = scaled
            energy = energy + fold(
                (0.5 * scaled * first - B[plane] * field)[0:mr, 0:LANES]
            )
    EN[0] = energy

    for colour in range(COLOURS):
        nodes_here = block_nodes(colour)
        inv = [I[r * CELL + c] for r, c in nodes_here]
        stiff = [S[r * CELL + c] for r, c in nodes_here]
        scaled = [stiff[n] * inv[n] for n in range(4)]
        diag = [
            stiff[n] * scaled[n] + neighbour_sum(I, *nodes_here[n]) for n in range(4)
        ]
        m01, m02 = -(scaled[0] + scaled[1]), -(scaled[0] + scaled[2])
        m13, m23 = -(scaled[1] + scaled[3]), -(scaled[2] + scaled[3])
        m03, m12 = inv[1] + inv[2], inv[0] + inv[3]
        r0 = lax.rsqrt(diag[0])
        l10, l20, l30 = m01 * r0, m02 * r0, m03 * r0
        r1 = lax.rsqrt(diag[1] - l10 * l10)
        l21, l31 = (m12 - l20 * l10) * r1, (m13 - l30 * l10) * r1
        r2 = lax.rsqrt(diag[2] - l20 * l20 - l21 * l21)
        l32 = (m23 - l30 * l20 - l31 * l21) * r2
        r3 = lax.rsqrt(diag[3] - l30 * l30 - l31 * l31 - l32 * l32)
        for n, value in enumerate((r0, r1, r2, r3, l10, l20, l30, l21, l31, l32)):
            LM[colour * 10 + n] = value

    def whole(ref, top):
        tile = ref[top : top + SUB, 0:LANES].astype(I32)
        return (tile * SEED_BASE + lroll(tile, LANES - PHASES))[0:1, :]

    base = 4 * HALO
    around = {
        "B": whole(below_ref, base), "T": whole(above_ref, base),
        "R": whole(right_ref, base), "L": whole(left_ref, base),
        "BR": whole(cbelow_ref, 4 * SUB), "BL": whole(cbelow_ref, 5 * SUB),
        "TR": whole(cabove_ref, 4 * SUB), "TL": whole(cabove_ref, 5 * SUB),
    }
    spot = lane % GROUP
    low = sub < HC
    for phase in range(PHASES):
        pick = {
            key: jnp.broadcast_to(value[:, phase : phase + 1], (SUB, LANES))
            for key, value in around.items()
        }
        ST[phase, 0] = jnp.where(low, pick["B"], pick["T"])
        side = jnp.where(spot < GROUP // 2, pick["R"], pick["L"])
        corner_right = jnp.where(low, pick["BR"], pick["TR"])
        corner_left = jnp.where(low, pick["BL"], pick["TL"])
        side = jnp.where((lane >= 2 * HC) & (lane < 3 * HC), corner_right, side)
        side = jnp.where((lane >= HC) & (lane < 2 * HC), corner_left, side)
        ST[phase, 1] = side

    node_row = 2 * CELL * tile_cols
    node_col = 2 * CELL
    offset_main = node_row * sub_iota((mr, LANES)) + node_col * lane_iota((mr, LANES))
    strip_cell = jnp.where(low, sub, sub + mr - 2 * HC)
    offset_strip = node_row * strip_cell + node_col * lane
    side_group = jnp.where(spot < GROUP // 2, lane // GROUP, (lane // GROUP + 1) % CELL)
    side_row = SUB * side_group + sub
    side_col = jnp.where(spot < GROUP // 2, spot, spot + LANES - GROUP)
    in_corner = (lane >= HC) & (lane < 3 * HC)
    side_row = jnp.where(in_corner, strip_cell, side_row)
    side_col = jnp.where(
        in_corner, jnp.where(lane >= 2 * HC, lane - 2 * HC, lane + LANES - 2 * HC), side_col
    )
    offset_side = node_row * side_row + node_col * side_col

    def noise_phase(phase, carry):
        colour = order_ref[phase % COLOURS]
        r0, c0 = 2 * (colour // 2), 2 * (colour % 2)
        own = seeds_ref[0, 0, phase // COLOURS, phase % COLOURS, 0]
        strip_seed = ST[phase, 0]
        side_seed = ST[phase, 1]
        for n in range(4):
            extra = 2 * ((r0 + n // 2) * tile_cols + c0 + n % 2)
            at = phase * 4 + n
            Z[at, 0:mr, 0:LANES] = gaussian(offset_main + (own + extra))
            Z[at, mr:er, 0:LANES] = gaussian(offset_strip + strip_seed + extra)
            side = gaussian(offset_side + side_seed + extra)
            for g in range(mr // SUB):
                Z[at, SUB * g : SUB * (g + 1), LANES : 2 * LANES] = lroll(side, -GROUP * g)
            Z[at, mr:er, LANES : 2 * LANES] = lroll(side, -2 * HC)
        return carry

    lax.fori_loop(0, PHASES, noise_phase, 0)

    def phase_body(colour, phase):
        nodes_here = block_nodes(colour)
        r0, c0 = nodes_here[0]
        own = [r * CELL + c for r, c in nodes_here]
        w = {}
        for r in range(r0 - 1, r0 + 3):
            for c in range(c0 - 1, c0 + 3):
                inside_row, inside_col = r0 <= r <= r0 + 1, c0 <= c <= c0 + 1
                if inside_row or inside_col:
                    w[r, c] = fetch(W, r, c)
        residual = []
        for n, (r, c) in enumerate(nodes_here):
            around_sum = w[r - 1, c] + w[r + 1, c] + w[r, c - 1] + w[r, c + 1]
            residual.append(B[own[n]] - (S[own[n]] * w[r, c] - around_sum))
        q0, q1, q2, q3, l10, l20, l30, l21, l31, l32 = [LM[colour * 10 + n] for n in range(10)]
        z = [Z[phase * 4 + n] for n in range(4)]
        f0 = residual[0] * q0
        f1 = (residual[1] - l10 * f0) * q1
        f2 = (residual[2] - l20 * f0 - l21 * f1) * q2
        f3 = (residual[3] - l30 * f0 - l31 * f1 - l32 * f2) * q3
        y0, y1, y2, y3 = f0 + z[0], f1 + z[1], f2 + z[2], f3 + z[3]
        d3 = y3 * q3
        d2 = (y2 - l32 * d3) * q2
        d1 = (y1 - l21 * d2 - l31 * d3) * q1
        d0 = (y0 - l10 * d1 - l20 * d2 - l30 * d3) * q0
        change = jnp.zeros((SUB, LANES), F32)
        for n, f in enumerate((f0, f1, f2, f3)):
            zi, fi = z[n][0:mr, 0:LANES], f[0:mr, 0:LANES]
            change = change + fold(zi * zi - fi * fi)
        EN[phase + 1] = 0.5 * change
        delta = [d0, d1, d2, d3]
        for n in range(4):
            X[own[n]] = X[own[n]] + delta[n]
        for n, (across, down) in enumerate(((1, 2), (0, 3), (3, 0), (2, 1))):
            step = S[own[n]] * delta[n] - (delta[across] + delta[down])
            W[own[n]] = w[nodes_here[n]] + I[own[n]] * step
        for n, (r, c) in enumerate(nodes_here):
            for rr, cc in ((r - 1 if r == r0 else r + 1, c), (r, c - 1 if c == c0 else c + 1)):
                plane, rows, cols = locate(rr, cc)
                W[plane] = W[plane] - I[plane] * shifted(delta[n], -rows, -cols)

    def run_phase(phase, carry):
        colour = order_ref[phase % COLOURS]
        for option in range(COLOURS):
            @pl.when(colour == option)
            def _():
                phase_body(option, phase)
        return carry

    lax.fori_loop(0, PHASES, run_phase, 0)

    running = EN[0]
    result = jnp.zeros((1, LANES), F32)
    first_row = lane_iota((1, LANES))
    for phase in range(PHASES):
        if phase:
            running = running + EN[phase]
        total = jnp.sum(jnp.sum(running, axis=0, keepdims=True), axis=1, keepdims=True)
        result = jnp.where(first_row == phase, total, result)
    energy_ref[...] = jnp.broadcast_to(result / nodes, energy_ref.shape)

    tall = lane_iota((mr, LANES))
    group_out = tall // GROUP
    back = [GROUP * ((tall % CELL + t) % CELL) + tall // CELL for t in range(CELL)]
    for r in range(CELL):
        turned = [lroll(X[r * CELL + c, 0:mr, 0:LANES], GROUP * c) for c in range(CELL)]
        for t in range(tiles):
            value = turned[(-t) % CELL]
            for g in range(1, CELL):
                value = jnp.where(group_out == g, turned[(g - t) % CELL], value)
            nat[t, pl.ds(r, mr, stride=CELL), :] = lane_gather(value, back[t])
    for t in range(tiles):
        out_ref[:, t * LANES : (t + 1) * LANES] = nat[t, 0:tile_rows, :]


def ring(count, step):
    return [(i, (i + step) % count) for i in range(count)]


def local(initial_field, information, kappa_squared, lumped_mass, noise_seeds, colour_order):
    chains, tile_rows, tile_cols = initial_field.shape
    row_count, col_count = lax.axis_size("row"), lax.axis_size("col")
    devices = row_count * col_count
    nodes = tile_rows * row_count * tile_cols * col_count
    mr = tile_rows // CELL
    er = mr + 2 * HC
    tiles = tile_cols // LANES
    vmem = pl.BlockSpec(memory_space=pltpu.VMEM)
    smem = pl.BlockSpec(memory_space=pltpu.SMEM)
    params = pltpu.CompilerParams(vmem_limit_bytes=32 * 1024 * 1024)
    field = initial_field[0]
    sources = (field, information, kappa_squared, lumped_mass)
    rows_shape = jax.ShapeDtypeStruct((4 * HALO + SUB, tile_cols), F32)
    cols_shape = jax.ShapeDtypeStruct((4 * tile_rows * HALO // LANES + SUB, LANES), F32)
    up, down, left, right = pl.pallas_call(
        pack_kernel,
        in_specs=[smem] + [vmem] * 4,
        out_specs=[vmem] * 4,
        out_shape=[rows_shape, rows_shape, cols_shape, cols_shape],
        compiler_params=params,
        name="pack",
    )(noise_seeds, *sources)
    from_right = lax.ppermute(left, "col", ring(col_count, -1))
    from_left = lax.ppermute(right, "col", ring(col_count, 1))
    from_below = lax.ppermute(up, "row", ring(row_count, -1))
    from_above = lax.ppermute(down, "row", ring(row_count, 1))
    corner_shape = jax.ShapeDtypeStruct((6 * SUB, LANES), F32)
    corner_up, corner_down = pl.pallas_call(
        corner_kernel,
        in_specs=[vmem] * 2,
        out_specs=[vmem] * 2,
        out_shape=[corner_shape, corner_shape],
        compiler_params=params,
        name="corners",
    )(from_right, from_left)
    corner_below = lax.ppermute(corner_up, "row", ring(row_count, -1))
    corner_above = lax.ppermute(corner_down, "row", ring(row_count, 1))
    planes = CELL * CELL
    result, energy = pl.pallas_call(
        functools.partial(main_kernel, tile_rows, tile_cols, nodes),
        in_specs=[smem, smem] + [vmem] * 10,
        out_specs=[vmem] * 2,
        out_shape=[
            jax.ShapeDtypeStruct((tile_rows, tile_cols), F32),
            jax.ShapeDtypeStruct((devices, LANES), F32),
        ],
        scratch_shapes=[
            pltpu.VMEM((4 * (tiles + 1), tile_rows + 2 * HALO, LANES), F32),
            pltpu.VMEM((planes, er, 2 * LANES), F32),
            pltpu.VMEM((planes, er, 2 * LANES), F32),
            pltpu.VMEM((planes, er, 2 * LANES), F32),
            pltpu.VMEM((planes, er, 2 * LANES), F32),
            pltpu.VMEM((planes, er, 2 * LANES), F32),
            pltpu.VMEM((COLOURS * 10, er, 2 * LANES), F32),
            pltpu.VMEM((PHASES * 4, er, 2 * LANES), F32),
            pltpu.VMEM((PHASES + 1, SUB, LANES), F32),
            pltpu.VMEM((PHASES, 2, SUB, LANES), I32),
        ],
        compiler_params=params,
        name="sweeps",
    )(
        colour_order, noise_seeds, *sources,
        from_below, from_above, from_right, from_left, corner_below, corner_above,
    )
    shared = lax.all_to_all(energy, AXES, 0, 0, tiled=True)
    energies = jnp.sum(shared, axis=0)[:PHASES].reshape(SWEEPS, COLOURS, chains)
    return (result[None], energies)


def solution(mesh):
    placed = (
        P(None, "row", "col"),
        P("row", "col"),
        P("row", "col"),
        P("row", "col"),
        P("row", "col", None, None, None),
        P(),
    )
    return jax.shard_map(
        local, mesh=mesh, in_specs=placed, out_specs=(P(None, "row", "col"), P()), check_vma=False
    )
```

time: 582 us -> 44.4 us (0.08); the launches traced: 570 us -> 44.1 us
  local copies, waits for them, and re-layouts: 356 us -> 5.22 us
  other arithmetic: 95.8 us -> 0.05 us
  starting transfers between devices: 49.4 us -> 9.44 us
  blocking collectives: 38.3 us -> 8.85 us
  waiting for transfers between devices: 26.1 us -> 9.91 us
  Pallas kernels: 0 us -> 9.98 us
    slice x98 -> x0, local copies, waits for them, and re-layouts: 236 us -> none  [the longest x84 233 us: corners(): source[..., first_index::2, second_index::2]]
    pad x32 -> x0, local copies, waits for them, and re-layouts: 103 us -> none  [join_corners(): padded = lax.pad(piece, jnp.zeros((), piece.dtype), config)]
    ppermute x40 -> x6, starting transfers between devices: 49.4 us -> 9.44 us  [the longest x1 3.97 us: local(): from_below = lax.ppermute(up, 'row', ring(row_count, -1))]
    select_n x20 -> x0, other arithmetic: 39.5 us -> none  [the longest x16 39.5 us: one_sweep(): jnp.where(chosen, updated[corner], before[corner])]
    psum x1 -> x0, blocking collectives: 38.3 us -> none  [local(): energies = lax.psum(energies, ('row', 'col')) / (total_rows * total_cols)]
    ppermute x40 -> x6, waiting for transfers between devices: 26.1 us -> 9.91 us  [the longest x1 3.54 us: local(): from_left = lax.ppermute(right, 'col', ring(col_count, 1))]
    another operation x10 -> x0, other arithmetic: 16 us -> none
    pallas_call x0 -> x3, Pallas kernels: none -> 9.98 us  [the longest x1 9.12 us: local(): pl.pallas_call(functools.partial(main_kernel, tile_rows, tile_cols, nodes...]
  transfers between devices with their start and end apart: 40 -> 6, of which waited for: 15 -> 4; matrix products, arithmetic and copies ran while one was open for 20% -> 0% of each run, Pallas kernels for 0% -> 0%
where the time goes in v1:
time: 44.4 us; the launch traced here: 44.1 us
  Pallas kernels  9.98 us (22%)
  waiting for transfers between devices  9.91 us (22%)
  starting transfers between devices  9.44 us (21%)
  blocking collectives  8.85 us (20%)
  local copies, waits for them, and re-layouts  5.22 us (12%)
  between operations  0.67 us (2%)
    pallas_call x1, Pallas kernels, local(): pl.pallas_call(functools.partial(main_kernel, tile_rows, tile_cols, nodes...  9.12 us
    all_to_all x1, blocking collectives, local(): shared = lax.all_to_all(energy, AXES, 0, 0, tiled=True)  8.85 us
    unnamed x13, local copies, waits for them, and re-layouts  4.58 us
    ppermute x1, starting transfers between devices, local(): from_below = lax.ppermute(up, 'row', ring(row_count, -1))  3.97 us
    ppermute x1, waiting for transfers between devices, local(): from_left = lax.ppermute(right, 'col', ring(col_count, 1))  3.54 us
    ppermute x1, waiting for transfers between devices, local(): corner_above = lax.ppermute(corner_down, 'row', ring(row_count, 1))  3.2 us
    ppermute x1, starting transfers between devices, local(): from_right = lax.ppermute(left, 'col', ring(col_count, -1))  2.76 us
    ppermute x1, starting transfers between devices, local(): corner_below = lax.ppermute(corner_up, 'row', ring(row_count, -1))  2.69 us
  transfers between devices with their start and end apart: 6, of which 4 were waited for; matrix products, arithmetic and copies ran while one was open for 0% of the time, Pallas kernels for 0%

profile of v1, /device:TPU:0, one launch (start us, length us, event | category | flops | bytes accessed | tf_op | source)
XLA Modules:
  0.0 44.1 jit_solution(13862350245435360884)
XLA Ops:
  0.6 0.8 %copy.12.seeds_ref = s32[1,1,2,4,1]{4,3,2,1,0:T(4,128)S(1)} copy(s32[1,1,2,4,1]{3,4,2,1,0:T(1,128)} %param.10) | data formatting | bytes 64 | tf_op args[4]
  1.4 0.0 copy-start
  1.4 0.9 %copy-done = f32[1,128,512]{2,1,0:T(8,128)S(1)} copy-done((f32[1,128,512]{2,1,0:T(8,128)S(1)}, f32[1,128,512]{2,1,0:T(8,128)}, u32[]{:S(2)}) %copy-start) | copy-done | bytes 262168
  2.4 0.0 copy-start.2
  2.4 0.9 %copy-done.2 = f32[128,512]{1,0:T(8,128)S(1)} copy-done((f32[128,512]{1,0:T(8,128)S(1)}, f32[128,512]{1,0:T(8,128)}, u32[]{:S(2)}) %copy-start.2) | copy-done | bytes 262168
  3.3 0.0 copy-start.3
  3.3 0.9 %copy-done.3 = f32[128,512]{1,0:T(8,128)S(1)} copy-done((f32[128,512]{1,0:T(8,128)S(1)}, f32[128,512]{1,0:T(8,128)}, u32[]{:S(2)}) %copy-start.3) | copy-done | bytes 262168
  4.3 0.0 copy-start.4
  4.3 0.9 %copy-done.4 = f32[128,512]{1,0:T(8,128)S(1)} copy-done((f32[128,512]{1,0:T(8,128)S(1)}, f32[128,512]{1,0:T(8,128)}, u32[]{:S(2)}) %copy-start.4) | copy-done | bytes 262168
  5.2 0.0 copy-start.1
  5.2 0.8 %pack.1 = (f32[72,512]{1,0:T(8,128)S(1)}, f32[72,512]{1,0:T(8,128)S(1)}, f32[72,128]{1,0:T(8,128)S(1)}, f32[72,128]{1,0:T(8,128)S(1)}) custom-call(s32[1,1,2,4,1]{4,3,2,1,0:T(4,128)S(1)} %copy.12.seeds_ref, f32[128,512]{1,0:T(8,128)S(1)} %bitcast.7, f32[128,512]{1,0:T(8,128)S(1)} %copy-done.2, f32[128,512]{1,0:T(8,128)S(1)} %copy-done.3, ...), custom_call_target="tpu_custom_call" | custom-call | tf_op jit(solution)/shard_map/pack/pallas_call | solution.py:429
  6.0 4.0 %collective-permute-start = (f32[72,512]{1,0:T(8,128)S(1)}, f32[72,512]{1,0:T(8,128)S(1)}, u32[]{:S(2)}, u32[]{:S(2)}) collective-permute-start(f32[72,512]{1,0:T(8,128)S(1)} %get-tuple-element.10), channel_id=1, source_target_pairs={{0,24},{8,0},{16,8},{24,16},{1,25},{9,1},{17,9},{25,17},{2,26},{10... | collective-permute-start | bytes 442376 | tf_op jit(solution)/shard_map/ppermute | solution.py:439
  10.0 0.0 collective-permute-start.1
  10.0 2.8 %collective-permute-start.2 = (f32[72,128]{1,0:T(8,128)S(1)}, f32[72,128]{1,0:T(8,128)S(1)}, u32[]{:S(2)}, u32[]{:S(2)}) collective-permute-start(f32[72,128]{1,0:T(8,128)S(1)} %get-tuple-element.12), channel_id=1, source_target_pairs={{0,7},{1,0},{2,1},{3,2},{4,3},{5,4},{6,5},{7,6},{8,15},{9,8},{10,9... | collective-permute-start | bytes 110600 | tf_op jit(solution)/shard_map/ppermute | solution.py:437
  12.7 0.0 collective-permute-start.3
  12.7 1.6 %collective-permute-done.2.right_ref = f32[72,128]{1,0:T(8,128)S(1)} collective-permute-done((f32[72,128]{1,0:T(8,128)S(1)}, f32[72,128]{1,0:T(8,128)S(1)}, u32[]{:S(2)}, u32[]{:S(2)}) %collective-permute-start.2) | collective-permute-done | bytes 36896 | tf_op jit(solution)/shard_map/ppermute | solution.py:437
  14.4 3.5 %collective-permute-done.3.left_ref = f32[72,128]{1,0:T(8,128)S(1)} collective-permute-done((f32[72,128]{1,0:T(8,128)S(1)}, f32[72,128]{1,0:T(8,128)S(1)}, u32[]{:S(2)}, u32[]{:S(2)}) %collective-permute-start.3) | collective-permute-done | bytes 36896 | tf_op jit(solution)/shard_map/ppermute | solution.py:438
  17.9 0.1 corners.1
  18.0 0.0 copy-start.5
  18.0 2.7 %collective-permute-start.4 = (f32[48,128]{1,0:T(8,128)S(1)}, f32[48,128]{1,0:T(8,128)S(1)}, u32[]{:S(2)}, u32[]{:S(2)}) collective-permute-start(f32[48,128]{1,0:T(8,128)S(1)} %get-tuple-element.14), channel_id=1, source_target_pairs={{0,24},{8,0},{16,8},{24,16},{1,25},{9,1},{17,9},{25,17},{2,26},{10... | collective-permute-start | bytes 73736 | tf_op jit(solution)/shard_map/ppermute | solution.py:450
  20.7 0.0 collective-permute-start.5
  20.7 1.5 %collective-permute-done.4.cbelow_ref = f32[48,128]{1,0:T(8,128)S(1)} collective-permute-done((f32[48,128]{1,0:T(8,128)S(1)}, f32[48,128]{1,0:T(8,128)S(1)}, u32[]{:S(2)}, u32[]{:S(2)}) %collective-permute-start.4) | collective-permute-done | bytes 24608 | tf_op jit(solution)/shard_map/ppermute | solution.py:450
  22.2 3.2 %collective-permute-done.5.cabove_ref = f32[48,128]{1,0:T(8,128)S(1)} collective-permute-done((f32[48,128]{1,0:T(8,128)S(1)}, f32[48,128]{1,0:T(8,128)S(1)}, u32[]{:S(2)}, u32[]{:S(2)}) %collective-permute-start.5) | collective-permute-done | bytes 24608 | tf_op jit(solution)/shard_map/ppermute | solution.py:451
  25.4 0.0 collective-permute-done.below_ref
  25.4 0.0 collective-permute-done.1.above_ref
  25.4 0.0 copy-done.1
  25.4 0.0 copy-done.5
  25.4 9.1 %sweeps.1 = (f32[128,512]{1,0:T(8,128)}, f32[32,128]{1,0:T(8,128)S(1)}) custom-call(s32[4]{0:T(128)S(1)} %copy-done.5, s32[1,1,2,4,1]{4,3,2,1,0:T(4,128)S(1)} %copy.12.seeds_ref, f32[128,512]{1,0:T(8,128)S(1)} %bitcast.8, f32[128,512]{1,0:T(8,128)S(1)} %copy-done.2, f32[128,512]{1,0:T(8,128)S(1)} %copy-done.3, f32[128,512]{1,0:T(8,128)S(1)} %copy-done.4, ...), custom_call_target="tpu_custom_call" | custom-call | tf_op jit(solution)/shard_map/sweeps/pallas_call | solution.py:453
  34.6 8.8 %all_to_all.9 = f32[32,1,128]{2,1,0:T(1,128)S(1)} all-to-all(f32[32,1,128]{2,1,0:T(1,128)S(1)} %bitcast.9), channel_id=1, replica_groups=mesh['row'=4,'col'=8] {'row','col'}, dimensions={0} | all-to-all | bytes 32768 | tf_op jit(solution)/shard_map/all_to_all | solution.py:479
  43.4 0.1 reduce_sum.9
  43.5 0.6 %reshape.17 = f32[2,4,1]{1,0,2:T(2,128)} reshape(f32[8]{0:T(128)S(1)} %bitcast.10) | data formatting | bytes 64 | tf_op jit(solution)/shard_map/reshape | solution.py:480
Async XLA Ops:
  1.4 0.9 %copy-start = (f32[1,128,512]{2,1,0:T(8,128)S(1)}, f32[1,128,512]{2,1,0:T(8,128)}, u32[]{:S(2)}) copy-start(f32[1,128,512]{2,1,0:T(8,128)} %param.6) | copy-start | bytes 786436
  2.4 0.9 %copy-start.2 = (f32[128,512]{1,0:T(8,128)S(1)}, f32[128,512]{1,0:T(8,128)}, u32[]{:S(2)}) copy-start(f32[128,512]{1,0:T(8,128)} %b_ref.1) | copy-start | bytes 786436
  3.3 0.9 %copy-start.3 = (f32[128,512]{1,0:T(8,128)S(1)}, f32[128,512]{1,0:T(8,128)}, u32[]{:S(2)}) copy-start(f32[128,512]{1,0:T(8,128)} %kappa_ref.1) | copy-start | bytes 786436
  4.3 0.9 %copy-start.4 = (f32[128,512]{1,0:T(8,128)S(1)}, f32[128,512]{1,0:T(8,128)}, u32[]{:S(2)}) copy-start(f32[128,512]{1,0:T(8,128)} %mass_ref.1) | copy-start | bytes 786436
  5.2 20.2 %copy-start.1 = (f32[1,128,512]{2,1,0:T(8,128)S(1)}, f32[1,128,512]{2,1,0:T(8,128)}, u32[]{:S(2)}) copy-start(f32[1,128,512]{2,1,0:T(8,128)} %param.6) | copy-start | bytes 786436
  6.0 19.4 %collective-permute-start = (f32[72,512]{1,0:T(8,128)S(1)}, f32[72,512]{1,0:T(8,128)S(1)}, u32[]{:S(2)}, u32[]{:S(2)}) collective-permute-start(f32[72,512]{1,0:T(8,128)S(1)} %get-tuple-element.10), channel_id=1, source_target_pairs={{0,24},{8,0},{16,8},{24,16},{1,25},{9,1},{17,9},{25,17},{2,26},{10... | collective-permute-start | bytes 442376 | tf_op jit(solution)/shard_map/ppermute | solution.py:439
  10.0 15.5 %collective-permute-start.1 = (f32[72,512]{1,0:T(8,128)S(1)}, f32[72,512]{1,0:T(8,128)S(1)}, u32[]{:S(2)}, u32[]{:S(2)}) collective-permute-start(f32[72,512]{1,0:T(8,128)S(1)} %get-tuple-element.11), channel_id=1, source_target_pairs={{0,8},{8,16},{16,24},{24,0},{1,9},{9,17},{17,25},{25,1},{2,10},{10... | collective-permute-start | bytes 442376 | tf_op jit(solution)/shard_map/ppermute | solution.py:440
  10.0 4.4 %collective-permute-start.2 = (f32[72,128]{1,0:T(8,128)S(1)}, f32[72,128]{1,0:T(8,128)S(1)}, u32[]{:S(2)}, u32[]{:S(2)}) collective-permute-start(f32[72,128]{1,0:T(8,128)S(1)} %get-tuple-element.12), channel_id=1, source_target_pairs={{0,7},{1,0},{2,1},{3,2},{4,3},{5,4},{6,5},{7,6},{8,15},{9,8},{10,9... | collective-permute-start | bytes 110600 | tf_op jit(solution)/shard_map/ppermute | solution.py:437
  12.7 5.2 %collective-permute-start.3 = (f32[72,128]{1,0:T(8,128)S(1)}, f32[72,128]{1,0:T(8,128)S(1)}, u32[]{:S(2)}, u32[]{:S(2)}) collective-permute-start(f32[72,128]{1,0:T(8,128)S(1)} %get-tuple-element.13), channel_id=1, source_target_pairs={{0,1},{1,2},{2,3},{3,4},{4,5},{5,6},{6,7},{7,0},{8,9},{9,10},{10,1... | collective-permute-start | bytes 110600 | tf_op jit(solution)/shard_map/ppermute | solution.py:438
  18.0 7.4 %copy-start.5 = (s32[4]{0:T(128)S(1)}, s32[4]{0:T(128)}, u32[]{:S(2)}) copy-start(s32[4]{0:T(128)} %order_ref.1) | copy-start | bytes 52
  18.0 4.2 %collective-permute-start.4 = (f32[48,128]{1,0:T(8,128)S(1)}, f32[48,128]{1,0:T(8,128)S(1)}, u32[]{:S(2)}, u32[]{:S(2)}) collective-permute-start(f32[48,128]{1,0:T(8,128)S(1)} %get-tuple-element.14), channel_id=1, source_target_pairs={{0,24},{8,0},{16,8},{24,16},{1,25},{9,1},{17,9},{25,17},{2,26},{10... | collective-permute-start | bytes 73736 | tf_op jit(solution)/shard_map/ppermute | solution.py:450
  20.7 4.7 %collective-permute-start.5 = (f32[48,128]{1,0:T(8,128)S(1)}, f32[48,128]{1,0:T(8,128)S(1)}, u32[]{:S(2)}, u32[]{:S(2)}) collective-permute-start(f32[48,128]{1,0:T(8,128)S(1)} %get-tuple-element.15), channel_id=1, source_target_pairs={{0,8},{8,16},{16,24},{24,0},{1,9},{9,17},{17,25},{25,1},{2,10},{10... | collective-permute-start | bytes 73736 | tf_op jit(solution)/shard_map/ppermute | solution.py:451

commit v2 on v1

v2 whole, which is shorter than its diff:
```python
import functools

import jax
import jax.numpy as jnp
from jax import lax
from jax.experimental import pallas as pl
from jax.experimental.pallas import tpu as pltpu
from jax.sharding import PartitionSpec as P

SWEEPS = 2
COLOURS = 4
PHASES = SWEEPS * COLOURS
HALO = 2 * PHASES
CELL = 4
HC = HALO // CELL
LANES = 128
SUB = 8
GROUP = LANES // CELL
AXES = ("row", "col")
F32 = jnp.float32
I32 = jnp.int32

unit_step = 1.0 / 8388608.0
mix_factor = 73244475
SEED_BASE = 32768

SIN_COEFFS = (
    6.283185306485777,
    -41.34170192921984,
    81.60520938153618,
    -76.70366601553475,
    41.99996083008805,
    -14.336855962945094,
)


def lane_iota(shape):
    return lax.broadcasted_iota(I32, shape, len(shape) - 1)


def sub_iota(shape):
    return lax.broadcasted_iota(I32, shape, len(shape) - 2)


def lane_gather(value, index):
    return jnp.take_along_axis(value, index, axis=1, mode="promise_in_bounds")


def lroll(value, amount):
    amount = amount % value.shape[1]
    return pltpu.roll(value, amount, 1) if amount else value


def pack_kernel(seeds_ref, *refs):
    sources, (up_ref, down_ref, left_ref, right_ref) = refs[:4], refs[4:8]
    edges, seeds_buf, sems = refs[8:]
    rows, cols = sources[0].shape
    per = LANES // HALO
    lane = lane_iota((SUB, LANES))
    copies = []

    def copy(source, target):
        made = pltpu.make_async_copy(source, target, sems.at[len(copies)])
        made.start()
        copies.append(made)

    copy(seeds_ref, seeds_buf)
    for a, source in enumerate(sources):
        copy(source.at[:, pl.ds(0, LANES)], edges.at[2 * a])
        copy(source.at[:, pl.ds(cols - LANES, LANES)], edges.at[2 * a + 1])
    for a, source in enumerate(sources):
        copy(source.at[pl.ds(0, HALO)], up_ref.at[pl.ds(a * HALO, HALO)])
        copy(source.at[pl.ds(rows - HALO, HALO)], down_ref.at[pl.ds(a * HALO, HALO)])
    copies[0].wait()
    base = 4 * HALO
    for sweep in range(SWEEPS):
        seeds = seeds_buf[0, 0, sweep]
        high = (seeds // SEED_BASE).astype(F32)
        low = (seeds % SEED_BASE).astype(F32)
        for out in (up_ref, down_ref, left_ref, right_ref):
            out[base + sweep : base + sweep + 1, 0:COLOURS] = high
            out[base + SWEEPS + sweep : base + SWEEPS + sweep + 1, 0:COLOURS] = low
    for a in range(4):
        for edge, out in ((0, left_ref), (1, right_ref)):
            copies[1 + 2 * a + edge].wait()
            for v in range(rows // (SUB * per)):
                packed = jnp.zeros((SUB, LANES), F32)
                for q in range(per):
                    top = SUB * (v * per + q)
                    piece = edges[2 * a + edge, top : top + SUB, :]
                    piece = lroll(piece, HALO * q - (LANES - HALO if edge else 0))
                    packed = jnp.where(lane // HALO == q, piece, packed)
                out[a * HALO + SUB * v : a * HALO + SUB * (v + 1), :] = packed
    for made in copies[9:]:
        made.wait()


def corner_kernel(right_ref, left_ref, up_ref, down_ref):
    lane = lane_iota((SUB, LANES))
    for a in range(4):
        for out, top, shift in ((up_ref, 0, 0), (down_ref, HALO - SUB, 2 * HALO)):
            r = right_ref[a * HALO + top : a * HALO + top + SUB, :]
            l = left_ref[a * HALO + top : a * HALO + top + SUB, :]
            r = lroll(r, shift)
            l = lroll(l, shift + 2 * HALO)
            out[a * SUB : (a + 1) * SUB, :] = jnp.where(lane < 2 * HALO, r, l)
    for out in (up_ref, down_ref):
        out[4 * SUB : 5 * SUB, :] = right_ref[4 * HALO : 4 * HALO + SUB, :]
        out[5 * SUB : 6 * SUB, :] = left_ref[4 * HALO : 4 * HALO + SUB, :]


def scramble(hashed):
    sixteen = jnp.full_like(hashed, 16)
    hashed = hashed ^ lax.shift_right_logical(hashed, sixteen)
    hashed = hashed * mix_factor
    hashed = hashed ^ lax.shift_right_logical(hashed, sixteen)
    hashed = hashed * mix_factor
    return hashed ^ lax.shift_right_logical(hashed, sixteen)


def gaussian(first):
    nine = jnp.full_like(first, 9)
    one = lax.shift_right_logical(scramble(first), nine).astype(F32)
    two = lax.shift_right_logical(scramble(first + 1), nine).astype(F32)
    u1 = (one + 1.0) * unit_step
    v = 0.25 - jnp.abs(two * unit_step - 0.5)
    square = v * v
    poly = jnp.full_like(v, SIN_COEFFS[-1])
    for coeff in SIN_COEFFS[-2::-1]:
        poly = poly * square + coeff
    return jnp.sqrt(-2.0 * jnp.log(u1)) * (-(v * poly))


BASE = SUB


def whole_rows(er, shift=0):
    return pl.ds(BASE + shift, er)


def lane_shift(value, cols):
    if not cols:
        return value
    moved = pltpu.roll(value, (-cols) % LANES, 2)
    other = jnp.concatenate([moved[1:2], moved[0:1]], axis=0)
    edge = LANES - 1 if cols > 0 else 0
    return jnp.where(lane_iota(value.shape) == edge, other, moved)


def locate(r, c):
    return (r % CELL) * CELL + c % CELL, r // CELL, c // CELL


def fetch(ref, er, r, c):
    plane, rows, cols = locate(r, c)
    return lane_shift(ref[plane, :, whole_rows(er, rows), :], cols)


def neighbour_sum(ref, er, r, c):
    return (
        fetch(ref, er, r - 1, c)
        + fetch(ref, er, r + 1, c)
        + fetch(ref, er, r, c - 1)
        + fetch(ref, er, r, c + 1)
    )


def fold(value):
    value = value[0]
    count = value.shape[0]
    sub = sub_iota((SUB, LANES))
    total = jnp.where(sub >= HC, value[0:SUB], value[count - SUB : count])
    for top in range(SUB, count - SUB, SUB):
        total = total + value[top : top + SUB]
    return total


def block_nodes(colour):
    r0, c0 = 2 * (colour // 2), 2 * (colour % 2)
    return [(r0, c0), (r0, c0 + 1), (r0 + 1, c0), (r0 + 1, c0 + 1)]


def column_planes(pieces):
    wide = lane_iota(pieces[0].shape)
    group = wide // GROUP
    turned = [
        lane_gather(piece, CELL * (wide % GROUP) + (group + CELL - t) % CELL)
        for t, piece in enumerate(pieces)
    ]
    result = []
    for c in range(CELL):
        value = turned[(-c) % CELL]
        for g in range(1, CELL):
            value = jnp.where(group == g, turned[(g - c) % CELL], value)
        result.append(lroll(value, -GROUP * c))
    return result


def natural_columns(planes):
    wide = lane_iota(planes[0].shape)
    group = wide // GROUP
    turned = [lroll(plane, GROUP * c) for c, plane in enumerate(planes)]
    result = []
    for t in range(CELL):
        value = turned[(-t) % CELL]
        for g in range(1, CELL):
            value = jnp.where(group == g, turned[(g - t) % CELL], value)
        back = GROUP * ((wide % CELL + t) % CELL) + wide // CELL
        result.append(lane_gather(value, back))
    return result


def node_offsets(tile_cols, row_cell, col_cell):
    return 2 * CELL * tile_cols * row_cell + 2 * CELL * col_cell


def prepare_kernel(
    tile_rows, tile_cols,
    order_ref, seeds_ref, x_ref, b_ref, kappa_ref, mass_ref, after_ref,
    X, B, S, I, Z,
    nat, sems,
):
    del after_ref
    mr = tile_rows // CELL
    tiles = tile_cols // LANES
    copies = []
    for a, source in enumerate((x_ref, b_ref, kappa_ref, mass_ref)):
        for t in range(tiles):
            made = pltpu.make_async_copy(
                source.at[:, pl.ds(t * LANES, LANES)], nat.at[a * tiles + t], sems.at[a * tiles + t]
            )
            made.start()
            copies.append(made)
    rows = pl.ds(BASE + HC, mr)
    offset_main = node_offsets(tile_cols, sub_iota((mr, LANES)), lane_iota((mr, LANES)))

    def noise_phase(phase, carry):
        colour = order_ref[phase % COLOURS]
        r0, c0 = 2 * (colour // 2), 2 * (colour % 2)
        own = seeds_ref[0, 0, phase // COLOURS, 0, phase % COLOURS]
        for n in range(4):
            extra = 2 * ((r0 + n // 2) * tile_cols + c0 + n % 2)
            Z[phase * 4 + n, 0, rows, :] = gaussian(offset_main + (own + extra))
        return carry

    lax.fori_loop(0, PHASES, noise_phase, 0)

    for made in copies:
        made.wait()

    def planes(a, r):
        return column_planes(
            [nat[a * tiles + t, pl.ds(r, mr, stride=CELL), :] for t in range(tiles)]
        )

    for r in range(CELL):
        for c, value in enumerate(planes(0, r)):
            X[r * CELL + c, 0, rows, :] = value
        for c, value in enumerate(planes(1, r)):
            B[r * CELL + c, 0, rows, :] = value
        for c, (kappa, mass) in enumerate(zip(planes(2, r), planes(3, r))):
            S[r * CELL + c, 0, rows, :] = kappa * mass + 4.0
            I[r * CELL + c, 0, rows, :] = 1.0 / mass


def sweep_kernel(
    tile_rows, tile_cols, nodes,
    order_ref, x_in, b_in, s_in, i_in, z_in,
    below_ref, above_ref, right_ref, left_ref, cbelow_ref, cabove_ref,
    out_ref, energy_ref, X, B, S, I, Z,
    nat, strip, W, LM, EN, ST,
):
    del x_in, b_in, s_in, i_in, z_in
    mr = tile_rows // CELL
    er = mr + 2 * HC
    tiles = tile_cols // LANES
    lane = lane_iota((SUB, LANES))
    sub = sub_iota((SUB, LANES))
    per = LANES // HALO
    every = whole_rows(er)
    top_rows, low_rows = pl.ds(BASE, HC), pl.ds(BASE + HC + mr, HC)

    for a in range(4):
        for t in range(tiles):
            lanes = slice(t * LANES, (t + 1) * LANES)
            for start, source in ((0, above_ref), (HALO, below_ref)):
                strip[a * tiles + t, start : start + HALO, :] = source[
                    a * HALO : (a + 1) * HALO, lanes
                ]

        def put(top, right, left):
            nat[a, top : top + SUB, :] = jnp.where(
                lane < HALO, right, jnp.where(lane >= LANES - HALO, left, 1.0)
            )

        for g in range(tile_rows // SUB):
            v, q = g // per, g % per
            rows = slice(a * HALO + SUB * v, a * HALO + SUB * (v + 1))
            put(
                HALO + SUB * g,
                lroll(right_ref[rows, :], -HALO * q),
                lroll(left_ref[rows, :], LANES - HALO - HALO * q),
            )
        for start, corner in ((0, cabove_ref), (HALO + tile_rows, cbelow_ref)):
            value = corner[a * SUB : (a + 1) * SUB, :]
            for h in range(HALO // SUB):
                put(
                    start + SUB * h,
                    lroll(value, -HALO * h),
                    lroll(value, LANES - HALO - 2 * HALO - HALO * h),
                )

    wide = lane_iota((er, LANES))
    halo_index = [CELL * (wide % GROUP) + c for c in range(CELL)]

    def strip_planes(a, r):
        return column_planes(
            [strip[a * tiles + t, pl.ds(r, SUB, stride=CELL), :] for t in range(tiles)]
        )

    def side_planes(a, r):
        outer = nat[a, pl.ds(r, er, stride=CELL), :]
        return [lane_gather(outer, halo_index[c]) for c in range(CELL)]

    def put_strip(ref, plane, value):
        ref[plane, 0, top_rows, :] = value[0:HC]
        ref[plane, 0, low_rows, :] = value[HC:SUB]

    for r in range(CELL):
        for a, ref in ((0, X), (1, B)):
            for c, value in enumerate(strip_planes(a, r)):
                put_strip(ref, r * CELL + c, value)
            for c, value in enumerate(side_planes(a, r)):
                ref[r * CELL + c, 1, every, :] = value
        for c, (kappa, mass) in enumerate(zip(strip_planes(2, r), strip_planes(3, r))):
            put_strip(S, r * CELL + c, kappa * mass + 4.0)
            put_strip(I, r * CELL + c, 1.0 / mass)
        for c, (kappa, mass) in enumerate(zip(side_planes(2, r), side_planes(3, r))):
            S[r * CELL + c, 1, every, :] = kappa * mass + 4.0
            I[r * CELL + c, 1, every, :] = 1.0 / mass

    energy = jnp.zeros((SUB, LANES), F32)
    for r in range(CELL):
        for c in range(CELL):
            plane = r * CELL + c
            field = X[plane, :, every, :]
            first = S[plane, :, every, :] * field - neighbour_sum(X, er, r, c)
            scaled = I[plane, :, every, :] * first
            W[plane, :, every, :] = scaled
            energy = energy + fold(0.5 * scaled * first - B[plane, :, every, :] * field)
    EN[0] = energy

    for colour in range(COLOURS):
        nodes_here = block_nodes(colour)
        inv = [I[r * CELL + c, :, every, :] for r, c in nodes_here]
        stiff = [S[r * CELL + c, :, every, :] for r, c in nodes_here]
        scaled = [stiff[n] * inv[n] for n in range(4)]
        diag = [stiff[n] * scaled[n] + neighbour_sum(I, er, *nodes_here[n]) for n in range(4)]
        m01, m02 = -(scaled[0] + scaled[1]), -(scaled[0] + scaled[2])
        m13, m23 = -(scaled[1] + scaled[3]), -(scaled[2] + scaled[3])
        m03, m12 = inv[1] + inv[2], inv[0] + inv[3]
        r0 = lax.rsqrt(diag[0])
        l10, l20, l30 = m01 * r0, m02 * r0, m03 * r0
        r1 = lax.rsqrt(diag[1] - l10 * l10)
        l21, l31 = (m12 - l20 * l10) * r1, (m13 - l30 * l10) * r1
        r2 = lax.rsqrt(diag[2] - l20 * l20 - l21 * l21)
        l32 = (m23 - l30 * l20 - l31 * l21) * r2
        r3 = lax.rsqrt(diag[3] - l30 * l30 - l31 * l31 - l32 * l32)
        for n, value in enumerate((r0, r1, r2, r3, l10, l20, l30, l21, l31, l32)):
            LM[colour * 10 + n] = value

    def whole(ref, top):
        tile = ref[top : top + SUB, 0:LANES].astype(I32)
        return tile[0:SWEEPS] * SEED_BASE + tile[SWEEPS : 2 * SWEEPS]

    base = 4 * HALO
    around = {
        "B": whole(below_ref, base), "T": whole(above_ref, base),
        "R": whole(right_ref, base), "L": whole(left_ref, base),
        "BR": whole(cbelow_ref, 4 * SUB), "BL": whole(cbelow_ref, 5 * SUB),
        "TR": whole(cabove_ref, 4 * SUB), "TL": whole(cabove_ref, 5 * SUB),
    }
    spot = lane % GROUP
    high = sub < HC
    in_right_corner = (lane >= 2 * HC) & (lane < 3 * HC)
    in_left_corner = (lane >= HC) & (lane < 2 * HC)
    in_corner = in_right_corner | in_left_corner
    for phase in range(PHASES):
        sweep, k = phase // COLOURS, phase % COLOURS
        pick = {
            key: jnp.broadcast_to(value[sweep : sweep + 1, k : k + 1], (SUB, LANES))
            for key, value in around.items()
        }
        ST[phase, 0] = jnp.where(high, pick["T"], pick["B"])
        side = jnp.where(spot < GROUP // 2, pick["R"], pick["L"])
        side = jnp.where(in_right_corner, jnp.where(high, pick["TR"], pick["BR"]), side)
        ST[phase, 1] = jnp.where(in_left_corner, jnp.where(high, pick["TL"], pick["BL"]), side)

    strip_cell = jnp.where(high, sub + mr - HC, sub - HC)
    offset_strip = node_offsets(tile_cols, strip_cell, lane)
    is_right = spot < GROUP // 2
    side_row = SUB * jnp.where(is_right, lane // GROUP, (lane // GROUP + 1) % CELL) + sub
    side_row = jnp.where(in_corner, strip_cell, side_row)
    side_col = jnp.where(is_right, spot, spot + LANES - GROUP)
    side_col = jnp.where(in_right_corner, lane - 2 * HC, side_col)
    side_col = jnp.where(in_left_corner, lane + LANES - 2 * HC, side_col)
    offset_side = node_offsets(tile_cols, side_row, side_col)

    def noise_phase(phase, carry):
        colour = order_ref[phase % COLOURS]
        r0, c0 = 2 * (colour // 2), 2 * (colour % 2)
        strip_seed = ST[phase, 0]
        side_seed = ST[phase, 1]
        for n in range(4):
            extra = 2 * ((r0 + n // 2) * tile_cols + c0 + n % 2)
            at = phase * 4 + n
            value = gaussian(offset_strip + strip_seed + extra)
            put_strip(Z, at, value)
            side = gaussian(offset_side + side_seed + extra)
            for g in range(mr // SUB):
                Z[at, 1, pl.ds(BASE + HC + SUB * g, SUB), :] = lroll(side, -GROUP * g)
            value = lroll(side, -2 * HC)
            Z[at, 1, top_rows, :] = value[0:HC]
            Z[at, 1, low_rows, :] = value[HC:SUB]
        return carry

    lax.fori_loop(0, PHASES, noise_phase, 0)

    def phase_body(colour, phase):
        nodes_here = block_nodes(colour)
        r0, c0 = nodes_here[0]
        own = [r * CELL + c for r, c in nodes_here]
        w = {}
        for r in range(r0 - 1, r0 + 3):
            for c in range(c0 - 1, c0 + 3):
                inside_row, inside_col = r0 <= r <= r0 + 1, c0 <= c <= c0 + 1
                if inside_row or inside_col:
                    w[r, c] = fetch(W, er, r, c)
        stiff = [S[plane, :, every, :] for plane in own]
        residual = []
        for n, (r, c) in enumerate(nodes_here):
            around_sum = w[r - 1, c] + w[r + 1, c] + w[r, c - 1] + w[r, c + 1]
            residual.append(B[own[n], :, every, :] - (stiff[n] * w[r, c] - around_sum))
        q0, q1, q2, q3, l10, l20, l30, l21, l31, l32 = [LM[colour * 10 + n] for n in range(10)]
        z = [Z[phase * 4 + n, :, every, :] for n in range(4)]
        f0 = residual[0] * q0
        f1 = (residual[1] - l10 * f0) * q1
        f2 = (residual[2] - l20 * f0 - l21 * f1) * q2
        f3 = (residual[3] - l30 * f0 - l31 * f1 - l32 * f2) * q3
        y0, y1, y2, y3 = f0 + z[0], f1 + z[1], f2 + z[2], f3 + z[3]
        d3 = y3 * q3
        d2 = (y2 - l32 * d3) * q2
        d1 = (y1 - l21 * d2 - l31 * d3) * q1
        d0 = (y0 - l10 * d1 - l20 * d2 - l30 * d3) * q0
        change = jnp.zeros((SUB, LANES), F32)
        for n, f in enumerate((f0, f1, f2, f3)):
            change = change + fold(z[n] * z[n] - f * f)
        EN[phase + 1] = 0.5 * change
        delta = [d0, d1, d2, d3]
        for n in range(4):
            X[own[n], :, every, :] = X[own[n], :, every, :] + delta[n]
        for n, (across, down) in enumerate(((1, 2), (0, 3), (3, 0), (2, 1))):
            step = stiff[n] * delta[n] - (delta[across] + delta[down])
            W[own[n], :, every, :] = w[nodes_here[n]] + I[own[n], :, every, :] * step
        for n, (r, c) in enumerate(nodes_here):
            for rr, cc in ((r - 1 if r == r0 else r + 1, c), (r, c - 1 if c == c0 else c + 1)):
                plane, rows, cols = locate(rr, cc)
                at = whole_rows(er, rows)
                W[plane, :, at, :] = W[plane, :, at, :] - I[plane, :, at, :] * lane_shift(
                    delta[n], -cols
                )

    def run_phase(phase, carry):
        colour = order_ref[phase % COLOURS]
        for option in range(COLOURS):
            @pl.when(colour == option)
            def _():
                phase_body(option, phase)
        return carry

    lax.fori_loop(0, PHASES, run_phase, 0)

    running = EN[0]
    result = jnp.zeros((1, LANES), F32)
    first_row = lane_iota((1, LANES))
    for phase in range(PHASES):
        if phase:
            running = running + EN[phase]
        total = jnp.sum(jnp.sum(running, axis=0, keepdims=True), axis=1, keepdims=True)
        result = jnp.where(first_row == phase, total, result)
    energy_ref[...] = jnp.broadcast_to(result / nodes, energy_ref.shape)

    inside = pl.ds(BASE + HC, mr)
    for r in range(CELL):
        columns = natural_columns([X[r * CELL + c, 0, inside, :] for c in range(CELL)])
        for t, value in enumerate(columns):
            nat[t, pl.ds(r, mr, stride=CELL), :] = value
    for t in range(tiles):
        out_ref[:, t * LANES : (t + 1) * LANES] = nat[t, 0:tile_rows, :]


def ring(count, step):
    return [(i, (i + step) % count) for i in range(count)]


def local(initial_field, information, kappa_squared, lumped_mass, noise_seeds, colour_order):
    chains, tile_rows, tile_cols = initial_field.shape
    row_count, col_count = lax.axis_size("row"), lax.axis_size("col")
    devices = row_count * col_count
    nodes = tile_rows * row_count * tile_cols * col_count
    mr = tile_rows // CELL
    er = mr + 2 * HC
    tiles = tile_cols // LANES
    vmem = pl.BlockSpec(memory_space=pltpu.VMEM)
    smem = pl.BlockSpec(memory_space=pltpu.SMEM)
    hbm = pl.BlockSpec(memory_space=pltpu.HBM)
    params = pltpu.CompilerParams(vmem_limit_bytes=16 * 1024 * 1024)
    field = initial_field[0]
    seeds = jnp.swapaxes(noise_seeds, 3, 4)
    sources = [
        pltpu.with_memory_space_constraint(value, pltpu.HBM)
        for value in (field, information, kappa_squared, lumped_mass)
    ]
    rows_shape = jax.ShapeDtypeStruct((4 * HALO + SUB, tile_cols), F32)
    cols_shape = jax.ShapeDtypeStruct((4 * tile_rows * HALO // LANES + SUB, LANES), F32)
    up, down, left, right = pl.pallas_call(
        pack_kernel,
        in_specs=[hbm] * 5,
        out_specs=[vmem] * 4,
        out_shape=[rows_shape, rows_shape, cols_shape, cols_shape],
        scratch_shapes=[
            pltpu.VMEM((8, tile_rows, LANES), F32),
            pltpu.VMEM(seeds.shape, I32),
            pltpu.SemaphoreType.DMA((17,)),
        ],
        compiler_params=params,
        name="pack",
    )(pltpu.with_memory_space_constraint(seeds, pltpu.HBM), *sources)
    from_right = lax.ppermute(left, "col", ring(col_count, -1))
    from_left = lax.ppermute(right, "col", ring(col_count, 1))
    from_below = lax.ppermute(up, "row", ring(row_count, -1))
    from_above = lax.ppermute(down, "row", ring(row_count, 1))
    corner_shape = jax.ShapeDtypeStruct((6 * SUB, LANES), F32)
    corner_up, corner_down = pl.pallas_call(
        corner_kernel,
        in_specs=[vmem] * 2,
        out_specs=[vmem] * 2,
        out_shape=[corner_shape, corner_shape],
        compiler_params=params,
        name="corners",
    )(from_right, from_left)
    corner_below = lax.ppermute(corner_up, "row", ring(row_count, -1))
    corner_above = lax.ppermute(corner_down, "row", ring(row_count, 1))
    planes = CELL * CELL
    plane_shape = jax.ShapeDtypeStruct((planes, 2, er + 2 * BASE, LANES), F32)
    noise_shape = jax.ShapeDtypeStruct((PHASES * 4, 2, er + 2 * BASE, LANES), F32)
    prepared = pl.pallas_call(
        functools.partial(prepare_kernel, tile_rows, tile_cols),
        in_specs=[smem, smem] + [hbm] * 4 + [vmem],
        out_specs=[vmem] * 5,
        out_shape=[plane_shape] * 4 + [noise_shape],
        scratch_shapes=[
            pltpu.VMEM((4 * tiles, tile_rows, LANES), F32),
            pltpu.SemaphoreType.DMA((4 * tiles,)),
        ],
        compiler_params=params,
        cost_estimate=pl.CostEstimate(flops=20_000_000, bytes_accessed=1_000_000, transcendentals=0),
        name="prepare",
    )(colour_order, seeds, *sources, corner_up)
    result, energy, *_ = pl.pallas_call(
        functools.partial(sweep_kernel, tile_rows, tile_cols, nodes),
        in_specs=[smem] + [vmem] * 11,
        out_specs=[vmem] * 7,
        out_shape=[
            jax.ShapeDtypeStruct((tile_rows, tile_cols), F32),
            jax.ShapeDtypeStruct((devices, LANES), F32),
        ]
        + [plane_shape] * 4
        + [noise_shape],
        input_output_aliases={1: 2, 2: 3, 3: 4, 4: 5, 5: 6},
        scratch_shapes=[
            pltpu.VMEM((max(4, tiles), tile_rows + 2 * HALO, LANES), F32),
            pltpu.VMEM((4 * tiles, 2 * HALO, LANES), F32),
            pltpu.VMEM((planes, 2, er + 2 * BASE, LANES), F32),
            pltpu.VMEM((COLOURS * 10, 2, er, LANES), F32),
            pltpu.VMEM((PHASES + 1, SUB, LANES), F32),
            pltpu.VMEM((PHASES, 2, SUB, LANES), I32),
        ],
        compiler_params=params,
        name="sweeps",
    )(
        colour_order, *prepared,
        from_below, from_above, from_right, from_left, corner_below, corner_above,
    )
    shared = lax.all_to_all(energy, AXES, 0, 0, tiled=True)
    energies = jnp.sum(shared, axis=0)[:PHASES].reshape(SWEEPS, COLOURS, chains)
    return (result[None], energies)


def solution(mesh):
    placed = (
        P(None, "row", "col"),
        P("row", "col"),
        P("row", "col"),
        P("row", "col"),
        P("row", "col", None, None, None),
        P(),
    )
    return jax.shard_map(
        local, mesh=mesh, in_specs=placed, out_specs=(P(None, "row", "col"), P()), check_vma=False
    )
```

time: 44.4 us -> 40.4 us (0.910)
  waiting for transfers between devices: 9.91 us -> 5.19 us
  Pallas kernels: 9.98 us -> 13.4 us
  local copies, waits for them, and re-layouts: 5.22 us -> 1.98 us
    pallas_call x2 -> x3, Pallas kernels: 9.9 us -> 13.4 us  [the longest x1 8.17 us: local(): pl.pallas_call(functools.partial(sweep_kernel, tile_rows, tile_cols, node...]
    unnamed x13 -> x4, local copies, waits for them, and re-layouts: 4.58 us -> 1.33 us
    ppermute x1, waiting for transfers between devices: 3.2 us -> 0.01 us  [local(): corner_above = lax.ppermute(corner_down, 'row', ring(row_count, 1))]
    ppermute x1, starting transfers between devices: 0.01 us -> 1.74 us  [local(): corner_above = lax.ppermute(corner_down, 'row', ring(row_count, 1))]
    ppermute x1, waiting for transfers between devices: 1.52 us -> 0.01 us  [local(): corner_below = lax.ppermute(corner_up, 'row', ring(row_count, -1))]
    ppermute x1, starting transfers between devices: 2.69 us -> 1.24 us  [local(): corner_below = lax.ppermute(corner_up, 'row', ring(row_count, -1))]
  transfers between devices with their start and end apart: 6 -> 6, of which waited for: 4 -> 2; matrix products, arithmetic and copies ran while one was open for 0% -> 0% of each run, Pallas kernels for 0% -> 9%
where the time goes in v2:
time: 40.4 us; the launch traced here: 40.1 us
  Pallas kernels  13.4 us (33%)
  starting transfers between devices  9.72 us (24%)
  blocking collectives  9.08 us (22%)
  waiting for transfers between devices  5.19 us (13%)
  local copies, waits for them, and re-layouts  1.98 us (5%)
  between operations  0.68 us (2%)
    all_to_all x1, blocking collectives, local(): shared = lax.all_to_all(energy, AXES, 0, 0, tiled=True)  9.08 us
    pallas_call x1, Pallas kernels, local(): pl.pallas_call(functools.partial(sweep_kernel, tile_rows, tile_cols, node...  8.17 us
    ppermute x1, starting transfers between devices, local(): from_below = lax.ppermute(up, 'row', ring(row_count, -1))  3.97 us
    ppermute x1, waiting for transfers between devices, local(): from_left = lax.ppermute(right, 'col', ring(col_count, 1))  3.54 us
    pallas_call x1, Pallas kernels, local(): pl.pallas_call(functools.partial(prepare_kernel, tile_rows, tile_cols), i...  3.51 us
    ppermute x1, starting transfers between devices, local(): from_right = lax.ppermute(left, 'col', ring(col_count, -1))  2.76 us
    ppermute x1, starting transfers between devices, local(): corner_above = lax.ppermute(corner_down, 'row', ring(row_count, 1))  1.74 us
    pallas_call x1, Pallas kernels, local(): pl.pallas_call(pack_kernel, in_specs=[hbm] * 5, out_specs=[vmem] * 4, out...  1.69 us
  transfers between devices with their start and end apart: 6, of which 2 were waited for; matrix products, arithmetic and copies ran while one was open for 0% of the time, Pallas kernels for 9%

profile of v2, /device:TPU:0, one launch (start us, length us, event | category | flops | bytes accessed | tf_op | source)
XLA Modules:
  0.0 40.1 jit_solution(4736966384308761924)
XLA Ops:
  0.6 1.7 %pack.1 = (f32[72,512]{1,0:T(8,128)S(1)}, f32[72,512]{1,0:T(8,128)S(1)}, f32[72,128]{1,0:T(8,128)S(1)}, f32[72,128]{1,0:T(8,128)S(1)}) custom-call(s32[1,1,2,1,4]{4,3,2,1,0:T(1,128)} %bitcast.11, f32[128,512]{1,0:T(8,128)} %bitcast.13, f32[128,512]{1,0:T(8,128)} %b_ref.1, f32[128,512]{1,0:T(8,128)} %kappa_ref.1, f32[128,512]{1,0:T(8,128)} %mass_ref.1), custom_call_target="tpu_custom_call" | custom-call | tf_op jit(solution)/shard_map/pack/pallas_call | solution.py:526
  2.3 4.0 %collective-permute-start.2 = (f32[72,512]{1,0:T(8,128)S(1)}, f32[72,512]{1,0:T(8,128)S(1)}, u32[]{:S(2)}, u32[]{:S(2)}) collective-permute-start(f32[72,512]{1,0:T(8,128)S(1)} %get-tuple-element.23), channel_id=1, source_target_pairs={{0,24},{8,0},{16,8},{24,16},{1,25},{9,1},{17,9},{25,17},{2,26},{10... | collective-permute-start | bytes 442376 | tf_op jit(solution)/shard_map/ppermute | solution.py:541
  6.3 0.0 collective-permute-start.3
  6.3 2.8 %collective-permute-start = (f32[72,128]{1,0:T(8,128)S(1)}, f32[72,128]{1,0:T(8,128)S(1)}, u32[]{:S(2)}, u32[]{:S(2)}) collective-permute-start(f32[72,128]{1,0:T(8,128)S(1)} %get-tuple-element.15), channel_id=1, source_target_pairs={{0,7},{1,0},{2,1},{3,2},{4,3},{5,4},{6,5},{7,6},{8,15},{9,8},{10,9... | collective-permute-start | bytes 110600 | tf_op jit(solution)/shard_map/ppermute | solution.py:539
  9.1 0.0 collective-permute-start.1
  9.1 1.6 %collective-permute-done.right_ref = f32[72,128]{1,0:T(8,128)S(1)} collective-permute-done((f32[72,128]{1,0:T(8,128)S(1)}, f32[72,128]{1,0:T(8,128)S(1)}, u32[]{:S(2)}, u32[]{:S(2)}) %collective-permute-start) | collective-permute-done | bytes 36896 | tf_op jit(solution)/shard_map/ppermute | solution.py:539
  10.7 3.5 %collective-permute-done.1.left_ref = f32[72,128]{1,0:T(8,128)S(1)} collective-permute-done((f32[72,128]{1,0:T(8,128)S(1)}, f32[72,128]{1,0:T(8,128)S(1)}, u32[]{:S(2)}, u32[]{:S(2)}) %collective-permute-start.1) | collective-permute-done | bytes 36896 | tf_op jit(solution)/shard_map/ppermute | solution.py:540
  14.2 0.1 corners.1
  14.3 1.7 %collective-permute-start.5 = (f32[48,128]{1,0:T(8,128)S(1)}, f32[48,128]{1,0:T(8,128)S(1)}, u32[]{:S(2)}, u32[]{:S(2)}) collective-permute-start(f32[48,128]{1,0:T(8,128)S(1)} %get-tuple-element.25), channel_id=1, source_target_pairs={{0,8},{8,16},{16,24},{24,0},{1,9},{9,17},{17,25},{25,1},{2,10},{10... | collective-permute-start | bytes 73736 | tf_op jit(solution)/shard_map/ppermute | solution.py:553
  16.1 1.2 %collective-permute-start.4 = (f32[48,128]{1,0:T(8,128)S(1)}, f32[48,128]{1,0:T(8,128)S(1)}, u32[]{:S(2)}, u32[]{:S(2)}) collective-permute-start(f32[48,128]{1,0:T(8,128)S(1)} %get-tuple-element.17.after_ref), channel_id=1, source_target_pairs={{0,24},{8,0},{16,8},{24,16},{1,25},{9,1},{17,9},{25,17},{2,26},{10... | collective-permute-start | bytes 73736 | tf_op jit(solution)/shard_map/ppermute | solution.py:552
  17.3 0.0 copy-start
  17.3 0.7 %copy-done = s32[1,1,2,4,1]{3,4,2,1,0:T(1,128)S(1)} copy-done((s32[1,1,2,4,1]{3,4,2,1,0:T(1,128)S(1)}, s32[1,1,2,4,1]{3,4,2,1,0:T(1,128)}, u32[]{:S(2)}) %copy-start) | copy-done | bytes 56
  18.0 0.0 copy-start.1
  18.0 0.7 %copy-done.1 = s32[4]{0:T(128)S(1)} copy-done((s32[4]{0:T(128)S(1)}, s32[4]{0:T(128)}, u32[]{:S(2)}) %copy-start.1) | copy-done | bytes 40
  18.6 3.5 %prepare.1 = (f32[16,2,56,128]{3,2,1,0:T(8,128)S(1)}, f32[16,2,56,128]{3,2,1,0:T(8,128)S(1)}, f32[16,2,56,128]{3,2,1,0:T(8,128)S(1)}, f32[16,2,56,128]{3,2,1,0:T(8,128)S(1)}, f32[32,2,56,128]{3,2,1,0:T(8,128)S(1)}) custom-call(s32[4]{0:T(128)S(1)} %copy-done.1, s32[1,1,2,1,4]{4,3,2,1,0:T(1,128)S(1)} %bitcast.12, f32[128,512]{1,0:T(8,128)} %bitcast.14, ...), custom_call_target="tpu_custom_call" | custom-call | flops 20000000 | bytes 1000000 | tf_op jit(solution)/shard_map/prepare/pallas_call | solution.py:557
  22.1 0.0 collective-permute-done.5.cabove_ref
  22.2 0.0 collective-permute-done.4.cbelow_ref
  22.2 0.0 collective-permute-done.2.below_ref
  22.2 0.0 collective-permute-done.3.above_ref
  22.2 8.2 %sweeps.1 = (f32[128,512]{1,0:T(8,128)}, f32[32,128]{1,0:T(8,128)S(1)}, f32[16,2,56,128]{3,2,1,0:T(8,128)S(1)}, f32[16,2,56,128]{3,2,1,0:T(8,128)S(1)}, f32[16,2...) custom-call(s32[4]{0:T(128)S(1)} %copy-done.1, ...), custom_call_target="tpu_custom_call", output_to_operand_aliasing={{2}: (1, {}), {3}: (2, {}), {4}: (3, {}), {5}: (4, {}), {6}... | custom-call | tf_op jit(solution)/shard_map/sweeps/pallas_call | solution.py:570
  30.4 9.1 %all_to_all.9 = f32[32,1,128]{2,1,0:T(1,128)S(1)} all-to-all(f32[32,1,128]{2,1,0:T(1,128)S(1)} %bitcast.10), channel_id=1, replica_groups=mesh['row'=4,'col'=8] {'row','col'}, dimensions={0} | all-to-all | bytes 32768 | tf_op jit(solution)/shard_map/all_to_all | solution.py:595
  39.4 0.1 reduce_sum.9
  39.5 0.6 %reshape.17 = f32[2,4,1]{1,0,2:T(2,128)} reshape(f32[8]{0:T(128)S(1)} %bitcast.15) | data formatting | bytes 64 | tf_op jit(solution)/shard_map/reshape | solution.py:596
Async XLA Ops:
  2.3 19.9 %collective-permute-start.2 = (f32[72,512]{1,0:T(8,128)S(1)}, f32[72,512]{1,0:T(8,128)S(1)}, u32[]{:S(2)}, u32[]{:S(2)}) collective-permute-start(f32[72,512]{1,0:T(8,128)S(1)} %get-tuple-element.23), channel_id=1, source_target_pairs={{0,24},{8,0},{16,8},{24,16},{1,25},{9,1},{17,9},{25,17},{2,26},{10... | collective-permute-start | bytes 442376 | tf_op jit(solution)/shard_map/ppermute | solution.py:541
  6.3 15.9 %collective-permute-start.3 = (f32[72,512]{1,0:T(8,128)S(1)}, f32[72,512]{1,0:T(8,128)S(1)}, u32[]{:S(2)}, u32[]{:S(2)}) collective-permute-start(f32[72,512]{1,0:T(8,128)S(1)} %get-tuple-element.24), channel_id=1, source_target_pairs={{0,8},{8,16},{16,24},{24,0},{1,9},{9,17},{17,25},{25,1},{2,10},{10... | collective-permute-start | bytes 442376 | tf_op jit(solution)/shard_map/ppermute | solution.py:542
  6.3 4.4 %collective-permute-start = (f32[72,128]{1,0:T(8,128)S(1)}, f32[72,128]{1,0:T(8,128)S(1)}, u32[]{:S(2)}, u32[]{:S(2)}) collective-permute-start(f32[72,128]{1,0:T(8,128)S(1)} %get-tuple-element.15), channel_id=1, source_target_pairs={{0,7},{1,0},{2,1},{3,2},{4,3},{5,4},{6,5},{7,6},{8,15},{9,8},{10,9... | collective-permute-start | bytes 110600 | tf_op jit(solution)/shard_map/ppermute | solution.py:539
  9.1 5.2 %collective-permute-start.1 = (f32[72,128]{1,0:T(8,128)S(1)}, f32[72,128]{1,0:T(8,128)S(1)}, u32[]{:S(2)}, u32[]{:S(2)}) collective-permute-start(f32[72,128]{1,0:T(8,128)S(1)} %get-tuple-element.16), channel_id=1, source_target_pairs={{0,1},{1,2},{2,3},{3,4},{4,5},{5,6},{6,7},{7,0},{8,9},{9,10},{10,1... | collective-permute-start | bytes 110600 | tf_op jit(solution)/shard_map/ppermute | solution.py:540
  14.3 7.8 %collective-permute-start.5 = (f32[48,128]{1,0:T(8,128)S(1)}, f32[48,128]{1,0:T(8,128)S(1)}, u32[]{:S(2)}, u32[]{:S(2)}) collective-permute-start(f32[48,128]{1,0:T(8,128)S(1)} %get-tuple-element.25), channel_id=1, source_target_pairs={{0,8},{8,16},{16,24},{24,0},{1,9},{9,17},{17,25},{25,1},{2,10},{10... | collective-permute-start | bytes 73736 | tf_op jit(solution)/shard_map/ppermute | solution.py:553
  16.1 6.1 %collective-permute-start.4 = (f32[48,128]{1,0:T(8,128)S(1)}, f32[48,128]{1,0:T(8,128)S(1)}, u32[]{:S(2)}, u32[]{:S(2)}) collective-permute-start(f32[48,128]{1,0:T(8,128)S(1)} %get-tuple-element.17.after_ref), channel_id=1, source_target_pairs={{0,24},{8,0},{16,8},{24,16},{1,25},{9,1},{17,9},{25,17},{2,26},{10... | collective-permute-start | bytes 73736 | tf_op jit(solution)/shard_map/ppermute | solution.py:552
  17.3 0.7 %copy-start = (s32[1,1,2,4,1]{3,4,2,1,0:T(1,128)S(1)}, s32[1,1,2,4,1]{3,4,2,1,0:T(1,128)}, u32[]{:S(2)}) copy-start(s32[1,1,2,4,1]{3,4,2,1,0:T(1,128)} %param.10) | copy-start | bytes 100
  18.0 0.7 %copy-start.1 = (s32[4]{0:T(128)S(1)}, s32[4]{0:T(128)}, u32[]{:S(2)}) copy-start(s32[4]{0:T(128)} %order_ref.3) | copy-start | bytes 52

commit v3 on v2

v3 whole, which is shorter than its diff:
```python
import functools

import jax
import jax.numpy as jnp
from jax import lax
from jax.experimental import pallas as pl
from jax.experimental.pallas import tpu as pltpu
from jax.sharding import PartitionSpec as P

SWEEPS = 2
COLOURS = 4
PHASES = SWEEPS * COLOURS
HALO = 2 * PHASES
CELL = 4
HC = HALO // CELL
LANES = 128
SUB = 8
GROUP = LANES // CELL
AXES = ("row", "col")
F32 = jnp.float32
I32 = jnp.int32

unit_step = 1.0 / 8388608.0
mix_factor = 73244475
SEED_BASE = 32768

SIN_COEFFS = (
    6.283185306485777,
    -41.34170192921984,
    81.60520938153618,
    -76.70366601553475,
    41.99996083008805,
    -14.336855962945094,
)


def lane_iota(shape):
    return lax.broadcasted_iota(I32, shape, len(shape) - 1)


def sub_iota(shape):
    return lax.broadcasted_iota(I32, shape, len(shape) - 2)


def lane_gather(value, index):
    return jnp.take_along_axis(value, index, axis=1, mode="promise_in_bounds")


def lroll(value, amount):
    amount = amount % value.shape[1]
    return pltpu.roll(value, amount, 1) if amount else value


SLOT = 8


def slot_gather(value, left):
    wide = lane_iota(value.shape)
    at = (wide + SLOT // 2) % LANES if left else wide
    index = CELL * (at % CELL) + (at % GROUP) // SLOT
    return lane_gather(value, index + (LANES - HALO if left else 0))


def lane_group(left):
    lane = lane_iota((SUB, LANES))
    return ((lane + SLOT // 2) % LANES if left else lane) // GROUP


def pick_group(group, values):
    result = values[0]
    for g in range(1, CELL):
        result = jnp.where(group == g, values[g], result)
    return result


def join_sides(right, left):
    return jnp.where(lane_iota(right.shape) % SLOT < SLOT // 2, right, left)


def pack_kernel(seeds_ref, *refs):
    sources, (up_ref, down_ref, left_ref, right_ref) = refs[:4], refs[4:8]
    edges, seeds_buf, sems = refs[8:]
    rows, cols = sources[0].shape
    mr = rows // CELL
    copies = []

    def copy(source, target):
        made = pltpu.make_async_copy(source, target, sems.at[len(copies)])
        made.start()
        copies.append(made)

    copy(seeds_ref, seeds_buf)
    for a, source in enumerate(sources):
        copy(source.at[:, pl.ds(0, LANES)], edges.at[2 * a])
        copy(source.at[:, pl.ds(cols - LANES, LANES)], edges.at[2 * a + 1])
    for a, source in enumerate(sources):
        copy(source.at[pl.ds(0, HALO)], up_ref.at[pl.ds(a * HALO, HALO)])
        copy(source.at[pl.ds(rows - HALO, HALO)], down_ref.at[pl.ds(a * HALO, HALO)])
    for made in copies:
        made.wait()
    for sweep in range(SWEEPS):
        seeds = seeds_buf[0, 0, sweep]
        high = (seeds // SEED_BASE).astype(F32)
        low = (seeds % SEED_BASE).astype(F32)
        for out in (up_ref, down_ref, left_ref, right_ref):
            base = out.shape[0] - SUB
            out[base + sweep : base + sweep + 1, 0:COLOURS] = high
            out[base + SWEEPS + sweep : base + SWEEPS + sweep + 1, 0:COLOURS] = low

    def pack(a, carry):
        for edge, out in ((0, left_ref), (1, right_ref)):
            group = lane_group(edge == 1)
            for r in range(CELL):
                value = slot_gather(edges[2 * a + edge, pl.ds(r, mr, stride=CELL), :], edge == 1)
                parts = [value[SUB * g : SUB * (g + 1)] for g in range(CELL)]
                at = pl.multiple_of((a * CELL + r) * SUB, SUB)
                out[pl.ds(at, SUB), :] = pick_group(group, parts)
        return carry

    lax.fori_loop(0, 4, pack, 0)


def corner_kernel(right_ref, left_ref, up_ref, down_ref):
    group = lane_group(True)
    for a in range(4):
        sides = []
        for r in range(CELL):
            rows = slice((a * CELL + r) * SUB, (a * CELL + r + 1) * SUB)
            sides.append(join_sides(right_ref[rows, :], left_ref[rows, :]))
        rows = slice(a * SUB, (a + 1) * SUB)
        up_ref[rows, :] = pick_group(group, [lroll(v, GROUP * r) for r, v in enumerate(sides)])
        down_ref[rows, :] = pick_group(
            group, [lroll(v, GROUP * (r + 1)) for r, v in enumerate(sides)]
        )
    base = right_ref.shape[0] - SUB
    for out in (up_ref, down_ref):
        out[4 * SUB : 5 * SUB, :] = right_ref[base : base + SUB, :]
        out[5 * SUB : 6 * SUB, :] = left_ref[base : base + SUB, :]


def scramble(hashed):
    sixteen = jnp.full_like(hashed, 16)
    hashed = hashed ^ lax.shift_right_logical(hashed, sixteen)
    hashed = hashed * mix_factor
    hashed = hashed ^ lax.shift_right_logical(hashed, sixteen)
    hashed = hashed * mix_factor
    return hashed ^ lax.shift_right_logical(hashed, sixteen)


def gaussian(first):
    nine = jnp.full_like(first, 9)
    one = lax.shift_right_logical(scramble(first), nine).astype(F32)
    two = lax.shift_right_logical(scramble(first + 1), nine).astype(F32)
    u1 = (one + 1.0) * unit_step
    v = 0.25 - jnp.abs(two * unit_step - 0.5)
    square = v * v
    poly = jnp.full_like(v, SIN_COEFFS[-1])
    for coeff in SIN_COEFFS[-2::-1]:
        poly = poly * square + coeff
    square = -2.0 * jnp.log(u1)
    return square * lax.rsqrt(jnp.maximum(square, 1e-30)) * (-(v * poly))


BASE = SUB


def rows_at(first, count):
    return pl.ds(BASE + first, count)


def lane_shift(value, amount, edge):
    moved = pltpu.roll(value, amount, 2)
    other = jnp.concatenate([moved[1:2], moved[0:1]], axis=0)
    return jnp.where(lane_iota(value.shape) == edge, other, moved)


def fold(value):
    count = value.shape[0]
    sub = sub_iota((SUB, LANES))
    total = jnp.where(sub >= HC, value[0:SUB], value[count - SUB : count])
    for top in range(SUB, count - SUB, SUB):
        total = total + value[top : top + SUB]
    return total


def gather_cells(value):
    wide = lane_iota(value.shape)
    return lane_gather(value, CELL * (wide % GROUP) + wide // GROUP)


def scatter_cells(value):
    wide = lane_iota(value.shape)
    return lane_gather(value, GROUP * (wide % CELL) + wide // CELL)


def column_planes(pieces):
    group = lane_iota(pieces[0].shape) // GROUP
    turned = [lroll(gather_cells(piece), GROUP * t) for t, piece in enumerate(pieces)]
    return [
        lroll(pick_group(group, [turned[(g - c) % CELL] for g in range(CELL)]), -GROUP * c)
        for c in range(CELL)
    ]


def natural_columns(planes):
    group = lane_iota(planes[0].shape) // GROUP
    turned = [lroll(plane, GROUP * c) for c, plane in enumerate(planes)]
    return [
        scatter_cells(
            lroll(pick_group(group, [turned[(g - t) % CELL] for g in range(CELL)]), -GROUP * t)
        )
        for t in range(CELL)
    ]


def put_ends(ref, plane, half, value):
    count = ref.shape[2] - 2 * BASE
    ref[plane, half, pl.ds(BASE + count - HC, HC), :] = value[0:HC]
    ref[plane, half, pl.ds(BASE, HC), :] = value[HC:SUB]


def node_offsets(tile_cols, row_cell, col_cell):
    return 2 * CELL * tile_cols * row_cell + 2 * CELL * col_cell


def phase_extra(colour, n, tile_cols):
    row, col = 2 * (colour // 2) + n // 2, 2 * (colour % 2) + n % 2
    return 2 * (row * tile_cols + col)


def noise_kernel(
    tile_rows, tile_cols,
    order_ref, seeds_ref, x_ref, b_ref, kappa_ref, mass_ref,
    Z, nat,
    order, seeds, sems,
):
    mr = tile_rows // CELL
    tiles = tile_cols // LANES
    copies = []

    def copy(source, target):
        made = pltpu.make_async_copy(source, target, sems.at[len(copies)])
        made.start()
        copies.append(made)

    copy(order_ref, order)
    copy(seeds_ref, seeds)
    for a, source in enumerate((x_ref, b_ref, kappa_ref, mass_ref)):
        for t in range(tiles):
            copy(
                source.at[:, pl.ds(t * LANES, LANES)],
                nat.at[a * tiles + t, pl.ds(0, tile_rows)],
            )
    copies[0].wait()
    copies[1].wait()
    offset_main = node_offsets(tile_cols, sub_iota((mr, LANES)), lane_iota((mr, LANES)))

    def noise_phase(phase, carry):
        own = seeds[0, 0, phase // COLOURS, 0, phase % COLOURS]
        colour = order[phase % COLOURS]
        for n in range(4):
            start = own + phase_extra(colour, n, tile_cols)
            Z[phase * 4 + n, 0, rows_at(HC, mr), :] = gaussian(offset_main + start)
        return carry

    lax.fori_loop(0, PHASES, noise_phase, 0)
    for made in copies[2:]:
        made.wait()


def planes_kernel(
    tile_rows, tile_cols,
    nat_in, below_ref, above_ref, right_ref, left_ref,
    X, B, S, I, nat,
):
    del nat_in
    mr = tile_rows // CELL
    er = mr + 2 * HC
    tiles = tile_cols // LANES

    def strips(a, carry):
        for t in range(tiles):
            lanes = slice(t * LANES, (t + 1) * LANES)
            at = pl.ds(pl.multiple_of(a * HALO, HALO), HALO)
            for start, source in ((0, below_ref), (HALO, above_ref)):
                nat[a * tiles + t, pl.ds(tile_rows + start, HALO), :] = source[at, lanes]
        return carry

    lax.fori_loop(0, 4, strips, 0)

    def put(ref, plane, value):
        ref[plane, 0, rows_at(HC, mr), :] = value[0:mr]
        put_ends(ref, plane, 0, value[mr:er])

    def row(r, carry):
        inner, outer = [], []
        for a in range(4):
            inner.append(
                column_planes(
                    [nat[a * tiles + t, pl.ds(r, er, stride=CELL), :] for t in range(tiles)]
                )
            )
            rows = pl.ds(pl.multiple_of((a * CELL + r) * SUB, SUB), SUB)
            side = join_sides(right_ref[rows, :], left_ref[rows, :])
            outer.append([lroll(side, -SLOT * slot) for slot in range(LANES // SLOT)])
        for c in range(CELL):
            plane = r * CELL + c
            put(X, plane, inner[0][c])
            put(B, plane, inner[1][c])
            put(S, plane, inner[2][c] * inner[3][c] + 4.0)
            put(I, plane, 1.0 / inner[3][c])
            for g in range(CELL):
                slot = CELL * g + c
                at = rows_at(HC + SUB * g, SUB)
                X[plane, 1, at, :] = outer[0][slot]
                B[plane, 1, at, :] = outer[1][slot]
                S[plane, 1, at, :] = outer[2][slot] * outer[3][slot] + 4.0
                I[plane, 1, at, :] = 1.0 / outer[3][slot]
        return carry

    lax.fori_loop(0, CELL, row, 0)


def sweep_kernel(
    tile_rows, tile_cols, nodes,
    order_ref, x_in, b_in, s_in, i_in, z_in,
    below_ref, above_ref, right_ref, left_ref, cbelow_ref, cabove_ref,
    out_ref, energy_ref, X, B, S, I, Z,
    W, D, EN, nat, order, around, sems,
):
    del x_in, b_in, s_in, i_in, z_in
    copies = []

    def copy(source, target):
        made = pltpu.make_async_copy(source, target, sems.at[len(copies)])
        made.start()
        copies.append(made)

    copy(order_ref, order)
    for at, (ref, back) in enumerate((
        (right_ref, 1), (left_ref, 1), (above_ref, 1), (below_ref, 1),
        (cabove_ref, 2), (cabove_ref, 1), (cbelow_ref, 2), (cbelow_ref, 1),
    )):
        top = ref.shape[0] - back * SUB
        copy(ref.at[pl.ds(top, SUB), pl.ds(0, LANES)], around.at[at])
    mr = tile_rows // CELL
    er = mr + 2 * HC
    tiles = tile_cols // LANES
    lane = lane_iota((SUB, LANES))
    sub = sub_iota((SUB, LANES))
    low = sub < HC

    corner = []
    for a in range(4):
        at = slice(a * SUB, (a + 1) * SUB)
        corner.append(jnp.where(low, cbelow_ref[at, :], cabove_ref[at, :]))

    def corners(r, carry):
        for c in range(CELL):
            plane = r * CELL + c
            value = [pltpu.roll(v, (2 * LANES - GROUP * r - SLOT * c) % LANES, 1) for v in carry]
            put_ends(X, plane, 1, value[0])
            put_ends(B, plane, 1, value[1])
            put_ends(S, plane, 1, value[2] * value[3] + 4.0)
            put_ends(I, plane, 1, 1.0 / value[3])
        return carry

    lax.fori_loop(0, CELL, corners, tuple(corner))

    every = rows_at(0, er)

    def start(r, energy):
        above, up = (r + CELL - 1) % CELL, jnp.where(r == 0, -1, 0)
        below, down = (r + 1) % CELL, jnp.where(r == CELL - 1, 1, 0)
        field = [X[r * CELL + c, :, every, :] for c in range(CELL)]
        inv = [I[r * CELL + c, :, every, :] for c in range(CELL)]

        def around_sum(ref, value, c):
            left = value[c - 1] if c else lane_shift(value[CELL - 1], 1, 0)
            right = value[c + 1] if c < CELL - 1 else lane_shift(value[0], LANES - 1, LANES - 1)
            return (
                ref[above * CELL + c, :, rows_at(up, er), :]
                + ref[below * CELL + c, :, rows_at(down, er), :]
                + left
                + right
            )

        for c in range(CELL):
            plane = r * CELL + c
            stiff = S[plane, :, every, :]
            first = stiff * field[c] - around_sum(X, field, c)
            scaled = inv[c] * first
            W[plane, :, every, :] = scaled
            D[plane, :, every, :] = stiff * stiff * inv[c] + around_sum(I, inv, c)
            part = 0.5 * scaled[0] * first[0] - B[plane, 0, every, :] * field[c][0]
            energy = energy + fold(part)
        return energy

    EN[0] = lax.fori_loop(0, CELL, start, jnp.zeros((SUB, LANES), F32))

    for made in copies:
        made.wait()
    spot = lane % GROUP
    is_right = spot < GROUP // 2
    in_right_corner = (lane >= 2 * HC) & (lane < 3 * HC)
    in_left_corner = (lane >= HC) & (lane < 2 * HC)
    end_cell = jnp.where(low, sub, sub + mr - 2 * HC)
    side_row = SUB * jnp.where(is_right, lane // GROUP, (lane // GROUP + 1) % CELL) + sub
    side_row = jnp.where(in_right_corner | in_left_corner, end_cell, side_row)
    side_col = jnp.where(is_right, spot, spot + LANES - GROUP)
    side_col = jnp.where(in_right_corner, lane - 2 * HC, side_col)
    side_col = jnp.where(in_left_corner, lane + LANES - 2 * HC, side_col)
    offset_side = node_offsets(tile_cols, side_row, side_col)
    offset_ends = node_offsets(tile_cols, end_cell, lane)

    def run_phase(phase, carry):
        sweep, k = phase // COLOURS, phase % COLOURS
        colour = order[k]
        ci, cj = colour // 2, colour % 2
        r0, c0 = 2 * ci, 2 * cj

        def seed(at):
            return around[at, sweep, k].astype(I32) * SEED_BASE + around[
                at, SWEEPS + sweep, k
            ].astype(I32)

        ends_seed = offset_ends + jnp.where(low, seed(3), seed(2))
        side_seed = jnp.where(is_right, seed(0), seed(1))
        side_seed = jnp.where(in_right_corner, jnp.where(low, seed(6), seed(4)), side_seed)
        side_seed = jnp.where(in_left_corner, jnp.where(low, seed(7), seed(5)), side_seed)
        side_seed = offset_side + side_seed
        for n in range(4):
            at = phase * 4 + n
            extra = phase_extra(colour, n, tile_cols)
            put_ends(Z, at, 0, gaussian(ends_seed + extra))
            value = gaussian(side_seed + extra)
            for g in range(mr // SUB):
                Z[at, 1, rows_at(HC + SUB * g, SUB), :] = lroll(value, -GROUP * g)
            put_ends(Z, at, 1, lroll(value, -2 * HC))
        z = [Z[phase * 4 + n, :, every, :] for n in range(4)]

        own = [(r0 + n // 2) * CELL + c0 + n % 2 for n in range(4)]
        above, up = (r0 + CELL - 1) % CELL, ci - 1
        below, down = (r0 + 2) % CELL, ci
        left, right = (c0 + CELL - 1) % CELL, (c0 + 2) % CELL
        above_rows, below_rows = rows_at(up, er), rows_at(down, er)
        w_own = [W[plane, :, every, :] for plane in own]
        w_above = [W[above * CELL + c0 + i, :, above_rows, :] for i in range(2)]
        w_below = [W[below * CELL + c0 + i, :, below_rows, :] for i in range(2)]
        w_left = [
            lane_shift(W[(r0 + i) * CELL + left, :, every, :], 1 - cj, -cj) for i in range(2)
        ]
        w_right = [
            lane_shift(
                W[(r0 + i) * CELL + right, :, every, :], (LANES - 1) * cj, LANES * cj - 1
            )
            for i in range(2)
        ]
        inv = [I[plane, :, every, :] for plane in own]
        stiff = [S[plane, :, every, :] for plane in own]
        sums = [
            w_above[0] + w_own[2] + w_left[0] + w_own[1],
            w_above[1] + w_own[3] + w_own[0] + w_right[0],
            w_own[0] + w_below[0] + w_left[1] + w_own[3],
            w_own[1] + w_below[1] + w_own[2] + w_right[1],
        ]
        residual = [
            B[own[n], :, every, :] - (stiff[n] * w_own[n] - sums[n]) for n in range(4)
        ]
        scaled = [stiff[n] * inv[n] for n in range(4)]
        diag = [D[plane, :, every, :] for plane in own]
        m01, m02 = -(scaled[0] + scaled[1]), -(scaled[0] + scaled[2])
        m13, m23 = -(scaled[1] + scaled[3]), -(scaled[2] + scaled[3])
        m03, m12 = inv[1] + inv[2], inv[0] + inv[3]
        q0 = lax.rsqrt(diag[0])
        l10, l20, l30 = m01 * q0, m02 * q0, m03 * q0
        q1 = lax.rsqrt(diag[1] - l10 * l10)
        l21, l31 = (m12 - l20 * l10) * q1, (m13 - l30 * l10) * q1
        q2 = lax.rsqrt(diag[2] - l20 * l20 - l21 * l21)
        l32 = (m23 - l30 * l20 - l31 * l21) * q2
        q3 = lax.rsqrt(diag[3] - l30 * l30 - l31 * l31 - l32 * l32)
        f0 = residual[0] * q0
        f1 = (residual[1] - l10 * f0) * q1
        f2 = (residual[2] - l20 * f0 - l21 * f1) * q2
        f3 = (residual[3] - l30 * f0 - l31 * f1 - l32 * f2) * q3
        y0, y1, y2, y3 = f0 + z[0], f1 + z[1], f2 + z[2], f3 + z[3]
        d3 = y3 * q3
        d2 = (y2 - l32 * d3) * q2
        d1 = (y1 - l21 * d2 - l31 * d3) * q1
        d0 = (y0 - l10 * d1 - l20 * d2 - l30 * d3) * q0
        delta = [d0, d1, d2, d3]
        for n in range(4):
            X[own[n], 0, every, :] = X[own[n], 0, every, :] + delta[n][0]
        change = 0.0
        for n, f in enumerate((f0, f1, f2, f3)):
            change = change + (z[n][0] * z[n][0] - f[0] * f[0])
        EN[phase + 1] = 0.5 * fold(change)
        for n, (across, beside) in enumerate(((1, 2), (0, 3), (3, 0), (2, 1))):
            step = stiff[n] * delta[n] - (delta[across] + delta[beside])
            W[own[n], :, every, :] = w_own[n] + inv[n] * step

        def spread(plane, rows, value):
            W[plane, :, rows, :] = W[plane, :, rows, :] - I[plane, :, rows, :] * value

        for i in range(2):
            spread(above * CELL + c0 + i, above_rows, delta[i])
            spread(below * CELL + c0 + i, below_rows, delta[2 + i])
            spread(
                (r0 + i) * CELL + left, every,
                lane_shift(delta[2 * i], (LANES - 1) * (1 - cj), LANES * (1 - cj) - 1),
            )
            spread(
                (r0 + i) * CELL + right, every, lane_shift(delta[2 * i + 1], cj, cj - 1)
            )
        return carry

    lax.fori_loop(0, PHASES, run_phase, 0)

    running = EN[0]
    result = jnp.zeros((1, LANES), F32)
    first_row = lane_iota((1, LANES))
    for phase in range(PHASES):
        if phase:
            running = running + EN[phase]
        total = jnp.sum(jnp.sum(running, axis=0, keepdims=True), axis=1, keepdims=True)
        result = jnp.where(first_row == phase, total, result)
    energy_ref[...] = jnp.broadcast_to(result / nodes, energy_ref.shape)

    def restore(i, carry):
        for r in (2 * i, 2 * i + 1):
            columns = natural_columns(
                [X[r * CELL + c, 0, rows_at(HC, mr), :] for c in range(CELL)]
            )
            for t, value in enumerate(columns):
                nat[t, pl.ds(r, mr, stride=CELL), :] = value
        return carry

    lax.fori_loop(0, CELL // 2, restore, 0)
    for t in range(tiles):
        out_ref[:, t * LANES : (t + 1) * LANES] = nat[t]


def ring(count, step):
    return [(i, (i + step) % count) for i in range(count)]


def estimate(flops):
    return pl.CostEstimate(flops=flops, bytes_accessed=1_000_000, transcendentals=0)


def local(initial_field, information, kappa_squared, lumped_mass, noise_seeds, colour_order):
    chains, tile_rows, tile_cols = initial_field.shape
    row_count, col_count = lax.axis_size("row"), lax.axis_size("col")
    devices = row_count * col_count
    nodes = tile_rows * row_count * tile_cols * col_count
    mr = tile_rows // CELL
    er = mr + 2 * HC
    tiles = tile_cols // LANES
    vmem = pl.BlockSpec(memory_space=pltpu.VMEM)
    hbm = pl.BlockSpec(memory_space=pltpu.HBM)
    params = pltpu.CompilerParams(vmem_limit_bytes=16 * 1024 * 1024)

    def in_hbm(value):
        return pltpu.with_memory_space_constraint(value, pltpu.HBM)

    seeds = in_hbm(jnp.swapaxes(noise_seeds, 3, 4))
    order = in_hbm(colour_order)
    sources = [
        in_hbm(value) for value in (initial_field[0], information, kappa_squared, lumped_mass)
    ]
    rows_shape = jax.ShapeDtypeStruct((4 * HALO + SUB, tile_cols), F32)
    cols_shape = jax.ShapeDtypeStruct((4 * CELL * SUB + SUB, LANES), F32)
    up, down, left, right = pl.pallas_call(
        pack_kernel,
        in_specs=[hbm] * 5,
        out_specs=[vmem] * 4,
        out_shape=[rows_shape, rows_shape, cols_shape, cols_shape],
        scratch_shapes=[
            pltpu.VMEM((8, tile_rows, LANES), F32),
            pltpu.VMEM(seeds.shape, I32),
            pltpu.SemaphoreType.DMA((17,)),
        ],
        compiler_params=params,
        name="pack",
    )(seeds, *sources)
    from_right = lax.ppermute(left, "col", ring(col_count, -1))
    from_left = lax.ppermute(right, "col", ring(col_count, 1))
    from_below = lax.ppermute(up, "row", ring(row_count, -1))
    from_above = lax.ppermute(down, "row", ring(row_count, 1))
    corner_shape = jax.ShapeDtypeStruct((6 * SUB, LANES), F32)
    corner_up, corner_down = pl.pallas_call(
        corner_kernel,
        in_specs=[vmem] * 2,
        out_specs=[vmem] * 2,
        out_shape=[corner_shape, corner_shape],
        compiler_params=params,
        name="corners",
    )(from_right, from_left)
    corner_below = lax.ppermute(corner_up, "row", ring(row_count, -1))
    corner_above = lax.ppermute(corner_down, "row", ring(row_count, 1))
    planes = CELL * CELL

    def stack(count):
        return (count, 2, er + 2 * BASE, LANES)

    plane_shape = jax.ShapeDtypeStruct(stack(planes), F32)
    noise_shape = jax.ShapeDtypeStruct(stack(PHASES * 4), F32)
    natural_shape = jax.ShapeDtypeStruct((4 * tiles, tile_rows + 2 * HALO, LANES), F32)
    order_scratch = pltpu.SMEM(colour_order.shape, I32)
    noise, natural = pl.pallas_call(
        functools.partial(noise_kernel, tile_rows, tile_cols),
        in_specs=[hbm] * 6,
        out_specs=[vmem] * 2,
        out_shape=[noise_shape, natural_shape],
        scratch_shapes=[
            order_scratch,
            pltpu.SMEM(seeds.shape, I32),
            pltpu.SemaphoreType.DMA((4 * tiles + 2,)),
        ],
        compiler_params=params,
        cost_estimate=estimate(4_000_000),
        name="noise",
    )(order, seeds, *sources)
    *state, _ = pl.pallas_call(
        functools.partial(planes_kernel, tile_rows, tile_cols),
        in_specs=[vmem] * 5,
        out_specs=[vmem] * 5,
        out_shape=[plane_shape] * 4 + [natural_shape],
        input_output_aliases={0: 4},
        compiler_params=params,
        cost_estimate=estimate(4_000_000),
        name="planes",
    )(natural, from_below, from_above, from_right, from_left)
    result, energy, *_ = pl.pallas_call(
        functools.partial(sweep_kernel, tile_rows, tile_cols, nodes),
        in_specs=[hbm] + [vmem] * 11,
        out_specs=[vmem] * 7,
        out_shape=[
            jax.ShapeDtypeStruct((tile_rows, tile_cols), F32),
            jax.ShapeDtypeStruct((devices, LANES), F32),
        ]
        + [plane_shape] * 4
        + [noise_shape],
        input_output_aliases={1 + i: 2 + i for i in range(5)},
        scratch_shapes=[
            pltpu.VMEM(stack(planes), F32),
            pltpu.VMEM(stack(planes), F32),
            pltpu.VMEM((PHASES + 1, SUB, LANES), F32),
            pltpu.VMEM((tiles, tile_rows, LANES), F32),
            order_scratch,
            pltpu.SMEM((8, SUB, LANES), F32),
            pltpu.SemaphoreType.DMA((9,)),
        ],
        compiler_params=params,
        cost_estimate=estimate(8_000_000),
        name="sweeps",
    )(
        order, *state, noise,
        from_below, from_above, from_right, from_left, corner_below, corner_above,
    )
    shared = lax.all_to_all(energy, AXES, 0, 0, tiled=True)
    energies = jnp.sum(shared, axis=0)[:PHASES].reshape(SWEEPS, COLOURS, chains)
    return (result[None], energies)


def solution(mesh):
    placed = (
        P(None, "row", "col"),
        P("row", "col"),
        P("row", "col"),
        P("row", "col"),
        P("row", "col", None, None, None),
        P(),
    )
    return jax.shard_map(
        local, mesh=mesh, in_specs=placed, out_specs=(P(None, "row", "col"), P()), check_vma=False
    )
```

time: 40.4 us -> 39.8 us (0.985)
  local copies, waits for them, and re-layouts: 1.98 us -> 0.65 us
  blocking collectives: 9.08 us -> 10.3 us
  Pallas kernels: 13.4 us -> 12.9 us
    pallas_call x1, Pallas kernels: 8.17 us -> 6.06 us  [local(): pl.pallas_call(functools.partial(sweep_kernel, tile_rows, tile_cols, node...]
    ppermute x1, starting transfers between devices: 1.74 us -> 0.01 us  [local(): corner_above = lax.ppermute(corner_down, 'row', ring(row_count, 1))]
    pallas_call x1 -> x2, Pallas kernels: 3.51 us -> 5.06 us  [the longest x1 3.13 us: local(): pl.pallas_call(functools.partial(planes_kernel, tile_rows, tile_cols), in...]
    ppermute x1, starting transfers between devices: 1.24 us -> 2.69 us  [local(): corner_below = lax.ppermute(corner_up, 'row', ring(row_count, -1))]
    unnamed x4 -> x0, local copies, waits for them, and re-layouts: 1.33 us -> none
    all_to_all x1, blocking collectives: 9.08 us -> 10.3 us  [local(): shared = lax.all_to_all(energy, AXES, 0, 0, tiled=True)]
  transfers between devices with their start and end apart: 6 -> 6, of which waited for: 2 -> 2; matrix products, arithmetic and copies ran while one was open for 0% -> 0% of each run, Pallas kernels for 9% -> 13%
where the time goes in v3:
time: 39.8 us; the launch traced here: 39.6 us
  Pallas kernels  12.9 us (32%)
  blocking collectives  10.3 us (26%)
  starting transfers between devices  9.44 us (24%)
  waiting for transfers between devices  5.54 us (14%)
  between operations  0.7 us (2%)
  local copies, waits for them, and re-layouts  0.65 us (2%)
    all_to_all x1, blocking collectives, local(): shared = lax.all_to_all(energy, AXES, 0, 0, tiled=True)  10.3 us
    pallas_call x1, Pallas kernels, local(): pl.pallas_call(functools.partial(sweep_kernel, tile_rows, tile_cols, node...  6.06 us
    ppermute x1, starting transfers between devices, local(): from_below = lax.ppermute(up, 'row', ring(row_count, -1))  3.97 us
    ppermute x1, waiting for transfers between devices, local(): from_left = lax.ppermute(right, 'col', ring(col_count, 1))  3.59 us
    pallas_call x1, Pallas kernels, local(): pl.pallas_call(functools.partial(planes_kernel, tile_rows, tile_cols), in...  3.13 us
    ppermute x1, starting transfers between devices, local(): from_right = lax.ppermute(left, 'col', ring(col_count, -1))  2.76 us
    ppermute x1, starting transfers between devices, local(): corner_below = lax.ppermute(corner_up, 'row', ring(row_count, -1))  2.69 us
    ppermute x1, waiting for transfers between devices, local(): from_right = lax.ppermute(left, 'col', ring(col_count, -1))  1.94 us
  transfers between devices with their start and end apart: 6, of which 2 were waited for; matrix products, arithmetic and copies ran while one was open for 0% of the time, Pallas kernels for 13%

profile of v3, /device:TPU:0, one launch (start us, length us, event | category | flops | bytes accessed | tf_op | source)
XLA Modules:
  0.0 39.6 jit_solution(13289415673378914343)
XLA Ops:
  0.6 1.7 %pack.1 = (f32[72,512]{1,0:T(8,128)S(1)}, f32[72,512]{1,0:T(8,128)S(1)}, f32[136,128]{1,0:T(8,128)S(1)}, f32[136,128]{1,0:T(8,128)S(1)}) custom-call(s32[1,1,2,1,4]{4,3,2,1,0:T(1,128)} %bitcast.13, f32[128,512]{1,0:T(8,128)} %bitcast.11, f32[128,512]{1,0:T(8,128)} %refs_1_.1, f32[128,512]{1,0:T(8,128)} %refs_2_.1, f32[128,512]{1,0:T(8,128)} %refs_3_.1), custom_call_target="tpu_custom_call" | custom-call | tf_op jit(solution)/shard_map/pack/pallas_call | solution.py:573
  2.4 4.0 %collective-permute-start = (f32[72,512]{1,0:T(8,128)S(1)}, f32[72,512]{1,0:T(8,128)S(1)}, u32[]{:S(2)}, u32[]{:S(2)}) collective-permute-start(f32[72,512]{1,0:T(8,128)S(1)} %get-tuple-element.17), channel_id=1, source_target_pairs={{0,24},{8,0},{16,8},{24,16},{1,25},{9,1},{17,9},{25,17},{2,26},{10... | collective-permute-start | bytes 442376 | tf_op jit(solution)/shard_map/ppermute | solution.py:588
  6.3 0.0 collective-permute-start.1
  6.3 2.8 %collective-permute-start.2 = (f32[136,128]{1,0:T(8,128)S(1)}, f32[136,128]{1,0:T(8,128)S(1)}, u32[]{:S(2)}, u32[]{:S(2)}) collective-permute-start(f32[136,128]{1,0:T(8,128)S(1)} %get-tuple-element.19), channel_id=1, source_target_pairs={{0,7},{1,0},{2,1},{3,2},{4,3},{5,4},{6,5},{7,6},{8,15},{9,8},{10,9... | collective-permute-start | bytes 208904 | tf_op jit(solution)/shard_map/ppermute | solution.py:586
  9.1 0.0 collective-permute-start.3
  9.1 1.9 %collective-permute-done.2.right_ref = f32[136,128]{1,0:T(8,128)S(1)} collective-permute-done((f32[136,128]{1,0:T(8,128)S(1)}, f32[136,128]{1,0:T(8,128)S(1)}, u32[]{:S(2)}, u32[]{:S(2)}) %collective-permute-start.2) | collective-permute-done | bytes 69664 | tf_op jit(solution)/shard_map/ppermute | solution.py:586
  11.0 3.6 %collective-permute-done.3.left_ref = f32[136,128]{1,0:T(8,128)S(1)} collective-permute-done((f32[136,128]{1,0:T(8,128)S(1)}, f32[136,128]{1,0:T(8,128)S(1)}, u32[]{:S(2)}, u32[]{:S(2)}) %collective-permute-start.3) | collective-permute-done | bytes 69664 | tf_op jit(solution)/shard_map/ppermute | solution.py:587
  14.6 0.1 corners.1
  14.7 2.7 %collective-permute-start.4 = (f32[48,128]{1,0:T(8,128)S(1)}, f32[48,128]{1,0:T(8,128)S(1)}, u32[]{:S(2)}, u32[]{:S(2)}) collective-permute-start(f32[48,128]{1,0:T(8,128)S(1)} %get-tuple-element.26), channel_id=1, source_target_pairs={{0,24},{8,0},{16,8},{24,16},{1,25},{9,1},{17,9},{25,17},{2,26},{10... | collective-permute-start | bytes 73736 | tf_op jit(solution)/shard_map/ppermute | solution.py:599
  17.4 0.0 collective-permute-start.5
  17.4 1.9 %noise.1 = (f32[32,2,56,128]{3,2,1,0:T(8,128)S(1)}, f32[16,160,128]{2,1,0:T(8,128)S(1)}) custom-call(s32[4]{0:T(128)} %order_ref.3, s32[1,1,2,1,4]{4,3,2,1,0:T(1,128)} %bitcast.14, f32[128,512]{1,0:T(8,128)} %bitcast.12, f32[128,512]{1,0:T(8,128)} %refs_1_.1, f32[128,512]{1,0:T(8,128)} %refs_2_.1, f32[128,512]{1,0:T(8,128)} %refs_3_.1), custom_call_target="tpu_custom_call" | custom-call | flops 4000000 | bytes 1000000 | tf_op jit(solution)/shard_map/noise/pallas_call | solution.py:610
  19.4 0.0 collective-permute-done.below_ref
  19.4 0.0 collective-permute-done.1.above_ref
  19.4 3.1 %planes.1 = (f32[16,2,56,128]{3,2,1,0:T(8,128)S(1)}, f32[16,2,56,128]{3,2,1,0:T(8,128)S(1)}, f32[16,2,56,128]{3,2,1,0:T(8,128)S(1)}, f32[16,2,56,128]{3,2,1,0:T(8,128)S(1)}, f32[16,160,128]{2,1,0:T(8,128)S(1)}) custom-call(f32[16,160,128]{2,1,0:T(8,128)S(1)} %get-tuple-element.16.nat_in, ...), custom_call_target="tpu_custom_call", output_to_operand_aliasing={{4}: (0, {})} | custom-call | flops 4000000 | bytes 1000000 | tf_op jit(solution)/shard_map/planes/pallas_call | solution.py:624
  22.5 0.0 collective-permute-done.4.cbelow_ref
  22.5 0.0 collective-permute-done.5.cabove_ref
  22.6 6.1 %sweeps.1 = (f32[128,512]{1,0:T(8,128)}, f32[32,128]{1,0:T(8,128)S(1)}, f32[16,2,56,128]{3,2,1,0:T(8,128)S(1)}, f32[16,2,56,128]{3,2,1,0:T(8,128)S(1)}, f32[16,2...) custom-call(s32[4]{0:T(128)} %order_ref.3, ...), custom_call_target="tpu_custom_call", output_to_operand_aliasing={{2}: (1, {}), {3}: (2, {}), {4}: (3, {}), {5}: (4, {}), {6}... | custom-call | flops 8000000 | bytes 1000000 | tf_op jit(solution)/shard_map/sweeps/pallas_call | solution.py:634
  28.6 10.3 %all_to_all.9 = f32[32,1,128]{2,1,0:T(1,128)S(1)} all-to-all(f32[32,1,128]{2,1,0:T(1,128)S(1)} %bitcast.10), channel_id=1, replica_groups=mesh['row'=4,'col'=8] {'row','col'}, dimensions={0} | all-to-all | bytes 32768 | tf_op jit(solution)/shard_map/all_to_all | solution.py:661
  38.9 0.1 reduce_sum.9
  38.9 0.6 %reshape.17 = f32[2,4,1]{1,0,2:T(2,128)} reshape(f32[8]{0:T(128)S(1)} %bitcast.15) | data formatting | bytes 64 | tf_op jit(solution)/shard_map/reshape | solution.py:662
Async XLA Ops:
  2.4 17.0 %collective-permute-start = (f32[72,512]{1,0:T(8,128)S(1)}, f32[72,512]{1,0:T(8,128)S(1)}, u32[]{:S(2)}, u32[]{:S(2)}) collective-permute-start(f32[72,512]{1,0:T(8,128)S(1)} %get-tuple-element.17), channel_id=1, source_target_pairs={{0,24},{8,0},{16,8},{24,16},{1,25},{9,1},{17,9},{25,17},{2,26},{10... | collective-permute-start | bytes 442376 | tf_op jit(solution)/shard_map/ppermute | solution.py:588
  6.3 13.0 %collective-permute-start.1 = (f32[72,512]{1,0:T(8,128)S(1)}, f32[72,512]{1,0:T(8,128)S(1)}, u32[]{:S(2)}, u32[]{:S(2)}) collective-permute-start(f32[72,512]{1,0:T(8,128)S(1)} %get-tuple-element.18), channel_id=1, source_target_pairs={{0,8},{8,16},{16,24},{24,0},{1,9},{9,17},{17,25},{25,1},{2,10},{10... | collective-permute-start | bytes 442376 | tf_op jit(solution)/shard_map/ppermute | solution.py:589
  6.3 4.7 %collective-permute-start.2 = (f32[136,128]{1,0:T(8,128)S(1)}, f32[136,128]{1,0:T(8,128)S(1)}, u32[]{:S(2)}, u32[]{:S(2)}) collective-permute-start(f32[136,128]{1,0:T(8,128)S(1)} %get-tuple-element.19), channel_id=1, source_target_pairs={{0,7},{1,0},{2,1},{3,2},{4,3},{5,4},{6,5},{7,6},{8,15},{9,8},{10,9... | collective-permute-start | bytes 208904 | tf_op jit(solution)/shard_map/ppermute | solution.py:586
  9.1 5.5 %collective-permute-start.3 = (f32[136,128]{1,0:T(8,128)S(1)}, f32[136,128]{1,0:T(8,128)S(1)}, u32[]{:S(2)}, u32[]{:S(2)}) collective-permute-start(f32[136,128]{1,0:T(8,128)S(1)} %get-tuple-element.20), channel_id=1, source_target_pairs={{0,1},{1,2},{2,3},{3,4},{4,5},{5,6},{6,7},{7,0},{8,9},{9,10},{10,1... | collective-permute-start | bytes 208904 | tf_op jit(solution)/shard_map/ppermute | solution.py:587
  14.7 7.8 %collective-permute-start.4 = (f32[48,128]{1,0:T(8,128)S(1)}, f32[48,128]{1,0:T(8,128)S(1)}, u32[]{:S(2)}, u32[]{:S(2)}) collective-permute-start(f32[48,128]{1,0:T(8,128)S(1)} %get-tuple-element.26), channel_id=1, source_target_pairs={{0,24},{8,0},{16,8},{24,16},{1,25},{9,1},{17,9},{25,17},{2,26},{10... | collective-permute-start | bytes 73736 | tf_op jit(solution)/shard_map/ppermute | solution.py:599
  17.4 5.1 %collective-permute-start.5 = (f32[48,128]{1,0:T(8,128)S(1)}, f32[48,128]{1,0:T(8,128)S(1)}, u32[]{:S(2)}, u32[]{:S(2)}) collective-permute-start(f32[48,128]{1,0:T(8,128)S(1)} %get-tuple-element.27), channel_id=1, source_target_pairs={{0,8},{8,16},{16,24},{24,0},{1,9},{9,17},{17,25},{25,1},{2,10},{10... | collective-permute-start | bytes 73736 | tf_op jit(solution)/shard_map/ppermute | solution.py:600

commit v4 on v3

--- a/solution.py
+++ b/solution.py
@@ -6,6 +6,7 @@
 from jax.experimental import pallas as pl
 from jax.experimental.pallas import tpu as pltpu
 from jax.sharding import PartitionSpec as P
+
 
 SWEEPS = 2
 COLOURS = 4
@@ -102,7 +103,7 @@
         seeds = seeds_buf[0, 0, sweep]
         high = (seeds // SEED_BASE).astype(F32)
         low = (seeds % SEED_BASE).astype(F32)
-        for out in (up_ref, down_ref, left_ref, right_ref):
+        for out in (left_ref, right_ref):
             base = out.shape[0] - SUB
             out[base + sweep : base + sweep + 1, 0:COLOURS] = high
             out[base + SWEEPS + sweep : base + SWEEPS + sweep + 1, 0:COLOURS] = low
@@ -120,7 +121,8 @@
     lax.fori_loop(0, 4, pack, 0)
 
 
-def corner_kernel(right_ref, left_ref, up_ref, down_ref):
+def corner_kernel(right_ref, left_ref, own_ref, after_ref, up_ref, down_ref):
+    del after_ref
     group = lane_group(True)
     for a in range(4):
         sides = []
@@ -134,8 +136,8 @@
         )
     base = right_ref.shape[0] - SUB
     for out in (up_ref, down_ref):
-        out[4 * SUB : 5 * SUB, :] = right_ref[base : base + SUB, :]
-        out[5 * SUB : 6 * SUB, :] = left_ref[base : base + SUB, :]
+        for i, source in enumerate((right_ref, left_ref, own_ref)):
+            out[(4 + i) * SUB : (5 + i) * SUB, :] = source[base : base + SUB, :]
 
 
 def scramble(hashed):
@@ -247,10 +249,7 @@
     copy(seeds_ref, seeds)
     for a, source in enumerate((x_ref, b_ref, kappa_ref, mass_ref)):
         for t in range(tiles):
-            copy(
-                source.at[:, pl.ds(t * LANES, LANES)],
-                nat.at[a * tiles + t, pl.ds(0, tile_rows)],
-            )
+            copy(source.at[:, pl.ds(t * LANES, LANES)], nat.at[a * tiles + t])
     copies[0].wait()
     copies[1].wait()
     offset_main = node_offsets(tile_cols, sub_iota((mr, LANES)), lane_iota((mr, LANES)))
@@ -268,36 +267,16 @@
         made.wait()
 
 
-def planes_kernel(
-    tile_rows, tile_cols,
-    nat_in, below_ref, above_ref, right_ref, left_ref,
-    X, B, S, I, nat,
-):
-    del nat_in
+def planes_kernel(tile_rows, tile_cols, nat, right_ref, left_ref, X, B, S, I):
     mr = tile_rows // CELL
-    er = mr + 2 * HC
     tiles = tile_cols // LANES
-
-    def strips(a, carry):
-        for t in range(tiles):
-            lanes = slice(t * LANES, (t + 1) * LANES)
-            at = pl.ds(pl.multiple_of(a * HALO, HALO), HALO)
-            for start, source in ((0, below_ref), (HALO, above_ref)):
-                nat[a * tiles + t, pl.ds(tile_rows + start, HALO), :] = source[at, lanes]
-        return carry
-
-    lax.fori_loop(0, 4, strips, 0)
-
-    def put(ref, plane, value):
-        ref[plane, 0, rows_at(HC, mr), :] = value[0:mr]
-        put_ends(ref, plane, 0, value[mr:er])
 
     def row(r, carry):
         inner, outer = [], []
         for a in range(4):
             inner.append(
                 column_planes(
-                    [nat[a * tiles + t, pl.ds(r, er, stride=CELL), :] for t in range(tiles)]
+                    [nat[a * tiles + t, pl.ds(r, mr, stride=CELL), :] for t in range(tiles)]
                 )
             )
             rows = pl.ds(pl.multiple_of((a * CELL + r) * SUB, SUB), SUB)
@@ -305,10 +284,10 @@
             outer.append([lroll(side, -SLOT * slot) for slot in range(LANES // SLOT)])
         for c in range(CELL):
             plane = r * CELL + c
-            put(X, plane, inner[0][c])
-            put(B, plane, inner[1][c])
-            put(S, plane, inner[2][c] * inner[3][c] + 4.0)
-            put(I, plane, 1.0 / inner[3][c])
+            X[plane, 0, rows_at(HC, mr), :] = inner[0][c]
+            B[plane, 0, rows_at(HC, mr), :] = inner[1][c]
+            S[plane, 0, rows_at(HC, mr), :] = inner[2][c] * inner[3][c] + 4.0
+            I[plane, 0, rows_at(HC, mr), :] = 1.0 / inner[3][c]
             for g in range(CELL):
                 slot = CELL * g + c
                 at = rows_at(HC + SUB * g, SUB)
@@ -326,7 +305,7 @@
     order_ref, x_in, b_in, s_in, i_in, z_in,
     below_ref, above_ref, right_ref, left_ref, cbelow_ref, cabove_ref,
     out_ref, energy_ref, X, B, S, I, Z,
-    W, D, EN, nat, order, around, sems,
+    strip, W, D, EN, nat, order, around, sems,
 ):
     del x_in, b_in, s_in, i_in, z_in
     copies = []
@@ -338,8 +317,8 @@
 
     copy(order_ref, order)
     for at, (ref, back) in enumerate((
-        (right_ref, 1), (left_ref, 1), (above_ref, 1), (below_ref, 1),
-        (cabove_ref, 2), (cabove_ref, 1), (cbelow_ref, 2), (cbelow_ref, 1),
+        (right_ref, 1), (left_ref, 1), (cabove_ref, 1), (cbelow_ref, 1),
+        (cabove_ref, 3), (cabove_ref, 2), (cbelow_ref, 3), (cbelow_ref, 2),
     )):
         top = ref.shape[0] - back * SUB
         copy(ref.at[pl.ds(top, SUB), pl.ds(0, LANES)], around.at[at])
@@ -355,17 +334,35 @@
         at = slice(a * SUB, (a + 1) * SUB)
         corner.append(jnp.where(low, cbelow_ref[at, :], cabove_ref[at, :]))
 
-    def corners(r, carry):
+    def strips(a, carry):
+        for t in range(tiles):
+            lanes = slice(t * LANES, (t + 1) * LANES)
+            at = pl.ds(pl.multiple_of(a * HALO, HALO), HALO)
+            for start, source in ((0, below_ref), (HALO, above_ref)):
+                strip[a * tiles + t, start : start + HALO, :] = source[at, lanes]
+        return carry
+
+    lax.fori_loop(0, 4, strips, 0)
+
+    def ends(r, carry):
+        inner = [
+            column_planes(
+                [strip[a * tiles + t, pl.ds(r, SUB, stride=CELL), :] for t in range(tiles)]
+            )
+            for a in range(4)
+        ]
         for c in range(CELL):
             plane = r * CELL + c
-            value = [pltpu.roll(v, (2 * LANES - GROUP * r - SLOT * c) % LANES, 1) for v in carry]
-            put_ends(X, plane, 1, value[0])
-            put_ends(B, plane, 1, value[1])
-            put_ends(S, plane, 1, value[2] * value[3] + 4.0)
-            put_ends(I, plane, 1, 1.0 / value[3])
+            amount = (2 * LANES - GROUP * r - SLOT * c) % LANES
+            outer = [pltpu.roll(value, amount, 1) for value in carry]
+            for half, value in enumerate(([v[c] for v in inner], outer)):
+                put_ends(X, plane, half, value[0])
+                put_ends(B, plane, half, value[1])
+                put_ends(S, plane, half, value[2] * value[3] + 4.0)
+                put_ends(I, plane, half, 1.0 / value[3])
         return carry
 
-    lax.fori_loop(0, CELL, corners, tuple(corner))
+    lax.fori_loop(0, CELL // 2, lambda i, carry: ends(2 * i + 1, ends(2 * i, carry)), tuple(corner))
 
     every = rows_at(0, er)
 
@@ -568,7 +565,7 @@
     sources = [
         in_hbm(value) for value in (initial_field[0], information, kappa_squared, lumped_mass)
     ]
-    rows_shape = jax.ShapeDtypeStruct((4 * HALO + SUB, tile_cols), F32)
+    rows_shape = jax.ShapeDtypeStruct((4 * HALO, tile_cols), F32)
     cols_shape = jax.ShapeDtypeStruct((4 * CELL * SUB + SUB, LANES), F32)
     up, down, left, right = pl.pallas_call(
         pack_kernel,
@@ -587,17 +584,6 @@
     from_left = lax.ppermute(right, "col", ring(col_count, 1))
     from_below = lax.ppermute(up, "row", ring(row_count, -1))
     from_above = lax.ppermute(down, "row", ring(row_count, 1))
-    corner_shape = jax.ShapeDtypeStruct((6 * SUB, LANES), F32)
-    corner_up, corner_down = pl.pallas_call(
-        corner_kernel,
-        in_specs=[vmem] * 2,
-        out_specs=[vmem] * 2,
-        out_shape=[corner_shape, corner_shape],
-        compiler_params=params,
-        name="corners",
-    )(from_right, from_left)
-    corner_below = lax.ppermute(corner_up, "row", ring(row_count, -1))
-    corner_above = lax.ppermute(corner_down, "row", ring(row_count, 1))
     planes = CELL * CELL
 
     def stack(count):
@@ -605,7 +591,7 @@
 
     plane_shape = jax.ShapeDtypeStruct(stack(planes), F32)
     noise_shape = jax.ShapeDtypeStruct(stack(PHASES * 4), F32)
-    natural_shape = jax.ShapeDtypeStruct((4 * tiles, tile_rows + 2 * HALO, LANES), F32)
+    natural_shape = jax.ShapeDtypeStruct((4 * tiles, tile_rows, LANES), F32)
     order_scratch = pltpu.SMEM(colour_order.shape, I32)
     noise, natural = pl.pallas_call(
         functools.partial(noise_kernel, tile_rows, tile_cols),
@@ -621,16 +607,26 @@
         cost_estimate=estimate(4_000_000),
         name="noise",
     )(order, seeds, *sources)
-    *state, _ = pl.pallas_call(
+    corner_shape = jax.ShapeDtypeStruct((7 * SUB, LANES), F32)
+    corner_up, corner_down = pl.pallas_call(
+        corner_kernel,
+        in_specs=[vmem] * 3 + [pl.BlockSpec(memory_space=pl.ANY)],
+        out_specs=[vmem] * 2,
+        out_shape=[corner_shape, corner_shape],
+        compiler_params=params,
+        name="corners",
+    )(from_right, from_left, left, noise)
+    corner_below = lax.ppermute(corner_up, "row", ring(row_count, -1))
+    corner_above = lax.ppermute(corner_down, "row", ring(row_count, 1))
+    state = pl.pallas_call(
         functools.partial(planes_kernel, tile_rows, tile_cols),
-        in_specs=[vmem] * 5,
-        out_specs=[vmem] * 5,
-        out_shape=[plane_shape] * 4 + [natural_shape],
-        input_output_aliases={0: 4},
+        in_specs=[vmem] * 3,
+        out_specs=[vmem] * 4,
+        out_shape=[plane_shape] * 4,
         compiler_params=params,
         cost_estimate=estimate(4_000_000),
         name="planes",
-    )(natural, from_below, from_above, from_right, from_left)
+    )(natural, from_right, from_left)
     result, energy, *_ = pl.pallas_call(
         functools.partial(sweep_kernel, tile_rows, tile_cols, nodes),
         in_specs=[hbm] + [vmem] * 11,
@@ -643,6 +639,7 @@
         + [noise_shape],
         input_output_aliases={1 + i: 2 + i for i in range(5)},
         scratch_shapes=[
+            pltpu.VMEM((4 * tiles, 2 * HALO, LANES), F32),
             pltpu.VMEM(stack(planes), F32),
             pltpu.VMEM(stack(planes), F32),
             pltpu.VMEM((PHASES + 1, SUB, LANES), F32),

time: 39.8 us -> 37.2 us (0.935)
  waiting for transfers between devices: 5.54 us -> 2.42 us
  starting transfers between devices: 9.44 us -> 10.5 us
  Pallas kernels: 12.9 us -> 12.3 us
    ppermute x1, waiting for transfers between devices: 3.59 us -> 0.12 us  [local(): from_left = lax.ppermute(right, 'col', ring(col_count, 1))]
    ppermute x1, waiting for transfers between devices: 0.01 us -> 2.29 us  [local(): corner_above = lax.ppermute(corner_down, 'row', ring(row_count, 1))]
    ppermute x1, waiting for transfers between devices: 1.94 us -> 0.01 us  [local(): from_right = lax.ppermute(left, 'col', ring(col_count, -1))]
    ppermute x1, starting transfers between devices: 2.76 us -> 3.54 us  [local(): from_right = lax.ppermute(left, 'col', ring(col_count, -1))]
    pallas_call x1, Pallas kernels: 3.13 us -> 2.46 us  [local(): pl.pallas_call(functools.partial(planes_kernel, tile_rows, tile_cols), in...]
  transfers between devices with their start and end apart: 6 -> 6, of which waited for: 2 -> 2; matrix products, arithmetic and copies ran while one was open for 0% -> 0% of each run, Pallas kernels for 13% -> 12%
where the time goes in v4:
time: 37.2 us; the launch traced here: 37 us
  Pallas kernels  12.3 us (33%)
  starting transfers between devices  10.5 us (28%)
  blocking collectives  10.4 us (28%)
  waiting for transfers between devices  2.42 us (7%)
  between operations  0.68 us (2%)
  local copies, waits for them, and re-layouts  0.65 us (2%)
    all_to_all x1, blocking collectives, local(): shared = lax.all_to_all(energy, AXES, 0, 0, tiled=True)  10.4 us
    pallas_call x1, Pallas kernels, local(): pl.pallas_call(functools.partial(sweep_kernel, tile_rows, tile_cols, node...  6.13 us
    ppermute x1, starting transfers between devices, local(): from_below = lax.ppermute(up, 'row', ring(row_count, -1))  3.97 us
    ppermute x1, starting transfers between devices, local(): from_right = lax.ppermute(left, 'col', ring(col_count, -1))  3.54 us
    ppermute x1, starting transfers between devices, local(): corner_below = lax.ppermute(corner_up, 'row', ring(row_count, -1))  2.97 us
    pallas_call x1, Pallas kernels, local(): pl.pallas_call(functools.partial(planes_kernel, tile_rows, tile_cols), in...  2.46 us
    ppermute x1, waiting for transfers between devices, local(): corner_above = lax.ppermute(corner_down, 'row', ring(row_count, 1))  2.29 us
    pallas_call x1, Pallas kernels, local(): pl.pallas_call(functools.partial(noise_kernel, tile_rows, tile_cols), in_...  1.93 us
  transfers between devices with their start and end apart: 6, of which 2 were waited for; matrix products, arithmetic and copies ran while one was open for 0% of the time, Pallas kernels for 12%

profile of v4, /device:TPU:0, one launch (start us, length us, event | category | flops | bytes accessed | tf_op | source)
XLA Modules:
  0.0 37.0 jit_solution(1943825376765339176)
XLA Ops:
  0.6 1.7 %pack.1 = (f32[64,512]{1,0:T(8,128)S(1)}, f32[64,512]{1,0:T(8,128)S(1)}, f32[136,128]{1,0:T(8,128)S(1)}, f32[136,128]{1,0:T(8,128)S(1)}) custom-call(s32[1,1,2,1,4]{4,3,2,1,0:T(1,128)} %bitcast.13, f32[128,512]{1,0:T(8,128)} %bitcast.11, f32[128,512]{1,0:T(8,128)} %refs_1_.1, f32[128,512]{1,0:T(8,128)} %refs_2_.1, f32[128,512]{1,0:T(8,128)} %refs_3_.1), custom_call_target="tpu_custom_call" | custom-call | tf_op jit(solution)/shard_map/pack/pallas_call | solution.py:570
  2.4 4.0 %collective-permute-start.2 = (f32[64,512]{1,0:T(8,128)S(1)}, f32[64,512]{1,0:T(8,128)S(1)}, u32[]{:S(2)}, u32[]{:S(2)}) collective-permute-start(f32[64,512]{1,0:T(8,128)S(1)} %get-tuple-element.24), channel_id=1, source_target_pairs={{0,24},{8,0},{16,8},{24,16},{1,25},{9,1},{17,9},{25,17},{2,26},{10... | collective-permute-start | bytes 393224 | tf_op jit(solution)/shard_map/ppermute | solution.py:585
  6.3 0.0 collective-permute-start.3
  6.3 0.0 collective-permute-start.1
  6.3 3.5 %collective-permute-start = (f32[136,128]{1,0:T(8,128)S(1)}, f32[136,128]{1,0:T(8,128)S(1)}, u32[]{:S(2)}, u32[]{:S(2)}) collective-permute-start(f32[136,128]{1,0:T(8,128)S(1)} %get-tuple-element.17.own_ref), channel_id=1, source_target_pairs={{0,7},{1,0},{2,1},{3,2},{4,3},{5,4},{6,5},{7,6},{8,15},{9,8},{10,9... | collective-permute-start | bytes 208904 | tf_op jit(solution)/shard_map/ppermute | solution.py:583
  9.9 1.9 %noise.1 = (f32[32,2,56,128]{3,2,1,0:T(8,128)S(1)}, f32[16,128,128]{2,1,0:T(8,128)S(1)}) custom-call(s32[4]{0:T(128)} %order_ref.3, s32[1,1,2,1,4]{4,3,2,1,0:T(1,128)} %bitcast.14, f32[128,512]{1,0:T(8,128)} %bitcast.12, f32[128,512]{1,0:T(8,128)} %refs_1_.1, f32[128,512]{1,0:T(8,128)} %refs_2_.1, f32[128,512]{1,0:T(8,128)} %refs_3_.1), custom_call_target="tpu_custom_call" | custom-call | flops 4000000 | bytes 1000000 | tf_op jit(solution)/shard_map/noise/pallas_call | solution.py:596
  11.8 0.1 collective-permute-done.1.left_ref
  11.9 0.0 collective-permute-done.right_ref
  11.9 0.1 corners.1
  12.0 3.0 %collective-permute-start.4 = (f32[56,128]{1,0:T(8,128)S(1)}, f32[56,128]{1,0:T(8,128)S(1)}, u32[]{:S(2)}, u32[]{:S(2)}) collective-permute-start(f32[56,128]{1,0:T(8,128)S(1)} %get-tuple-element.26), channel_id=1, source_target_pairs={{0,24},{8,0},{16,8},{24,16},{1,25},{9,1},{17,9},{25,17},{2,26},{10... | collective-permute-start | bytes 86024 | tf_op jit(solution)/shard_map/ppermute | solution.py:619
  15.0 0.0 collective-permute-start.5
  15.0 2.5 %planes.1 = (f32[16,2,56,128]{3,2,1,0:T(8,128)S(1)}, f32[16,2,56,128]{3,2,1,0:T(8,128)S(1)}, f32[16,2,56,128]{3,2,1,0:T(8,128)S(1)}, f32[16,2,56,128]{3,2,1,0:T(8,128)S(1)}) custom-call(f32[16,128,128]{2,1,0:T(8,128)S(1)} %get-tuple-element.16.nat, f32[136,128]{1,0:T(8,128)S(1)} %collective-permute-done.right_ref, f32[136,128]{1,0:T(8,128)S(1)} %collective-permute-done.1.left_ref), custom_call_target="tpu_custom_call" | custom-call | flops 4000000 | bytes 1000000 | tf_op jit(solution)/shard_map/planes/pallas_call | solution.py:621
  17.5 0.0 collective-permute-done.4.cbelow_ref
  17.5 2.3 %collective-permute-done.5.cabove_ref = f32[56,128]{1,0:T(8,128)S(1)} collective-permute-done((f32[56,128]{1,0:T(8,128)S(1)}, f32[56,128]{1,0:T(8,128)S(1)}, u32[]{:S(2)}, u32[]{:S(2)}) %collective-permute-start.5) | collective-permute-done | bytes 28704 | tf_op jit(solution)/shard_map/ppermute | solution.py:620
  19.8 0.0 collective-permute-done.2.below_ref
  19.8 0.0 collective-permute-done.3.above_ref
  19.8 6.1 %sweeps.1 = (f32[128,512]{1,0:T(8,128)}, f32[32,128]{1,0:T(8,128)S(1)}, f32[16,2,56,128]{3,2,1,0:T(8,128)S(1)}, f32[16,2,56,128]{3,2,1,0:T(8,128)S(1)}, f32[16,2...) custom-call(s32[4]{0:T(128)} %order_ref.3, ...), custom_call_target="tpu_custom_call", output_to_operand_aliasing={{2}: (1, {}), {3}: (2, {}), {4}: (3, {}), {5}: (4, {}), {6}... | custom-call | flops 8000000 | bytes 1000000 | tf_op jit(solution)/shard_map/sweeps/pallas_call | solution.py:630
  25.9 10.4 %all_to_all.9 = f32[32,1,128]{2,1,0:T(1,128)S(1)} all-to-all(f32[32,1,128]{2,1,0:T(1,128)S(1)} %bitcast.10), channel_id=1, replica_groups=mesh['row'=4,'col'=8] {'row','col'}, dimensions={0} | all-to-all | bytes 32768 | tf_op jit(solution)/shard_map/all_to_all | solution.py:658
  36.3 0.1 reduce_sum.9
  36.4 0.6 %reshape.17 = f32[2,4,1]{1,0,2:T(2,128)} reshape(f32[8]{0:T(128)S(1)} %bitcast.15) | data formatting | bytes 64 | tf_op jit(solution)/shard_map/reshape | solution.py:659
Async XLA Ops:
  2.4 17.4 %collective-permute-start.2 = (f32[64,512]{1,0:T(8,128)S(1)}, f32[64,512]{1,0:T(8,128)S(1)}, u32[]{:S(2)}, u32[]{:S(2)}) collective-permute-start(f32[64,512]{1,0:T(8,128)S(1)} %get-tuple-element.24), channel_id=1, source_target_pairs={{0,24},{8,0},{16,8},{24,16},{1,25},{9,1},{17,9},{25,17},{2,26},{10... | collective-permute-start | bytes 393224 | tf_op jit(solution)/shard_map/ppermute | solution.py:585
  6.3 13.5 %collective-permute-start.3 = (f32[64,512]{1,0:T(8,128)S(1)}, f32[64,512]{1,0:T(8,128)S(1)}, u32[]{:S(2)}, u32[]{:S(2)}) collective-permute-start(f32[64,512]{1,0:T(8,128)S(1)} %get-tuple-element.25), channel_id=1, source_target_pairs={{0,8},{8,16},{16,24},{24,0},{1,9},{9,17},{17,25},{25,1},{2,10},{10... | collective-permute-start | bytes 393224 | tf_op jit(solution)/shard_map/ppermute | solution.py:586
  6.3 5.6 %collective-permute-start.1 = (f32[136,128]{1,0:T(8,128)S(1)}, f32[136,128]{1,0:T(8,128)S(1)}, u32[]{:S(2)}, u32[]{:S(2)}) collective-permute-start(f32[136,128]{1,0:T(8,128)S(1)} %get-tuple-element.18), channel_id=1, source_target_pairs={{0,1},{1,2},{2,3},{3,4},{4,5},{5,6},{6,7},{7,0},{8,9},{9,10},{10,1... | collective-permute-start | bytes 208904 | tf_op jit(solution)/shard_map/ppermute | solution.py:584
  6.3 5.6 %collective-permute-start = (f32[136,128]{1,0:T(8,128)S(1)}, f32[136,128]{1,0:T(8,128)S(1)}, u32[]{:S(2)}, u32[]{:S(2)}) collective-permute-start(f32[136,128]{1,0:T(8,128)S(1)} %get-tuple-element.17.own_ref), channel_id=1, source_target_pairs={{0,7},{1,0},{2,1},{3,2},{4,3},{5,4},{6,5},{7,6},{8,15},{9,8},{10,9... | collective-permute-start | bytes 208904 | tf_op jit(solution)/shard_map/ppermute | solution.py:583
  12.0 5.5 %collective-permute-start.4 = (f32[56,128]{1,0:T(8,128)S(1)}, f32[56,128]{1,0:T(8,128)S(1)}, u32[]{:S(2)}, u32[]{:S(2)}) collective-permute-start(f32[56,128]{1,0:T(8,128)S(1)} %get-tuple-element.26), channel_id=1, source_target_pairs={{0,24},{8,0},{16,8},{24,16},{1,25},{9,1},{17,9},{25,17},{2,26},{10... | collective-permute-start | bytes 86024 | tf_op jit(solution)/shard_map/ppermute | solution.py:619
  15.0 4.8 %collective-permute-start.5 = (f32[56,128]{1,0:T(8,128)S(1)}, f32[56,128]{1,0:T(8,128)S(1)}, u32[]{:S(2)}, u32[]{:S(2)}) collective-permute-start(f32[56,128]{1,0:T(8,128)S(1)} %get-tuple-element.27), channel_id=1, source_target_pairs={{0,8},{8,16},{16,24},{24,0},{1,9},{9,17},{17,25},{25,1},{2,10},{10... | collective-permute-start | bytes 86024 | tf_op jit(solution)/shard_map/ppermute | solution.py:620

commit v5 on v4

--- a/solution.py
+++ b/solution.py
@@ -26,12 +26,11 @@
 SEED_BASE = 32768
 
 SIN_COEFFS = (
-    6.283185306485777,
-    -41.34170192921984,
-    81.60520938153618,
-    -76.70366601553475,
-    41.99996083008805,
-    -14.336855962945094,
+    -6.283185159611163,
+    41.3416549293435,
+    -81.60099819261265,
+    76.54965682062002,
+    -39.535813711455276,
 )
 
 
@@ -78,9 +77,9 @@
     return jnp.where(lane_iota(right.shape) % SLOT < SLOT // 2, right, left)
 
 
-def pack_kernel(seeds_ref, *refs):
-    sources, (up_ref, down_ref, left_ref, right_ref) = refs[:4], refs[4:8]
-    edges, seeds_buf, sems = refs[8:]
+def pack_kernel(order_ref, seeds_ref, *refs):
+    sources, (up_ref, down_ref, left_ref, right_ref, order_out, seeds_buf) = refs[:4], refs[4:10]
+    edges, sems = refs[10:]
     rows, cols = sources[0].shape
     mr = rows // CELL
     copies = []
@@ -91,6 +90,7 @@
         copies.append(made)
 
     copy(seeds_ref, seeds_buf)
+    copy(order_ref, order_out)
     for a, source in enumerate(sources):
         copy(source.at[:, pl.ds(0, LANES)], edges.at[2 * a])
         copy(source.at[:, pl.ds(cols - LANES, LANES)], edges.at[2 * a + 1])
@@ -121,23 +121,32 @@
     lax.fori_loop(0, 4, pack, 0)
 
 
+def half_turn(value):
+    return pltpu.roll(value, SUB // 2, 0)
+
+
 def corner_kernel(right_ref, left_ref, own_ref, after_ref, up_ref, down_ref):
     del after_ref
     group = lane_group(True)
+    low = sub_iota((SUB, LANES)) < HC
+    ups, downs = [], []
     for a in range(4):
         sides = []
         for r in range(CELL):
             rows = slice((a * CELL + r) * SUB, (a * CELL + r + 1) * SUB)
             sides.append(join_sides(right_ref[rows, :], left_ref[rows, :]))
-        rows = slice(a * SUB, (a + 1) * SUB)
-        up_ref[rows, :] = pick_group(group, [lroll(v, GROUP * r) for r, v in enumerate(sides)])
-        down_ref[rows, :] = pick_group(
-            group, [lroll(v, GROUP * (r + 1)) for r, v in enumerate(sides)]
-        )
+        ups.append(pick_group(group, [lroll(v, GROUP * r) for r, v in enumerate(sides)]))
+        downs.append(pick_group(group, [lroll(v, GROUP * (r + 1)) for r, v in enumerate(sides)]))
+    for pair in range(2):
+        rows = slice(pair * SUB, (pair + 1) * SUB)
+        up_ref[rows, :] = jnp.where(low, ups[2 * pair], half_turn(ups[2 * pair + 1]))
+        down_ref[rows, :] = jnp.where(low, half_turn(downs[2 * pair + 1]), downs[2 * pair])
     base = right_ref.shape[0] - SUB
     for out in (up_ref, down_ref):
         for i, source in enumerate((right_ref, left_ref, own_ref)):
-            out[(4 + i) * SUB : (5 + i) * SUB, :] = source[base : base + SUB, :]
+            out[2 * SUB : 2 * SUB + SUB // 2, i * SUB : i * SUB + COLOURS] = source[
+                base : base + SUB // 2, 0:COLOURS
+            ]
 
 
 def scramble(hashed):
@@ -160,7 +169,7 @@
     for coeff in SIN_COEFFS[-2::-1]:
         poly = poly * square + coeff
     square = -2.0 * jnp.log(u1)
-    return square * lax.rsqrt(jnp.maximum(square, 1e-30)) * (-(v * poly))
+    return square * lax.rsqrt(jnp.maximum(square, 1e-30)) * (v * poly)
 
 
 BASE = SUB
@@ -302,12 +311,12 @@
 
 def sweep_kernel(
     tile_rows, tile_cols, nodes,
-    order_ref, x_in, b_in, s_in, i_in, z_in,
+    order_ref, x_in, b_in, s_in, i_in, Z,
     below_ref, above_ref, right_ref, left_ref, cbelow_ref, cabove_ref,
-    out_ref, energy_ref, X, B, S, I, Z,
-    strip, W, D, EN, nat, order, around, sems,
+    out_ref, energy_ref, X, B, S, I,
+    strip, W, D, SH, DL, ZH, ZE, EN, nat, order, around, sems, out_sems,
 ):
-    del x_in, b_in, s_in, i_in, z_in
+    del x_in, b_in, s_in, i_in
     copies = []
 
     def copy(source, target):
@@ -316,12 +325,8 @@
         copies.append(made)
 
     copy(order_ref, order)
-    for at, (ref, back) in enumerate((
-        (right_ref, 1), (left_ref, 1), (cabove_ref, 1), (cbelow_ref, 1),
-        (cabove_ref, 3), (cabove_ref, 2), (cbelow_ref, 3), (cbelow_ref, 2),
-    )):
-        top = ref.shape[0] - back * SUB
-        copy(ref.at[pl.ds(top, SUB), pl.ds(0, LANES)], around.at[at])
+    for at, ref in enumerate((right_ref, left_ref, cabove_ref, cbelow_ref)):
+        copy(ref.at[pl.ds(ref.shape[0] - SUB, SUB)], around.at[at])
     mr = tile_rows // CELL
     er = mr + 2 * HC
     tiles = tile_cols // LANES
@@ -330,9 +335,11 @@
     low = sub < HC
 
     corner = []
-    for a in range(4):
-        at = slice(a * SUB, (a + 1) * SUB)
-        corner.append(jnp.where(low, cbelow_ref[at, :], cabove_ref[at, :]))
+    for pair in range(2):
+        at = slice(pair * SUB, (pair + 1) * SUB)
+        under, over = cbelow_ref[at, :], cabove_ref[at, :]
+        corner.append(jnp.where(low, under, over))
+        corner.append(half_turn(jnp.where(low, over, under)))
 
     def strips(a, carry):
         for t in range(tiles):
@@ -410,108 +417,158 @@
     offset_side = node_offsets(tile_cols, side_row, side_col)
     offset_ends = node_offsets(tile_cols, end_cell, lane)
 
-    def run_phase(phase, carry):
+    def halo_noise(phase):
         sweep, k = phase // COLOURS, phase % COLOURS
         colour = order[k]
+
+        def seed(at, block):
+            high = around[at, sweep, block * SUB + k].astype(I32)
+            return high * SEED_BASE + around[at, SWEEPS + sweep, block * SUB + k].astype(I32)
+
+        ends_seed = offset_ends + jnp.where(low, seed(3, 2), seed(2, 2))
+        side_seed = jnp.where(is_right, seed(0, 0), seed(1, 0))
+        ends = jnp.where(low, seed(3, 0), seed(2, 0))
+        side_seed = jnp.where(in_right_corner, ends, side_seed)
+        ends = jnp.where(low, seed(3, 1), seed(2, 1))
+        side_seed = offset_side + jnp.where(in_left_corner, ends, side_seed)
+        for n in range(4):
+            extra = phase_extra(colour, n, tile_cols)
+            at = (phase % 2) * 4 + n
+            ZE[at] = half_turn(gaussian(ends_seed + extra))
+            value = gaussian(side_seed + extra)
+            for g in range(mr // SUB):
+                ZH[at, HC + SUB * g : HC + SUB * (g + 1), :] = lroll(value, -GROUP * g)
+            value = lroll(value, -2 * HC)
+            ZH[at, er - HC : er, :] = value[0:HC]
+            ZH[at, 0:HC, :] = value[HC:SUB]
+
+    halo_noise(jnp.int32(0))
+
+    def run_phase(phase, carry):
+        colour = order[phase % COLOURS]
         ci, cj = colour // 2, colour % 2
         r0, c0 = 2 * ci, 2 * cj
-
-        def seed(at):
-            return around[at, sweep, k].astype(I32) * SEED_BASE + around[
-                at, SWEEPS + sweep, k
-            ].astype(I32)
-
-        ends_seed = offset_ends + jnp.where(low, seed(3), seed(2))
-        side_seed = jnp.where(is_right, seed(0), seed(1))
-        side_seed = jnp.where(in_right_corner, jnp.where(low, seed(6), seed(4)), side_seed)
-        side_seed = jnp.where(in_left_corner, jnp.where(low, seed(7), seed(5)), side_seed)
-        side_seed = offset_side + side_seed
-        for n in range(4):
-            at = phase * 4 + n
-            extra = phase_extra(colour, n, tile_cols)
-            put_ends(Z, at, 0, gaussian(ends_seed + extra))
-            value = gaussian(side_seed + extra)
-            for g in range(mr // SUB):
-                Z[at, 1, rows_at(HC + SUB * g, SUB), :] = lroll(value, -GROUP * g)
-            put_ends(Z, at, 1, lroll(value, -2 * HC))
-        z = [Z[phase * 4 + n, :, every, :] for n in range(4)]
-
+        slot = (phase % 2) * 4
+        z_ends = [ZE[slot + n] for n in range(4)]
         own = [(r0 + n // 2) * CELL + c0 + n % 2 for n in range(4)]
         above, up = (r0 + CELL - 1) % CELL, ci - 1
         below, down = (r0 + 2) % CELL, ci
         left, right = (c0 + CELL - 1) % CELL, (c0 + 2) % CELL
-        above_rows, below_rows = rows_at(up, er), rows_at(down, er)
-        w_own = [W[plane, :, every, :] for plane in own]
-        w_above = [W[above * CELL + c0 + i, :, above_rows, :] for i in range(2)]
-        w_below = [W[below * CELL + c0 + i, :, below_rows, :] for i in range(2)]
-        w_left = [
-            lane_shift(W[(r0 + i) * CELL + left, :, every, :], 1 - cj, -cj) for i in range(2)
-        ]
-        w_right = [
-            lane_shift(
-                W[(r0 + i) * CELL + right, :, every, :], (LANES - 1) * cj, LANES * cj - 1
+        above = [above * CELL + c0 + i for i in range(2)]
+        below = [below * CELL + c0 + i for i in range(2)]
+        left = [(r0 + i) * CELL + left for i in range(2)]
+        right = [(r0 + i) * CELL + right for i in range(2)]
+        for i in range(2):
+            SH[i] = lane_shift(W[left[i], :, every, :], 1 - cj, -cj)
+            SH[2 + i] = lane_shift(W[right[i], :, every, :], (LANES - 1) * cj, LANES * cj - 1)
+
+        def load(k):
+            rows = rows_at(SUB * k, SUB)
+            return (
+                [W[plane, :, rows, :] for plane in own],
+                [W[plane, :, rows_at(SUB * k + up, SUB), :] for plane in above],
+                [W[plane, :, rows_at(SUB * k + down, SUB), :] for plane in below],
+                [X[plane, 0, rows, :] for plane in own],
             )
-            for i in range(2)
-        ]
-        inv = [I[plane, :, every, :] for plane in own]
-        stiff = [S[plane, :, every, :] for plane in own]
-        sums = [
-            w_above[0] + w_own[2] + w_left[0] + w_own[1],
-            w_above[1] + w_own[3] + w_own[0] + w_right[0],
-            w_own[0] + w_below[0] + w_left[1] + w_own[3],
-            w_own[1] + w_below[1] + w_own[2] + w_right[1],
-        ]
-        residual = [
-            B[own[n], :, every, :] - (stiff[n] * w_own[n] - sums[n]) for n in range(4)
-        ]
-        scaled = [stiff[n] * inv[n] for n in range(4)]
-        diag = [D[plane, :, every, :] for plane in own]
-        m01, m02 = -(scaled[0] + scaled[1]), -(scaled[0] + scaled[2])
-        m13, m23 = -(scaled[1] + scaled[3]), -(scaled[2] + scaled[3])
-        m03, m12 = inv[1] + inv[2], inv[0] + inv[3]
-        q0 = lax.rsqrt(diag[0])
-        l10, l20, l30 = m01 * q0, m02 * q0, m03 * q0
-        q1 = lax.rsqrt(diag[1] - l10 * l10)
-        l21, l31 = (m12 - l20 * l10) * q1, (m13 - l30 * l10) * q1
-        q2 = lax.rsqrt(diag[2] - l20 * l20 - l21 * l21)
-        l32 = (m23 - l30 * l20 - l31 * l21) * q2
-        q3 = lax.rsqrt(diag[3] - l30 * l30 - l31 * l31 - l32 * l32)
-        f0 = residual[0] * q0
-        f1 = (residual[1] - l10 * f0) * q1
-        f2 = (residual[2] - l20 * f0 - l21 * f1) * q2
-        f3 = (residual[3] - l30 * f0 - l31 * f1 - l32 * f2) * q3
-        y0, y1, y2, y3 = f0 + z[0], f1 + z[1], f2 + z[2], f3 + z[3]
-        d3 = y3 * q3
-        d2 = (y2 - l32 * d3) * q2
-        d1 = (y1 - l21 * d2 - l31 * d3) * q1
-        d0 = (y0 - l10 * d1 - l20 * d2 - l30 * d3) * q0
-        delta = [d0, d1, d2, d3]
-        for n in range(4):
-            X[own[n], 0, every, :] = X[own[n], 0, every, :] + delta[n][0]
-        change = 0.0
-        for n, f in enumerate((f0, f1, f2, f3)):
-            change = change + (z[n][0] * z[n][0] - f[0] * f[0])
-        EN[phase + 1] = 0.5 * fold(change)
-        for n, (across, beside) in enumerate(((1, 2), (0, 3), (3, 0), (2, 1))):
-            step = stiff[n] * delta[n] - (delta[across] + delta[beside])
-            W[own[n], :, every, :] = w_own[n] + inv[n] * step
-
-        def spread(plane, rows, value):
-            W[plane, :, rows, :] = W[plane, :, rows, :] - I[plane, :, rows, :] * value
-
+
+        change = jnp.zeros((SUB, LANES), F32)
+        loaded = load(0)
+        count = er // SUB
+        for k in range(count):
+            rows, flat = rows_at(SUB * k, SUB), slice(SUB * k, SUB * (k + 1))
+            w_own, w_above, w_below, field = loaded
+            if k < count - 1:
+                loaded = load(k + 1)
+            w_left = [SH[i, :, flat, :] for i in range(2)]
+            w_right = [SH[2 + i, :, flat, :] for i in range(2)]
+            inv = [I[plane, :, rows, :] for plane in own]
+            stiff = [S[plane, :, rows, :] for plane in own]
+            sums = [
+                w_above[0] + w_own[2] + w_left[0] + w_own[1],
+                w_above[1] + w_own[3] + w_own[0] + w_right[0],
+                w_own[0] + w_below[0] + w_left[1] + w_own[3],
+                w_own[1] + w_below[1] + w_own[2] + w_right[1],
+            ]
+            residual = [
+                B[own[n], :, rows, :] - (stiff[n] * w_own[n] - sums[n]) for n in range(4)
+            ]
+            scaled = [stiff[n] * inv[n] for n in range(4)]
+            diag = [D[plane, :, rows, :] for plane in own]
+            q0 = lax.rsqrt(diag[0])
+            l10, l20 = (scaled[0] + scaled[1]) * q0, (scaled[0] + scaled[2]) * q0
+            l30 = -((inv[1] + inv[2]) * q0)
+            q1 = lax.rsqrt(diag[1] - l10 * l10)
+            l21 = (l20 * l10 - (inv[0] + inv[3])) * q1
+            l31 = (l30 * l10 + (scaled[1] + scaled[3])) * q1
+            q2 = lax.rsqrt(diag[2] - l20 * l20 - l21 * l21)
+            l32 = (l30 * l20 + l31 * l21 + (scaled[2] + scaled[3])) * q2
+            q3 = lax.rsqrt(diag[3] - l30 * l30 - l31 * l31 - l32 * l32)
+            f0 = residual[0] * q0
+            f1 = (residual[1] + l10 * f0) * q1
+            f2 = (residual[2] + l20 * f0 + l21 * f1) * q2
+            f3 = (residual[3] + l30 * f0 + l31 * f1 + l32 * f2) * q3
+            z = []
+            for n in range(4):
+                inner = Z[phase * 4 + n, 0, rows, :]
+                if k == 0:
+                    inner = jnp.where(low, z_ends[n], inner)
+                if k == count - 1:
+                    inner = jnp.where(low, inner, z_ends[n])
+                z.append(jnp.stack([inner, ZH[slot + n, flat, :]]))
+            y0, y1, y2, y3 = f0 + z[0], f1 + z[1], f2 + z[2], f3 + z[3]
+            d3 = y3 * q3
+            d2 = (y2 + l32 * d3) * q2
+            d1 = (y1 + l21 * d2 + l31 * d3) * q1
+            d0 = (y0 + l10 * d1 + l20 * d2 + l30 * d3) * q0
+            delta = [d0, d1, d2, d3]
+            part = 0.0
+            for n, f in enumerate((f0, f1, f2, f3)):
+                part = part + (z[n][0] * z[n][0] - f[0] * f[0])
+            if k == 0:
+                part = jnp.where(low, 0.0, part)
+            if k == count - 1:
+                part = jnp.where(low, part, 0.0)
+            change = change + part
+            for n, (across, beside) in enumerate(((1, 2), (0, 3), (3, 0), (2, 1))):
+                DL[n, :, flat, :] = delta[n]
+                X[own[n], 0, rows, :] = field[n] + delta[n][0]
+                step = stiff[n] * delta[n] - (delta[across] + delta[beside])
+                W[own[n], :, rows, :] = w_own[n] + inv[n] * step
+            for i in range(2):
+                at = rows_at(SUB * k + up, SUB)
+                W[above[i], :, at, :] = w_above[i] - I[above[i], :, at, :] * delta[i]
+                at = rows_at(SUB * k + down, SUB)
+                W[below[i], :, at, :] = w_below[i] - I[below[i], :, at, :] * delta[2 + i]
+        EN[phase + 1] = 0.5 * change
         for i in range(2):
-            spread(above * CELL + c0 + i, above_rows, delta[i])
-            spread(below * CELL + c0 + i, below_rows, delta[2 + i])
-            spread(
-                (r0 + i) * CELL + left, every,
-                lane_shift(delta[2 * i], (LANES - 1) * (1 - cj), LANES * (1 - cj) - 1),
+            for plane, n, amount, edge in (
+                (left[i], 2 * i, (LANES - 1) * (1 - cj), LANES * (1 - cj) - 1),
+                (right[i], 2 * i + 1, cj, cj - 1),
+            ):
+                value = I[plane, :, every, :] * lane_shift(DL[n], amount, edge)
+                W[plane, :, every, :] = W[plane, :, every, :] - value
+        halo_noise(jnp.minimum(phase + 1, PHASES - 1))
+        return carry
+
+    lax.fori_loop(0, PHASES, run_phase, 0)
+
+    def restore(i, carry):
+        for r in (2 * i, 2 * i + 1):
+            columns = natural_columns(
+                [X[r * CELL + c, 0, rows_at(HC, mr), :] for c in range(CELL)]
             )
-            spread(
-                (r0 + i) * CELL + right, every, lane_shift(delta[2 * i + 1], cj, cj - 1)
-            )
+            for t, value in enumerate(columns):
+                nat[t, pl.ds(r, mr, stride=CELL), :] = value
         return carry
 
-    lax.fori_loop(0, PHASES, run_phase, 0)
+    lax.fori_loop(0, CELL // 2, restore, 0)
+    leaving = []
+    for t in range(tiles):
+        made = pltpu.make_async_copy(
+            nat.at[t], out_ref.at[:, pl.ds(t * LANES, LANES)], out_sems.at[t]
+        )
+        made.start()
+        leaving.append(made)
 
     running = EN[0]
     result = jnp.zeros((1, LANES), F32)
@@ -522,19 +579,8 @@
         total = jnp.sum(jnp.sum(running, axis=0, keepdims=True), axis=1, keepdims=True)
         result = jnp.where(first_row == phase, total, result)
     energy_ref[...] = jnp.broadcast_to(result / nodes, energy_ref.shape)
-
-    def restore(i, carry):
-        for r in (2 * i, 2 * i + 1):
-            columns = natural_columns(
-                [X[r * CELL + c, 0, rows_at(HC, mr), :] for c in range(CELL)]
-            )
-            for t, value in enumerate(columns):
-                nat[t, pl.ds(r, mr, stride=CELL), :] = value
-        return carry
-
-    lax.fori_loop(0, CELL // 2, restore, 0)
-    for t in range(tiles):
-        out_ref[:, t * LANES : (t + 1) * LANES] = nat[t]
+    for made in leaving:
+        made.wait()
 
 
 def ring(count, step):
@@ -567,19 +613,22 @@
     ]
     rows_shape = jax.ShapeDtypeStruct((4 * HALO, tile_cols), F32)
     cols_shape = jax.ShapeDtypeStruct((4 * CELL * SUB + SUB, LANES), F32)
-    up, down, left, right = pl.pallas_call(
+    up, down, left, right, order_near, seeds_near = pl.pallas_call(
         pack_kernel,
-        in_specs=[hbm] * 5,
-        out_specs=[vmem] * 4,
-        out_shape=[rows_shape, rows_shape, cols_shape, cols_shape],
+        in_specs=[hbm] * 6,
+        out_specs=[vmem] * 6,
+        out_shape=[
+            rows_shape, rows_shape, cols_shape, cols_shape,
+            jax.ShapeDtypeStruct(colour_order.shape, I32),
+            jax.ShapeDtypeStruct(seeds.shape, I32),
+        ],
         scratch_shapes=[
             pltpu.VMEM((8, tile_rows, LANES), F32),
-            pltpu.VMEM(seeds.shape, I32),
-            pltpu.SemaphoreType.DMA((17,)),
+            pltpu.SemaphoreType.DMA((18,)),
         ],
         compiler_params=params,
         name="pack",
-    )(seeds, *sources)
+    )(order, seeds, *sources)
     from_right = lax.ppermute(left, "col", ring(col_count, -1))
     from_left = lax.ppermute(right, "col", ring(col_count, 1))
     from_below = lax.ppermute(up, "row", ring(row_count, -1))
@@ -595,7 +644,7 @@
     order_scratch = pltpu.SMEM(colour_order.shape, I32)
     noise, natural = pl.pallas_call(
         functools.partial(noise_kernel, tile_rows, tile_cols),
-        in_specs=[hbm] * 6,
+        in_specs=[vmem] * 2 + [hbm] * 4,
         out_specs=[vmem] * 2,
         out_shape=[noise_shape, natural_shape],
         scratch_shapes=[
@@ -606,8 +655,8 @@
         compiler_params=params,
         cost_estimate=estimate(4_000_000),
         name="noise",
-    )(order, seeds, *sources)
-    corner_shape = jax.ShapeDtypeStruct((7 * SUB, LANES), F32)
+    )(order_near, seeds_near, *sources)
+    corner_shape = jax.ShapeDtypeStruct((3 * SUB, LANES), F32)
     corner_up, corner_down = pl.pallas_call(
         corner_kernel,
         in_specs=[vmem] * 3 + [pl.BlockSpec(memory_space=pl.ANY)],
@@ -629,30 +678,34 @@
     )(natural, from_right, from_left)
     result, energy, *_ = pl.pallas_call(
         functools.partial(sweep_kernel, tile_rows, tile_cols, nodes),
-        in_specs=[hbm] + [vmem] * 11,
-        out_specs=[vmem] * 7,
+        in_specs=[vmem] * 12,
+        out_specs=[hbm] + [vmem] * 5,
         out_shape=[
             jax.ShapeDtypeStruct((tile_rows, tile_cols), F32),
             jax.ShapeDtypeStruct((devices, LANES), F32),
         ]
-        + [plane_shape] * 4
-        + [noise_shape],
-        input_output_aliases={1 + i: 2 + i for i in range(5)},
+        + [plane_shape] * 4,
+        input_output_aliases={1 + i: 2 + i for i in range(4)},
         scratch_shapes=[
             pltpu.VMEM((4 * tiles, 2 * HALO, LANES), F32),
             pltpu.VMEM(stack(planes), F32),
             pltpu.VMEM(stack(planes), F32),
+            pltpu.VMEM((4, 2, er, LANES), F32),
+            pltpu.VMEM((4, 2, er, LANES), F32),
+            pltpu.VMEM((8, er, LANES), F32),
+            pltpu.VMEM((8, SUB, LANES), F32),
             pltpu.VMEM((PHASES + 1, SUB, LANES), F32),
             pltpu.VMEM((tiles, tile_rows, LANES), F32),
             order_scratch,
-            pltpu.SMEM((8, SUB, LANES), F32),
-            pltpu.SemaphoreType.DMA((9,)),
+            pltpu.SMEM((4, SUB, LANES), F32),
+            pltpu.SemaphoreType.DMA((5,)),
+            pltpu.SemaphoreType.DMA((tiles,)),
         ],
         compiler_params=params,
         cost_estimate=estimate(8_000_000),
         name="sweeps",
     )(
-        order, *state, noise,
+        order_near, *state, noise,
         from_below, from_above, from_right, from_left, corner_below, corner_above,
     )
     shared = lax.all_to_all(energy, AXES, 0, 0, tiled=True)

time: 37.2 us -> 36.9 us (level)
  Pallas kernels: 12.3 us -> 11.8 us
where the time goes in v5:
time: 36.9 us; the launch traced here: 36.7 us
  Pallas kernels  11.8 us (32%)
  starting transfers between devices  10.5 us (28%)
  blocking collectives  10.5 us (28%)
  waiting for transfers between devices  2.42 us (7%)
  between operations  0.68 us (2%)
  local copies, waits for them, and re-layouts  0.65 us (2%)
    all_to_all x1, blocking collectives, local(): shared = lax.all_to_all(energy, AXES, 0, 0, tiled=True)  10.5 us
    pallas_call x1, Pallas kernels, local(): pl.pallas_call(functools.partial(sweep_kernel, tile_rows, tile_cols, node...  5.78 us
    ppermute x1, starting transfers between devices, local(): from_below = lax.ppermute(up, 'row', ring(row_count, -1))  3.97 us
    ppermute x1, starting transfers between devices, local(): from_right = lax.ppermute(left, 'col', ring(col_count, -1))  3.54 us
    ppermute x1, starting transfers between devices, local(): corner_below = lax.ppermute(corner_up, 'row', ring(row_count, -1))  2.97 us
    pallas_call x1, Pallas kernels, local(): pl.pallas_call(functools.partial(planes_kernel, tile_rows, tile_cols), in...  2.46 us
    ppermute x1, waiting for transfers between devices, local(): corner_above = lax.ppermute(corner_down, 'row', ring(row_count, 1))  2.11 us
    pallas_call x1, Pallas kernels, local(): pl.pallas_call(functools.partial(noise_kernel, tile_rows, tile_cols), in_...  1.75 us
  transfers between devices with their start and end apart: 6, of which 2 were waited for; matrix products, arithmetic and copies ran while one was open for 0% of the time, Pallas kernels for 12%

profile of v5, /device:TPU:0, one launch (start us, length us, event | category | flops | bytes accessed | tf_op | source)
XLA Modules:
  0.0 36.7 jit_solution(9933679746346324759)
XLA Ops:
  0.6 1.7 %pack.1 = (f32[64,512]{1,0:T(8,128)S(1)}, f32[64,512]{1,0:T(8,128)S(1)}, f32[136,128]{1,0:T(8,128)S(1)}, f32[136,128]{1,0:T(8,128)S(1)}, s32[4]{0:T(128)S(1)}, /*index=5*/s32[1,1,2,1,4]{4,3,2,1,0:T(1,128)S(1)}) custom-call(s32[4]{0:T(128)} %order_ref.1, s32[1,1,2,1,4]{4,3,2,1,0:T(1,128)} %bitcast.13, f32[128,512]{1,0:T(8,128)} %bitcast.11, ...), custom_call_target="tpu_custom_call" | custom-call | tf_op jit(solution)/shard_map/pack/pallas_call | solution.py:616
  2.4 4.0 %collective-permute-start.2 = (f32[64,512]{1,0:T(8,128)S(1)}, f32[64,512]{1,0:T(8,128)S(1)}, u32[]{:S(2)}, u32[]{:S(2)}) collective-permute-start(f32[64,512]{1,0:T(8,128)S(1)} %get-tuple-element.28), channel_id=1, source_target_pairs={{0,24},{8,0},{16,8},{24,16},{1,25},{9,1},{17,9},{25,17},{2,26},{10... | collective-permute-start | bytes 393224 | tf_op jit(solution)/shard_map/ppermute | solution.py:634
  6.4 0.0 collective-permute-start.3
  6.4 0.0 collective-permute-start.1
  6.4 3.5 %collective-permute-start = (f32[136,128]{1,0:T(8,128)S(1)}, f32[136,128]{1,0:T(8,128)S(1)}, u32[]{:S(2)}, u32[]{:S(2)}) collective-permute-start(f32[136,128]{1,0:T(8,128)S(1)} %get-tuple-element.21.own_ref), channel_id=1, source_target_pairs={{0,7},{1,0},{2,1},{3,2},{4,3},{5,4},{6,5},{7,6},{8,15},{9,8},{10,9... | collective-permute-start | bytes 208904 | tf_op jit(solution)/shard_map/ppermute | solution.py:632
  9.9 1.8 %noise.1 = (f32[32,2,56,128]{3,2,1,0:T(8,128)S(1)}, f32[16,128,128]{2,1,0:T(8,128)S(1)}) custom-call(s32[4]{0:T(128)S(1)} %get-tuple-element.18.order_ref, s32[1,1,2,1,4]{4,3,2,1,0:T(1,128)S(1)} %get-tuple-element.19.seeds_ref, f32[128,512]{1,0:T(8,128)} %bitcast.12, f32[128,512]{1,0:T(8,128)} %b_ref.1, f32[128,512]{1,0:T(8,128)} %kappa_ref.1, ...), custom_call_target="tpu_custom_call" | custom-call | flops 4000000 | bytes 1000000 | tf_op jit(solution)/shard_map/noise/pallas_call | solution.py:645
  11.7 0.3 collective-permute-done.1.left_ref
  12.0 0.0 collective-permute-done.right_ref
  12.0 0.1 corners.1
  12.1 3.0 %collective-permute-start.4 = (f32[24,128]{1,0:T(8,128)S(1)}, f32[24,128]{1,0:T(8,128)S(1)}, u32[]{:S(2)}, u32[]{:S(2)}) collective-permute-start(f32[24,128]{1,0:T(8,128)S(1)} %get-tuple-element.30), channel_id=1, source_target_pairs={{0,24},{8,0},{16,8},{24,16},{1,25},{9,1},{17,9},{25,17},{2,26},{10... | collective-permute-start | bytes 36872 | tf_op jit(solution)/shard_map/ppermute | solution.py:668
  15.1 0.0 collective-permute-start.5
  15.1 2.5 %planes.1 = (f32[16,2,56,128]{3,2,1,0:T(8,128)S(1)}, f32[16,2,56,128]{3,2,1,0:T(8,128)S(1)}, f32[16,2,56,128]{3,2,1,0:T(8,128)S(1)}, f32[16,2,56,128]{3,2,1,0:T(8,128)S(1)}) custom-call(f32[16,128,128]{2,1,0:T(8,128)S(1)} %get-tuple-element.20.nat, f32[136,128]{1,0:T(8,128)S(1)} %collective-permute-done.right_ref, f32[136,128]{1,0:T(8,128)S(1)} %collective-permute-done.1.left_ref), custom_call_target="tpu_custom_call" | custom-call | flops 4000000 | bytes 1000000 | tf_op jit(solution)/shard_map/planes/pallas_call | solution.py:670
  17.5 0.0 collective-permute-done.4.cbelow_ref
  17.5 2.1 %collective-permute-done.5.cabove_ref = f32[24,128]{1,0:T(8,128)S(1)} collective-permute-done((f32[24,128]{1,0:T(8,128)S(1)}, f32[24,128]{1,0:T(8,128)S(1)}, u32[]{:S(2)}, u32[]{:S(2)}) %collective-permute-start.5) | collective-permute-done | bytes 12320 | tf_op jit(solution)/shard_map/ppermute | solution.py:669
  19.6 0.0 collective-permute-done.2.below_ref
  19.6 0.0 collective-permute-done.3.above_ref
  19.7 5.8 %sweeps.1 = (f32[128,512]{1,0:T(8,128)}, f32[32,128]{1,0:T(8,128)S(1)}, f32[16,2,56,128]{3,2,1,0:T(8,128)S(1)}, f32[16,2,56,128]{3,2,1,0:T(8,128)S(1)}, f32[16,2...) custom-call(s32[4]{0:T(128)S(1)} %get-tuple-element.18.order_ref, ...), custom_call_target="tpu_custom_call", output_to_operand_aliasing={{2}: (1, {}), {3}: (2, {}), {4}: (3, {}), {5}: (4, {})} | custom-call | flops 8000000 | bytes 1000000 | tf_op jit(solution)/shard_map/sweeps/pallas_call | solution.py:679
  25.4 10.5 %all_to_all.9 = f32[32,1,128]{2,1,0:T(1,128)S(1)} all-to-all(f32[32,1,128]{2,1,0:T(1,128)S(1)} %bitcast.10), channel_id=1, replica_groups=mesh['row'=4,'col'=8] {'row','col'}, dimensions={0} | all-to-all | bytes 32768 | tf_op jit(solution)/shard_map/all_to_all | solution.py:711
  36.0 0.1 reduce_sum.9
  36.0 0.6 %reshape.17 = f32[2,4,1]{1,0,2:T(2,128)} reshape(f32[8]{0:T(128)S(1)} %bitcast.14) | data formatting | bytes 64 | tf_op jit(solution)/shard_map/reshape | solution.py:712
Async XLA Ops:
  2.4 17.3 %collective-permute-start.2 = (f32[64,512]{1,0:T(8,128)S(1)}, f32[64,512]{1,0:T(8,128)S(1)}, u32[]{:S(2)}, u32[]{:S(2)}) collective-permute-start(f32[64,512]{1,0:T(8,128)S(1)} %get-tuple-element.28), channel_id=1, source_target_pairs={{0,24},{8,0},{16,8},{24,16},{1,25},{9,1},{17,9},{25,17},{2,26},{10... | collective-permute-start | bytes 393224 | tf_op jit(solution)/shard_map/ppermute | solution.py:634
  6.4 13.3 %collective-permute-start.3 = (f32[64,512]{1,0:T(8,128)S(1)}, f32[64,512]{1,0:T(8,128)S(1)}, u32[]{:S(2)}, u32[]{:S(2)}) collective-permute-start(f32[64,512]{1,0:T(8,128)S(1)} %get-tuple-element.29), channel_id=1, source_target_pairs={{0,8},{8,16},{16,24},{24,0},{1,9},{9,17},{17,25},{25,1},{2,10},{10... | collective-permute-start | bytes 393224 | tf_op jit(solution)/shard_map/ppermute | solution.py:635
  6.4 5.6 %collective-permute-start.1 = (f32[136,128]{1,0:T(8,128)S(1)}, f32[136,128]{1,0:T(8,128)S(1)}, u32[]{:S(2)}, u32[]{:S(2)}) collective-permute-start(f32[136,128]{1,0:T(8,128)S(1)} %get-tuple-element.22), channel_id=1, source_target_pairs={{0,1},{1,2},{2,3},{3,4},{4,5},{5,6},{6,7},{7,0},{8,9},{9,10},{10,1... | collective-permute-start | bytes 208904 | tf_op jit(solution)/shard_map/ppermute | solution.py:633
  6.4 5.6 %collective-permute-start = (f32[136,128]{1,0:T(8,128)S(1)}, f32[136,128]{1,0:T(8,128)S(1)}, u32[]{:S(2)}, u32[]{:S(2)}) collective-permute-start(f32[136,128]{1,0:T(8,128)S(1)} %get-tuple-element.21.own_ref), channel_id=1, source_target_pairs={{0,7},{1,0},{2,1},{3,2},{4,3},{5,4},{6,5},{7,6},{8,15},{9,8},{10,9... | collective-permute-start | bytes 208904 | tf_op jit(solution)/shard_map/ppermute | solution.py:632
  12.1 5.5 %collective-permute-start.4 = (f32[24,128]{1,0:T(8,128)S(1)}, f32[24,128]{1,0:T(8,128)S(1)}, u32[]{:S(2)}, u32[]{:S(2)}) collective-permute-start(f32[24,128]{1,0:T(8,128)S(1)} %get-tuple-element.30), channel_id=1, source_target_pairs={{0,24},{8,0},{16,8},{24,16},{1,25},{9,1},{17,9},{25,17},{2,26},{10... | collective-permute-start | bytes 36872 | tf_op jit(solution)/shard_map/ppermute | solution.py:668
  15.1 4.6 %collective-permute-start.5 = (f32[24,128]{1,0:T(8,128)S(1)}, f32[24,128]{1,0:T(8,128)S(1)}, u32[]{:S(2)}, u32[]{:S(2)}) collective-permute-start(f32[24,128]{1,0:T(8,128)S(1)} %get-tuple-element.31), channel_id=1, source_target_pairs={{0,8},{8,16},{16,24},{24,0},{1,9},{9,17},{17,25},{25,1},{2,10},{10... | collective-permute-start | bytes 36872 | tf_op jit(solution)/shard_map/ppermute | solution.py:669
